TPU v7x, 256 devices: a whole 4x4x8 slice. The times are simulated.
256 devices in a mesh: img: 32 (over z, x), row: 8 (over y, core).
Axes of the slice: x: 4, y: 4, z: 8, core: 2. Of those that a mesh axis runs over, the one named last changes fastest.
Arguments:
- tokens: bfloat16 [32, 64, 128, 1024], P('img', 'row'), may hold values from -14 to 14
- proj_weight: bfloat16 [1024, 256], replicated, may hold values from -0.1875 to 0.1875
- proj_bias: float32 [256], replicated, may hold values from -3 to 3
- conv_weight: bfloat16 [4, 3, 3, 256, 256], replicated, may hold values from -0.125 to 0.125
- bn_gain: float32 [4, 256], replicated, may hold values from 0.1 to 1.9
- bn_bias: float32 [4, 256], replicated, may hold values from -3 to 3
Outputs:
- joining_out: bfloat16 [32, 64, 128, 256], P('img', 'row')
All inputs are finite; a program needn't handle non-finite values.
Results may differ from a plain program's by a relative error of at most 0.0071.
Values may be sent and summed in bfloat16 or wider, within the bound.
No kernel may reach another device: no remote copies, remote signals or barrier semaphores. Data moves between devices by JAX's collectives and lax.ppermute only.
A program may use at most 64 MiB of HBM per device.

v0:
```python
import jax
import jax.numpy as jnp
from jax import lax
from jax.sharding import Mesh
from jax.sharding import PartitionSpec as P

ROW = ("row_0", "row_1")
IMG = ("img_0", "img_1")


epsilon = 1e-05


def sent_to_all(value, axis):
    devices = lax.axis_size(axis)
    return lax.all_to_all(
        jnp.broadcast_to(value[None], (devices, *value.shape)), axis, 0, 0, tiled=True
    )


def of_everyone(value, axis):
    return sent_to_all(value, axis).sum(axis=0)


def by_axis(value, axes):
    far, near = axes
    nearer = of_everyone(value, near)
    return of_everyone(nearer, far)


def in_one(arrays, axis):
    ravelled, at, finished = (jnp.concatenate([a.reshape(-1) for a in arrays]), 0, [])
    running = by_axis(ravelled, axis)
    for a in arrays:
        finished.append(running[at : at + a.size].reshape(a.shape))
        at += a.size
    return tuple(finished)


def extended(value, sides, width):
    for axis, dim in sides:
        devices, length = (lax.axis_size(axis), value.shape[dim])
        up = [(i, (i + 1) % devices) for i in range(devices - 1)]
        down = [(j, i) for i, j in up]
        last = lax.slice_in_dim(value, length - width, length, axis=dim)
        leading = lax.slice_in_dim(value, 0, width, axis=dim)
        before = lax.ppermute(last, axis, up)
        after = lax.ppermute(leading, axis, down)
        value = jnp.concatenate([before, value, after], axis=dim)
    return value


def conv_valid(padded, kernel):
    return lax.conv_general_dilated(
        padded,
        kernel,
        (1, 1),
        ((0, 0), (1, 1)),
        dimension_numbers=("NHWC", "HWIO", "NHWC"),
        preferred_element_type=jnp.float32,
    )


def batch_norm(conv_out, interior, gain_row, shift_row, cell_total):
    first_moment, squares = in_one(
        (jnp.sum(interior, axis=(0, 1, 2)), jnp.sum(jnp.square(interior), axis=(0, 1, 2))),
        (("img_0", "img_1"), ("row_0", "row_1")),
    )
    average = first_moment / cell_total
    spread = squares / cell_total - average * average
    return (conv_out - average) * lax.rsqrt(spread + epsilon) * gain_row + shift_row


def residual_unit(source, conv_weight, bn_gain, bn_bias, first, cell_total):
    widened = extended(source, ((ROW, 1),), 2)
    conv_first = conv_valid(jax.nn.relu(widened), conv_weight[first])
    normed = batch_norm(conv_first, conv_first[:, 1:-1], bn_gain[first], bn_bias[first], cell_total)
    strip_index = lax.axis_index(ROW)
    last_index = lax.axis_size(ROW) - 1
    position = jnp.arange(conv_first.shape[1])
    inside = jnp.logical_not(
        jnp.logical_or(
            jnp.logical_and(position == 0, strip_index == 0),
            jnp.logical_and(position == conv_first.shape[1] - 1, strip_index == last_index),
        )
    )
    hidden = jnp.where(inside[None, :, None, None], jax.nn.relu(normed), 0.0).astype(jnp.bfloat16)
    conv_second = conv_valid(hidden, conv_weight[first + 1])
    branch = batch_norm(
        conv_second, conv_second, bn_gain[first + 1], bn_bias[first + 1], cell_total
    )
    return source.astype(jnp.float32) + branch


def on_device(tokens, proj_weight, proj_bias, conv_weight, bn_gain, bn_bias):
    img_count, row_count, col_count, embed_dim = tokens.shape
    flat = (
        jnp.dot(tokens.reshape(-1, embed_dim), proj_weight, preferred_element_type=jnp.float32)
        + proj_bias
    )
    feature = flat.astype(jnp.bfloat16).reshape(img_count, row_count, col_count, -1)
    cell_total = float(lax.axis_size(IMG) * lax.axis_size(ROW) * img_count * row_count * col_count)
    joined = residual_unit(feature, conv_weight, bn_gain, bn_bias, 0, cell_total).astype(
        jnp.bfloat16
    )
    return residual_unit(joined, conv_weight, bn_gain, bn_bias, 2, cell_total).astype(jnp.bfloat16)


def solution(mesh):
    split = Mesh(mesh.devices.reshape(8, 4, 4, 2), ("img_0", "img_1", "row_0", "row_1"))
    placed = (P(IMG, ROW, None, None), P(), P(), P(), P(), P())
    return jax.shard_map(
        on_device, mesh=split, in_specs=placed, out_specs=P(IMG, ROW, None, None), check_vma=False
    )
```

profile of v0, /device:TPU:1, one launch (start us, length us, event | category | flops | bytes accessed | tf_op | source)
XLA Modules:
  0.0 143.5 jit_solution(2154558728067527569)
XLA Ops:
  0.0 1.6 %copy-done = bf16[1,8,128,1024]{3,2,1,0:T(8,128)(2,1)S(1)} copy-done((bf16[1,8,128,1024]{3,2,1,0:T(8,128)(2,1)S(1)}, bf16[1,8,128,1024]{3,2,1,0:T(8,128)(2,1)}, u32[]{:S(2)}) %copy-start) | copy-done | bytes 2097176
  1.6 1.8 %fusion.6 = bf16[1024,256]{1,0:T(8,128)(2,1)S(1)} fusion(bf16[1024,1024]{1,0:T(8,128)(2,1)S(1)} %bitcast.68, bf16[1024,256]{1,0:T(8,128)(2,1)} %param.7, f32[256]{0:T(256)} %param.8), kind=kOutput, calls=%fused_computation.14 | convolution fusion | flops 537395200 | bytes 3146752 | tf_op jit(solution)/shard_map/dot_general | solution.py:98
  3.8 4.6 %collective-permute-start = (bf16[1,2,128,256]{3,1,2,0:T(2,128)(2,1)S(1)}, bf16[1,2,128,256]{3,1,2,0:T(2,128)(2,1)S(1)}, u32[]{:S(2)}, u32[]{:S(2)}) collective-permute-start(bf16[1,2,128,256]{3,1,2,0:T(2,128)(2,1)S(1)} %get-tuple-element.19), channel_id=1, source_target_pairs={{0,1},{1,2},{2,3},{3,4},{4,5},{5,6},{6,7},{8,9},{9,10},{10,11},{11... | collective-permute-start | bytes 393224 | tf_op jit(solution)/shard_map/ppermute | solution.py:47
  8.4 1.9 %collective-permute-start.1 = (bf16[1,2,128,256]{3,1,2,0:T(2,128)(2,1)S(1)}, bf16[1,2,128,256]{3,1,2,0:T(2,128)(2,1)S(1)}, u32[]{:S(2)}, u32[]{:S(2)}) collective-permute-start(bf16[1,2,128,256]{3,1,2,0:T(2,128)(2,1)S(1)} %get-tuple-element.20), channel_id=1, source_target_pairs={{1,0},{2,1},{3,2},{4,3},{5,4},{6,5},{7,6},{9,8},{10,9},{11,10},{12... | collective-permute-start | bytes 393224 | tf_op jit(solution)/shard_map/ppermute | solution.py:48
  10.4 4.3 %collective-permute-done.1 = bf16[1,2,128,256]{3,1,2,0:T(2,128)(2,1)S(1)} collective-permute-done((bf16[1,2,128,256]{3,1,2,0:T(2,128)(2,1)S(1)}, bf16[1,2,128,256]{3,1,2,0:T(2,128)(2,1)S(1)}, u32[]{:S(2)}, u32[]{:S(2)}) %collective-permute-start.1) | collective-permute-done | bytes 131104 | tf_op jit(solution)/shard_map/ppermute | solution.py:48
  14.7 0.8 fusion.21
  16.3 3.1 %convolution_select_fusion.1 = f32[10,8,17,256]{3,1,2,0:T(8,128)S(1)} fusion(bf16[4,3,3,256,256]{4,3,2,1,0:T(8,128)(2,1)} %param.9, bf16[12,1,7,2,256]{4,2,3,0,1:T(8,128)(2,1)S(1)} %slice.116, bf16[12,1,8,17,256]{4,2,3,0,1:T(8,128)(2,1)S(1)} %copy.39, pred[8,17]{0,1:T(8,128)(4,1)S(1)} %copy-done.4), kind=kOutput, calls=%fused_computation.12 | convolution fusion | flops 1607471104 | bytes 3494024 | tf_op jit(solution)/shard_map/conv_general_dilated | solution.py:54
  20.3 4.3 %all-to-all-start = ((f32[8,1,512]{2,1,0:T(1,128)}), f32[8,1,512]{2,1,0:T(1,128)S(1)}, u32[]{:S(2)}, u32[]{:S(2)}) async-start(f32[8,1,512]{2,1,0:T(1,128)} %broadcast_in_dim.31), calls=%async_computation | async-start | bytes 32768 | tf_op jit(solution)/shard_map/all_to_all | solution.py:16
  25.2 4.0 %all-to-all-done = f32[8,1,512]{2,1,0:T(1,128)S(1)} async-done(((f32[8,1,512]{2,1,0:T(1,128)}), f32[8,1,512]{2,1,0:T(1,128)S(1)}, u32[]{:S(2)}, u32[]{:S(2)}) %all-to-all-start) | async-done | bytes 16416 | tf_op jit(solution)/shard_map/all_to_all | solution.py:16
  30.0 11.0 %all-to-all-start.1 = ((f32[32,1,512]{2,1,0:T(1,128)}), f32[32,1,512]{2,1,0:T(1,128)S(1)}, u32[]{:S(2)}, u32[]{:S(2)}) async-start(f32[32,1,512]{2,1,0:T(1,128)} %broadcast_in_dim.32), calls=%async_computation.1 | async-start | bytes 131072 | tf_op jit(solution)/shard_map/all_to_all | solution.py:16
  41.0 1.4 %fusion.82 = (f32[1,256]{1,0:T(1,128)}, f32[1,256]{1,0:T(1,128)}, f32[1,256]{1,0:T(1,128)}, f32[1,256]{1,0:T(1,128)}) fusion(f32[4,256]{1,0:T(4,128)} %param.11), kind=kLoop, calls=%fused_computation.111 | loop fusion | bytes 8192 | tf_op jit(solution)/shard_map/slice | solution.py:90
  43.0 6.8 %all-to-all-done.1 = f32[32,1,512]{2,1,0:T(1,128)S(1)} async-done(((f32[32,1,512]{2,1,0:T(1,128)}), f32[32,1,512]{2,1,0:T(1,128)S(1)}, u32[]{:S(2)}, u32[]{:S(2)}) %all-to-all-start.1) | async-done | bytes 65568 | tf_op jit(solution)/shard_map/all_to_all | solution.py:16
  50.5 0.7 slice_multiply_fusion.3
  51.2 1.1 fusion.56
  52.3 2.8 %select_reduce_fusion.5 = (f32[256]{0:T(256)S(1)}, f32[256]{0:T(256)S(1)}, f32[8,8,17,256]{3,1,2,0:T(8,128)S(1)}) fusion(pred[8,17]{0,1:T(8,128)(4,1)S(1)} %copy-done.5, bf16[4,3,3,256,256]{4,3,2,1,0:T(8,128)(2,1)} %param.9, bf16[10,1,7,1,256]{4,2,3,0,1:T(8,128)(2,1)S(1)} %get-tuple-element.16, bf16[10,1,7,1,256]{4,2,3,0,1:T(8,128)(2,1)S(1)} %get-tuple-element.15, ...), kind=kOutput, calls=%fused_computation.32 | convolution fusion | flops 1288740352 | bytes 3063944 | tf_op jit(solution)/shard_map/conv_general_dilated | solution.py:54
  55.1 9.2 %all_to_all.48 = f32[8,1,512]{2,1,0:T(1,128)S(1)} all-to-all(f32[8,1,512]{2,1,0:T(1,128)S(1)} %broadcast_in_dim.33), channel_id=1, replica_groups=mesh['img_0'=8,'img_1'=4,'row_0'=4,'row_1'=2] {'row_0','row_1'}, dimensions={0} | all-to-all | bytes 32768 | tf_op jit(solution)/shard_map/all_to_all | solution.py:16
  64.3 11.9 %all_to_all.49 = f32[32,1,512]{2,1,0:T(1,128)S(1)} all-to-all(f32[32,1,512]{2,1,0:T(1,128)S(1)} %broadcast_in_dim.34), channel_id=1, replica_groups=mesh['img_0'=8,'img_1'=4,'row_0'=4,'row_1'=2] {'img_0','img_1'}, dimensions={0} | all-to-all | bytes 131072 | tf_op jit(solution)/shard_map/all_to_all | solution.py:16
  76.9 0.7 copy-done.3
  78.1 4.0 %collective-permute-start.2 = (bf16[1,2,128,256]{3,1,2,0:T(2,128)(2,1)S(1)}, bf16[1,2,128,256]{3,1,2,0:T(2,128)(2,1)S(1)}, u32[]{:S(2)}, u32[]{:S(2)}) collective-permute-start(bf16[1,2,128,256]{3,1,2,0:T(2,128)(2,1)S(1)} %get-tuple-element.17), channel_id=1, source_target_pairs={{0,1},{1,2},{2,3},{3,4},{4,5},{5,6},{6,7},{8,9},{9,10},{10,11},{11... | collective-permute-start | bytes 393224 | tf_op jit(solution)/shard_map/ppermute | solution.py:47
  82.1 2.1 %collective-permute-start.3 = (bf16[1,2,128,256]{3,1,2,0:T(2,128)(2,1)S(1)}, bf16[1,2,128,256]{3,1,2,0:T(2,128)(2,1)S(1)}, u32[]{:S(2)}, u32[]{:S(2)}) collective-permute-start(bf16[1,2,128,256]{3,1,2,0:T(2,128)(2,1)S(1)} %get-tuple-element.18), channel_id=1, source_target_pairs={{1,0},{2,1},{3,2},{4,3},{5,4},{6,5},{7,6},{9,8},{10,9},{11,10},{12... | collective-permute-start | bytes 393224 | tf_op jit(solution)/shard_map/ppermute | solution.py:48
  84.2 4.2 %collective-permute-done.3 = bf16[1,2,128,256]{3,1,2,0:T(2,128)(2,1)S(1)} collective-permute-done((bf16[1,2,128,256]{3,1,2,0:T(2,128)(2,1)S(1)}, bf16[1,2,128,256]{3,1,2,0:T(2,128)(2,1)S(1)}, u32[]{:S(2)}, u32[]{:S(2)}) %collective-permute-start.3) | collective-permute-done | bytes 131104 | tf_op jit(solution)/shard_map/ppermute | solution.py:48
  88.4 0.8 fusion.22
  89.6 3.1 %convolution_select_fusion = f32[10,8,17,256]{3,1,2,0:T(8,128)S(1)} fusion(bf16[4,3,3,256,256]{4,3,2,1,0:T(8,128)(2,1)} %param.9, bf16[12,1,7,2,256]{4,2,3,0,1:T(8,128)(2,1)S(1)} %slice.123, bf16[12,1,8,17,256]{4,2,3,0,1:T(8,128)(2,1)S(1)} %copy.47, pred[8,17]{0,1:T(8,128)(4,1)S(1)} %copy-done.5), kind=kOutput, calls=%fused_computation.11 | convolution fusion | flops 1607471104 | bytes 3494024 | tf_op jit(solution)/shard_map/conv_general_dilated | solution.py:54
  92.8 1.1 copy-done.1
  94.2 7.9 %all_to_all.50 = f32[8,1,512]{2,1,0:T(1,128)S(1)} all-to-all(f32[8,1,512]{2,1,0:T(1,128)S(1)} %broadcast_in_dim.35), channel_id=1, replica_groups=mesh['img_0'=8,'img_1'=4,'row_0'=4,'row_1'=2] {'row_0','row_1'}, dimensions={0} | all-to-all | bytes 32768 | tf_op jit(solution)/shard_map/all_to_all | solution.py:16
  102.2 11.9 %all_to_all.51 = f32[32,1,512]{2,1,0:T(1,128)S(1)} all-to-all(f32[32,1,512]{2,1,0:T(1,128)S(1)} %broadcast_in_dim.36), channel_id=1, replica_groups=mesh['img_0'=8,'img_1'=4,'row_0'=4,'row_1'=2] {'img_0','img_1'}, dimensions={0} | all-to-all | bytes 131072 | tf_op jit(solution)/shard_map/all_to_all | solution.py:16
  114.2 1.7 %fusion.58 = bf16[10,1,8,17,256]{4,2,3,0,1:T(8,128)(2,1)S(1)} fusion(f32[10,8,17,256]{3,1,2,0:T(8,128)} %copy-done.1, f32[256]{0:T(256)S(1)} %bitcast.76, f32[256]{0:T(256)S(1)} %bitcast.75, f32[256]{0:T(256)S(1)} %get-tuple-element.32, f32[256]{0:T(256)S(1)} %get-tuple-element.31, pred[10]{0:T(512)(128)(4,1)S(1)} %copy-done.13, pred[8,17]{0,1:T(8,128)(4,1)S(1)} %copy-done.5), kind=kLoop, calls=%fused_computation.74 | loop fusion | flops 2785280 | bytes 2093202 | tf_op jit(solution)/shard_map/convert_element_type | solution.py:87
  115.9 3.7 %select_reduce_fusion.1 = (f32[256]{0:T(256)S(1)}, f32[256]{0:T(256)S(1)}, f32[8,8,17,256]{3,1,2,0:T(8,128)}) fusion(pred[8,17]{0,1:T(8,128)(4,1)S(1)} %copy-done.5, bf16[4,3,3,256,256]{4,3,2,1,0:T(8,128)(2,1)} %param.9, bf16[10,1,7,1,256]{4,2,3,0,1:T(8,128)(2,1)S(1)} %get-tuple-element.14, bf16[10,1,7,1,256]{4,2,3,0,1:T(8,128)(2,1)S(1)} %get-tuple-element.13, ...), kind=kOutput, calls=%fused_computation.27 | convolution fusion | flops 1288740352 | bytes 3063944 | tf_op jit(solution)/shard_map/conv_general_dilated | solution.py:54
  119.7 8.9 %all_to_all.52 = f32[8,1,512]{2,1,0:T(1,128)S(1)} all-to-all(f32[8,1,512]{2,1,0:T(1,128)S(1)} %broadcast_in_dim.37), channel_id=1, replica_groups=mesh['img_0'=8,'img_1'=4,'row_0'=4,'row_1'=2] {'row_0','row_1'}, dimensions={0} | all-to-all | bytes 32768 | tf_op jit(solution)/shard_map/all_to_all | solution.py:16
  128.6 11.9 %all_to_all.53 = f32[32,1,512]{2,1,0:T(1,128)S(1)} all-to-all(f32[32,1,512]{2,1,0:T(1,128)S(1)} %broadcast_in_dim.38), channel_id=1, replica_groups=mesh['img_0'=8,'img_1'=4,'row_0'=4,'row_1'=2] {'img_0','img_1'}, dimensions={0} | all-to-all | bytes 131072 | tf_op jit(solution)/shard_map/all_to_all | solution.py:16
  140.7 1.4 multiply_add_fusion
  142.6 0.9 copy.53
  (70 shorter events, 7.5 us)
Async XLA Ops:
  0.0 1.6 %copy-start = (bf16[1,8,128,1024]{3,2,1,0:T(8,128)(2,1)S(1)}, bf16[1,8,128,1024]{3,2,1,0:T(8,128)(2,1)}, u32[]{:S(2)}) copy-start(bf16[1,8,128,1024]{3,2,1,0:T(8,128)(2,1)} %param.6) | copy-start | bytes 6291460
  3.3 11.4 %copy-start.2 = (bf16[1024,256]{1,0:T(8,128)(2,1)}, bf16[1024,256]{1,0:T(8,128)(2,1)S(1)}, u32[]{:S(2)}) copy-start(bf16[1024,256]{1,0:T(8,128)(2,1)S(1)} %fusion.6) | copy-start | bytes 1572868
  3.8 6.5 %collective-permute-start = (bf16[1,2,128,256]{3,1,2,0:T(2,128)(2,1)S(1)}, bf16[1,2,128,256]{3,1,2,0:T(2,128)(2,1)S(1)}, u32[]{:S(2)}, u32[]{:S(2)}) collective-permute-start(bf16[1,2,128,256]{3,1,2,0:T(2,128)(2,1)S(1)} %get-tuple-element.19), channel_id=1, source_target_pairs={{0,1},{1,2},{2,3},{3,4},{4,5},{5,6},{6,7},{8,9},{9,10},{10,11},{11... | collective-permute-start | bytes 393224 | tf_op jit(solution)/shard_map/ppermute | solution.py:47
  8.4 6.3 %collective-permute-start.1 = (bf16[1,2,128,256]{3,1,2,0:T(2,128)(2,1)S(1)}, bf16[1,2,128,256]{3,1,2,0:T(2,128)(2,1)S(1)}, u32[]{:S(2)}, u32[]{:S(2)}) collective-permute-start(bf16[1,2,128,256]{3,1,2,0:T(2,128)(2,1)S(1)} %get-tuple-element.20), channel_id=1, source_target_pairs={{1,0},{2,1},{3,2},{4,3},{5,4},{6,5},{7,6},{9,8},{10,9},{11,10},{12... | collective-permute-start | bytes 393224 | tf_op jit(solution)/shard_map/ppermute | solution.py:48
  15.7 0.7 copy-start.4
  16.3 8.3 %copy-start.12 = (f32[4,256]{1,0:T(4,128)S(1)}, f32[4,256]{1,0:T(4,128)}, u32[]{:S(2)}) copy-start(f32[4,256]{1,0:T(4,128)} %param.10) | copy-start | bytes 12292
  20.3 8.9 %all-to-all-start = ((f32[8,1,512]{2,1,0:T(1,128)}), f32[8,1,512]{2,1,0:T(1,128)S(1)}, u32[]{:S(2)}, u32[]{:S(2)}) async-start(f32[8,1,512]{2,1,0:T(1,128)} %broadcast_in_dim.31), calls=%async_computation | async-start | bytes 32768 | tf_op jit(solution)/shard_map/all_to_all | solution.py:16
  30.0 19.9 %all-to-all-start.1 = ((f32[32,1,512]{2,1,0:T(1,128)}), f32[32,1,512]{2,1,0:T(1,128)S(1)}, u32[]{:S(2)}, u32[]{:S(2)}) async-start(f32[32,1,512]{2,1,0:T(1,128)} %broadcast_in_dim.32), calls=%async_computation.1 | async-start | bytes 131072 | tf_op jit(solution)/shard_map/all_to_all | solution.py:16
  50.5 1.8 %copy-start.5 = (pred[8,17]{0,1:T(8,128)(4,1)S(1)}, pred[8,17]{0,1:T(8,128)(4,1)}, u32[]{:S(2)}) copy-start(pred[8,17]{0,1:T(8,128)(4,1)} %constant.61) | copy-start | bytes 412
  52.3 24.0 %copy-start.10 = (f32[1,256]{1,0:T(1,128)S(1)}, f32[1,256]{1,0:T(1,128)}, u32[]{:S(2)}) copy-start(f32[1,256]{1,0:T(1,128)} %get-tuple-element.22) | copy-start | bytes 3076
  52.3 24.0 %copy-start.11 = (f32[1,256]{1,0:T(1,128)S(1)}, f32[1,256]{1,0:T(1,128)}, u32[]{:S(2)}) copy-start(f32[1,256]{1,0:T(1,128)} %get-tuple-element.26) | copy-start | bytes 3076
  76.5 1.0 copy-start.3
  78.1 6.1 %collective-permute-start.2 = (bf16[1,2,128,256]{3,1,2,0:T(2,128)(2,1)S(1)}, bf16[1,2,128,256]{3,1,2,0:T(2,128)(2,1)S(1)}, u32[]{:S(2)}, u32[]{:S(2)}) collective-permute-start(bf16[1,2,128,256]{3,1,2,0:T(2,128)(2,1)S(1)} %get-tuple-element.17), channel_id=1, source_target_pairs={{0,1},{1,2},{2,3},{3,4},{4,5},{5,6},{6,7},{8,9},{9,10},{10,11},{11... | collective-permute-start | bytes 393224 | tf_op jit(solution)/shard_map/ppermute | solution.py:47
  82.1 6.3 %collective-permute-start.3 = (bf16[1,2,128,256]{3,1,2,0:T(2,128)(2,1)S(1)}, bf16[1,2,128,256]{3,1,2,0:T(2,128)(2,1)S(1)}, u32[]{:S(2)}, u32[]{:S(2)}) collective-permute-start(bf16[1,2,128,256]{3,1,2,0:T(2,128)(2,1)S(1)} %get-tuple-element.18), channel_id=1, source_target_pairs={{1,0},{2,1},{3,2},{4,3},{5,4},{6,5},{7,6},{9,8},{10,9},{11,10},{12... | collective-permute-start | bytes 393224 | tf_op jit(solution)/shard_map/ppermute | solution.py:48
  92.8 1.1 copy-start.1
  93.9 20.3 %copy-start.6 = (f32[1,256]{1,0:T(1,128)S(1)}, f32[1,256]{1,0:T(1,128)}, u32[]{:S(2)}) copy-start(f32[1,256]{1,0:T(1,128)} %get-tuple-element.24) | copy-start | bytes 3076
  93.9 20.3 %copy-start.7 = (f32[1,256]{1,0:T(1,128)S(1)}, f32[1,256]{1,0:T(1,128)}, u32[]{:S(2)}) copy-start(f32[1,256]{1,0:T(1,128)} %get-tuple-element.28) | copy-start | bytes 3076
  93.9 20.3 %copy-start.13 = (pred[10]{0:T(512)(128)(4,1)S(1)}, pred[10]{0:T(512)(128)(4,1)}, u32[]{:S(2)}) copy-start(pred[10]{0:T(512)(128)(4,1)} %or_not_fusion) | copy-start | bytes 34
  115.9 24.7 %copy-start.8 = (f32[1,256]{1,0:T(1,128)S(1)}, f32[1,256]{1,0:T(1,128)}, u32[]{:S(2)}) copy-start(f32[1,256]{1,0:T(1,128)} %get-tuple-element.21) | copy-start | bytes 3076
  115.9 24.7 %copy-start.9 = (f32[1,256]{1,0:T(1,128)S(1)}, f32[1,256]{1,0:T(1,128)}, u32[]{:S(2)}) copy-start(f32[1,256]{1,0:T(1,128)} %get-tuple-element.25) | copy-start | bytes 3076
where the time goes:
time: 144 us; the launch traced here: 143 us
  blocking collectives  61.7 us (43%)
  starting transfers between devices  27.9 us (19%)
  waiting for transfers between devices  19.4 us (13%)
  matrix products  14.5 us (10%)
  local copies, waits for them, and re-layouts  10.4 us (7%)
  other arithmetic  9.33 us (6%)
    all_to_all x6, blocking collectives, sent_to_all(): lax.all_to_all(jnp.broadcast_to(value[None], (devices, *value.shape)), ax...  61.7 us
    all_to_all x2, starting transfers between devices, sent_to_all(): lax.all_to_all(jnp.broadcast_to(value[None], (devices, *value.shape)), ax...  15.3 us
    conv_general_dilated x4, matrix products, conv_valid(): lax.conv_general_dilated(padded, kernel, (1, 1), ((0, 0), (1, 1)), dimens...  12.7 us
    all_to_all x2, waiting for transfers between devices, sent_to_all(): lax.all_to_all(jnp.broadcast_to(value[None], (devices, *value.shape)), ax...  10.8 us
    ppermute x2, starting transfers between devices, extended(): before = lax.ppermute(last, axis, up)  8.54 us
    ppermute x2, waiting for transfers between devices, extended(): after = lax.ppermute(leading, axis, down)  8.52 us
    ppermute x2, starting transfers between devices, extended(): after = lax.ppermute(leading, axis, down)  4.02 us
    unnamed x28, local copies, waits for them, and re-layouts  3.76 us
  transfers between devices with their start and end apart: 6, of which 4 were waited for; matrix products, arithmetic and copies ran while one was open for 2% of the time, Pallas kernels for 0%

commit v1 on v0

v1 whole, which is shorter than its diff:
```python
import functools

import jax
import jax.numpy as jnp
from jax import lax
from jax.experimental import pallas as pl
from jax.experimental.pallas import tpu as pltpu
from jax.sharding import PartitionSpec as P

EPS = 1e-05
HALO = 4
STEP = 4
AHEAD = 0
VM = pl.BlockSpec(memory_space=pltpu.VMEM)
HBM = pl.BlockSpec(memory_space=pltpu.HBM)
BF = jnp.bfloat16
F32 = jnp.float32
PARAMS = pltpu.CompilerParams(vmem_limit_bytes=24 << 20)


def sds(shape, dtype):
    return jax.ShapeDtypeStruct(shape, dtype)


def in_hbm(x):
    return pltpu.with_memory_space_constraint(x, pltpu.HBM)


def in_vmem(x):
    return pltpu.with_memory_space_constraint(x, pltpu.VMEM)


def put_row(a3, row, x):
    cols, ch = x.shape
    col = lax.broadcasted_iota(jnp.int32, x.shape, 0)
    a3[row, :, ch : 2 * ch] = x.astype(BF)
    a3[row, :, 0:ch] = jnp.where(col == 0, 0.0, pltpu.roll(x, 1, 0)).astype(BF)
    a3[row, :, 2 * ch :] = jnp.where(col == cols - 1, 0.0, pltpu.roll(x, cols - 1, 0)).astype(BF)


def conv_block(a3, wbuf, first, rows):
    cols, k = a3.shape[1:]
    acc = None
    for dy in range(3):
        lhs = a3[first + dy : first + dy + rows].reshape(rows * cols, k)
        part = jnp.dot(lhs, wbuf[dy].reshape(k, -1), preferred_element_type=F32)
        acc = part if acc is None else acc + part
    return acc


def fold8(x):
    return x.reshape(-1, 8, x.shape[-1]).sum(axis=0)


def norm_terms(stats_ref, gain_ref, bias_ref, k, total):
    s = jnp.sum(stats_ref[...], axis=0)
    ch = s.shape[-1] // 2
    mean = s[:, :ch] / total
    spread = jnp.maximum(s[:, ch:] / total - mean * mean, 0.0)
    return mean, lax.rsqrt(spread + EPS) * gain_ref[k : k + 1, :], bias_ref[k : k + 1, :]


def write_stats(out_ref, sums, squares):
    both = jnp.concatenate(
        [jnp.sum(sums, axis=0, keepdims=True), jnp.sum(squares, axis=0, keepdims=True)], axis=1
    )
    out_ref[...] = jnp.broadcast_to(both[None], out_ref.shape)


def inside(local_row, strip, axis):
    if 0 <= local_row < strip:
        return None
    r = lax.axis_index(axis)
    edge = r > 0 if local_row < 0 else r < lax.axis_size(axis) - 1
    return edge.astype(F32)


def masked(x, m):
    return x if m is None else x * m


def load_weights(w, k, wbuf, sems):
    copies = [pltpu.make_async_copy(w.at[k, dy], wbuf.at[dy], sems.at[dy]) for dy in range(3)]
    for c in copies:
        c.start()
    return copies


def run_conv(row_at, n_in, a3, wbuf, waits, c_ref, at, lo, strip, sums=None, squares=None):
    cols, ch = c_ref.shape[1:]
    n_out = n_in - 2
    filled = done = 0
    while done < n_out:
        rows = min(STEP, n_out - done)
        while filled < min(n_in, done + rows + 2 + AHEAD):
            put_row(a3, filled, row_at(filled))
            filled += 1
        while waits:
            waits.pop(0).wait()
        acc = conv_block(a3, wbuf, done, rows)
        c_ref[at + done : at + done + rows] = acc.reshape(rows, cols, ch)
        own_from = max(0, -(lo + done))
        own_to = min(rows, strip - (lo + done))
        if own_to > own_from:
            own = acc[own_from * cols : own_to * cols]
            s, q = fold8(own), fold8(own * own)
            sums = s if sums is None else sums + s
            squares = q if squares is None else squares + q
        done += rows
    return sums, squares


def proj_kernel(tok, w, bias, top, bot, tbuf, wbuf, sems):
    rows = tok.shape[0]
    cw = pltpu.make_async_copy(w, wbuf, sems.at[rows])
    cw.start()
    copies = [pltpu.make_async_copy(tok.at[i], tbuf.at[i], sems.at[i]) for i in range(rows)]
    for c in copies:
        c.start()
    cw.wait()
    half = rows // 2
    for i in range(0, rows, 2):
        copies[i].wait()
        copies[i + 1].wait()
        x = tbuf[i : i + 2].reshape(-1, tok.shape[2])
        y = jnp.dot(x, wbuf[...], preferred_element_type=F32) + bias[...]
        y = y.astype(BF).reshape(2, tok.shape[1], -1)
        if i < half:
            top[i : i + 2] = y
        else:
            bot[i - half : i - half + 2] = y


def relu_row(x):
    return jnp.maximum(x.astype(F32), 0.0)


def conv0_inner_kernel(top, bot, w, c_ref, wbuf, part, a3, sems, *, strip):
    waits = load_weights(w, 0, wbuf, sems)

    def row_at(i):
        return relu_row(top[i] if i < HALO else bot[i - HALO])

    sums, squares = run_conv(row_at, strip, a3, wbuf, waits, c_ref, HALO, 1, strip)
    part[0] = sums
    part[1] = squares


def conv0_outer_kernel(before, top, bot, after, wbuf, part, c_in, c_ref, st, a3, *, strip):
    sums, squares = part[0], part[1]

    def upper(i):
        return relu_row(before[i] if i < HALO else top[i - HALO])

    sums, squares = run_conv(upper, HALO + 2, a3, wbuf, [], c_ref, 0, 1 - HALO, strip, sums, squares)

    def lower(i):
        return relu_row(bot[i + HALO - 2] if i < 2 else after[i - 2])

    sums, squares = run_conv(
        lower, HALO + 2, a3, wbuf, [], c_ref, strip + HALO - 2, strip - 1, strip, sums, squares
    )
    write_stats(st, sums, squares)


def hidden_conv_kernel(c_in, stats, gain, shift, w, c_ref, st, a3, wbuf, sems, *, k, lo, n_in, strip, total, axis):
    waits = load_weights(w, k + 1, wbuf, sems)
    mean, scale, bias = norm_terms(stats, gain, shift, k, total)

    def row_at(i):
        x = jnp.maximum((c_in[i] - mean) * scale + bias, 0.0)
        return masked(x, inside(lo + i, strip, axis))

    sums, squares = run_conv(row_at, n_in, a3, wbuf, waits, c_ref, 0, lo + 1, strip)
    write_stats(st, sums, squares)


def joined_conv_kernel(
    c_in, stats, gain, shift, before, top, bot, after, w, c_ref, st, joined, a3, wbuf, sems,
    *, k, lo, n_in, strip, total, axis
):
    waits = load_weights(w, k + 1, wbuf, sems)
    mean, scale, bias = norm_terms(stats, gain, shift, k, total)
    parts = (before, top, bot, after)

    def row_at(i):
        local = lo + i
        f = parts[(local + HALO) // HALO][(local + HALO) % HALO].astype(F32)
        y = (f + ((c_in[i] - mean) * scale + bias)).astype(BF)
        if 0 <= local < strip:
            joined[local] = y
        return masked(relu_row(y), inside(local, strip, axis))

    sums, squares = run_conv(row_at, n_in, a3, wbuf, waits, c_ref, 0, lo + 1, strip)
    write_stats(st, sums, squares)


def final_kernel(joined, c_in, stats, gain, shift, out, *, k, total):
    mean, scale, bias = norm_terms(stats, gain, shift, k, total)
    for i in range(out.shape[0]):
        out[i] = (joined[i].astype(F32) + ((c_in[i] - mean) * scale + bias)).astype(BF)


def sent_to_all(value, axis):
    return lax.all_to_all(value, axis, 0, 0, tiled=True)


def reduce_all(partial):
    near = sent_to_all(partial, "row").sum(axis=0)
    far = lax.axis_size("img")
    return sent_to_all(jnp.broadcast_to(near[None], (far, *near.shape)), "img")


def on_device(tokens, proj_weight, proj_bias, conv_weight, bn_gain, bn_bias):
    imgs, strip, cols, embed = tokens.shape
    ch = proj_weight.shape[1]
    nrow = lax.axis_size("row")
    total = float(lax.axis_size("img") * nrow * imgs * strip * cols)
    weights = in_hbm(conv_weight)
    norm_args = (bn_gain, bn_bias)

    half = sds((HALO, cols, ch), BF)
    top, bot = pl.pallas_call(
        proj_kernel,
        out_shape=(half, half),
        in_specs=[HBM, HBM, VM],
        out_specs=(VM, VM),
        scratch_shapes=[
            pltpu.VMEM((strip, cols, embed), BF),
            pltpu.VMEM((embed, ch), BF),
            pltpu.SemaphoreType.DMA((strip + 1,)),
        ],
        compiler_params=PARAMS,
    )(in_hbm(tokens[0]), in_hbm(proj_weight), proj_bias[None])
    before = lax.ppermute(bot, "row", [(i, i + 1) for i in range(nrow - 1)])
    after = lax.ppermute(top, "row", [(i + 1, i) for i in range(nrow - 1)])
    top, bot, before, after = map(in_vmem, (top, bot, before, after))

    field = sds((strip + 2 * HALO - 2, cols, ch), F32)
    stat = sds((nrow, 1, 2 * ch), F32)
    wshape = (3, 3, ch, ch)

    def rows_scratch(rows):
        return pltpu.VMEM((rows, cols, 3 * ch), BF)

    wsems = pltpu.SemaphoreType.DMA((3,))
    c0, w0, part = pl.pallas_call(
        functools.partial(conv0_inner_kernel, strip=strip),
        out_shape=(field, sds(wshape, BF), sds((2, 8, ch), F32)),
        in_specs=[VM, VM, HBM],
        out_specs=(VM, VM, VM),
        scratch_shapes=[rows_scratch(strip), wsems],
        compiler_params=PARAMS,
        cost_estimate=pl.CostEstimate(
            flops=2 * 9 * ch * ch * cols * (strip - 2), transcendentals=0, bytes_accessed=9 * ch * ch * 2
        ),
    )(top, bot, weights)
    c0, st = pl.pallas_call(
        functools.partial(conv0_outer_kernel, strip=strip),
        out_shape=(field, stat),
        in_specs=[VM] * 7,
        out_specs=(VM, VM),
        input_output_aliases={6: 0},
        scratch_shapes=[rows_scratch(HALO + 2)],
        compiler_params=PARAMS,
    )(before, top, bot, after, in_vmem(w0), in_vmem(part), in_vmem(c0))

    def call(kernel, c, st, features, extra_out, n_in, **kw):
        args = (in_vmem(c), in_vmem(st), *norm_args, *features)
        return pl.pallas_call(
            functools.partial(kernel, n_in=n_in, strip=strip, total=total, axis="row", **kw),
            out_shape=(field, stat, *extra_out),
            in_specs=[VM] * len(args) + [HBM],
            out_specs=(VM,) * (2 + len(extra_out)),
            input_output_aliases={0: 0},
            scratch_shapes=[rows_scratch(n_in), pltpu.VMEM(wshape, BF), wsems],
            compiler_params=PARAMS,
        )(*args, weights)

    st = reduce_all(st)
    c1, st = call(hidden_conv_kernel, c0, st, (), (), strip + 6, k=0, lo=-3)
    st = reduce_all(st)
    c2, st, joined = call(
        joined_conv_kernel, c1, st, (before, top, bot, after), (sds((strip, cols, ch), BF),), strip + 4, k=1, lo=-2
    )
    st = reduce_all(st)
    c3, st = call(hidden_conv_kernel, c2, st, (), (), strip + 2, k=2, lo=-1)
    st = reduce_all(st)
    out = pl.pallas_call(
        functools.partial(final_kernel, k=3, total=total),
        out_shape=sds((strip, cols, ch), BF),
        in_specs=[VM] * 5,
        out_specs=VM,
        compiler_params=PARAMS,
    )(in_vmem(joined), in_vmem(c3), in_vmem(st), *norm_args)
    return out[None]


def solution(mesh):
    placed = (P("img", "row", None, None), P(), P(), P(), P(), P())
    return jax.shard_map(
        on_device, mesh=mesh, in_specs=placed, out_specs=P("img", "row", None, None), check_vma=False
    )
```

time: 144 us -> 119 us (0.83)
  blocking collectives: 61.7 us -> 91 us
  starting transfers between devices: 27.9 us -> 6.5 us
  Pallas kernels: 0 us -> 16.9 us
  waiting for transfers between devices: 19.4 us -> 3.39 us
  matrix products: 14.5 us -> 0 us
  local copies, waits for them, and re-layouts: 10.4 us -> 0.84 us
  other arithmetic: 9.33 us -> 0.12 us
    all_to_all x6 -> x8, blocking collectives: 61.7 us -> 91 us  [sent_to_all(): return lax.all_to_all(value, axis, 0, 0, tiled=True)]
    pallas_call x0 -> x7, Pallas kernels: none -> 16.9 us  [the longest x3 9.17 us: call(): pl.pallas_call(functools.partial(kernel, n_in=n_in, strip=strip, total=to...]
    all_to_all x2 -> x0, starting transfers between devices: 15.3 us -> none  [sent_to_all(): lax.all_to_all(jnp.broadcast_to(value[None], (devices, *value.shape)), ax...]
    conv_general_dilated x4 -> x0, matrix products: 12.7 us -> none  [conv_valid(): lax.conv_general_dilated(padded, kernel, (1, 1), ((0, 0), (1, 1)), dimens...]
    all_to_all x2 -> x0, waiting for transfers between devices: 10.8 us -> none  [sent_to_all(): lax.all_to_all(jnp.broadcast_to(value[None], (devices, *value.shape)), ax...]
    ppermute x4 -> x2, starting transfers between devices: 12.6 us -> 6.5 us  [the longest x1 4.58 us: on_device(): before = lax.ppermute(bot, 'row', [(i, i + 1) for i in range(nrow - 1)])]
    ppermute x4 -> x2, waiting for transfers between devices: 8.52 us -> 3.39 us  [the longest x1 3.38 us: on_device(): after = lax.ppermute(top, 'row', [(i + 1, i) for i in range(nrow - 1)])]
    convert_element_type x4 -> x0, other arithmetic: 3.24 us -> none  [the longest x2 2.76 us: residual_unit(): jnp.where(inside[None, :, None, None], jax.nn.relu(normed), 0.0)]
  transfers between devices with their start and end apart: 6 -> 2, of which waited for: 4 -> 1; matrix products, arithmetic and copies ran while one was open for 2% -> 0% of each run, Pallas kernels for 0% -> 2%
where the time goes in v1:
time: 119 us
  blocking collectives  91 us (76%)
  Pallas kernels  16.9 us (14%)
  starting transfers between devices  6.5 us (5%)
  waiting for transfers between devices  3.39 us (3%)
    all_to_all x8, blocking collectives, sent_to_all(): return lax.all_to_all(value, axis, 0, 0, tiled=True)  91 us
    pallas_call x3, Pallas kernels, call(): pl.pallas_call(functools.partial(kernel, n_in=n_in, strip=strip, total=to...  9.17 us
    ppermute x1, starting transfers between devices, on_device(): before = lax.ppermute(bot, 'row', [(i, i + 1) for i in range(nrow - 1)])  4.58 us
    ppermute x1, waiting for transfers between devices, on_device(): after = lax.ppermute(top, 'row', [(i + 1, i) for i in range(nrow - 1)])  3.38 us
    pallas_call x1, Pallas kernels, on_device(): pl.pallas_call(proj_kernel, out_shape=(half, half), in_specs=[HBM, HBM, V...  2.95 us
  transfers between devices with their start and end apart: 2, of which 1 were waited for; matrix products, arithmetic and copies ran while one was open for 0% of the time, Pallas kernels for 2%

profile of v1, /device:TPU:1, one launch (start us, length us, event | category | flops | bytes accessed | tf_op | source)
XLA Modules:
  0.0 118.9 jit_solution(9140446946937340598)
XLA Ops:
  0.0 0.0 copy-start.2
  0.0 0.7 copy-done.2
  0.7 3.0 %shard_map.64 = (bf16[4,128,256]{2,1,0:T(8,128)(2,1)S(1)}, bf16[4,128,256]{2,1,0:T(8,128)(2,1)S(1)}) custom-call(bf16[8,128,1024]{2,1,0:T(8,128)(2,1)} %bitcast.4, bf16[1024,256]{1,0:T(8,128)(2,1)} %w.5, f32[1,256]{1,0:T(1,128)S(1)} %bitcast.3), custom_call_target="tpu_custom_call" | custom-call | tf_op jit(solution)/shard_map/pallas_call | solution.py:223
  3.6 4.6 %collective-permute-start = (bf16[4,128,256]{2,1,0:T(8,128)(2,1)S(1)}, bf16[4,128,256]{2,1,0:T(8,128)(2,1)S(1)}, u32[]{:S(2)}, u32[]{:S(2)}) collective-permute-start(bf16[4,128,256]{2,1,0:T(8,128)(2,1)S(1)} %get-tuple-element.19.bot), channel_id=1, source_target_pairs={{0,1},{1,2},{2,3},{3,4},{4,5},{5,6},{6,7},{8,9},{9,10},{10,11},{11... | collective-permute-start | bytes 786440 | tf_op jit(solution)/shard_map/ppermute | solution.py:235
  8.2 1.9 %collective-permute-start.1 = (bf16[4,128,256]{2,1,0:T(8,128)(2,1)S(1)}, bf16[4,128,256]{2,1,0:T(8,128)(2,1)S(1)}, u32[]{:S(2)}, u32[]{:S(2)}) collective-permute-start(bf16[4,128,256]{2,1,0:T(8,128)(2,1)S(1)} %get-tuple-element.20.top), channel_id=1, source_target_pairs={{1,0},{2,1},{3,2},{4,3},{5,4},{6,5},{7,6},{9,8},{10,9},{11,10},{12... | collective-permute-start | bytes 786440 | tf_op jit(solution)/shard_map/ppermute | solution.py:236
  10.2 2.4 %shard_map.65 = (f32[14,128,256]{2,1,0:T(8,128)S(1)}, bf16[3,3,256,256]{3,2,1,0:T(8,128)(2,1)S(1)}, f32[2,8,256]{2,1,0:T(8,128)S(1)}) custom-call(bf16[4,128,256]{2,1,0:T(8,128)(2,1)S(1)} %get-tuple-element.20.top, bf16[4,128,256]{2,1,0:T(8,128)(2,1)S(1)} %get-tuple-element.19.bot, bf16[4,3,3,256,256]{4,3,2,1,0:T(8,128)(2,1)} %w.9), custom_call_target="tpu_custom_call" | custom-call | flops 905969664 | bytes 1179648 | tf_op jit(solution)/shard_map/pallas_call | solution.py:247
  12.5 0.0 collective-permute-done.before
  12.5 3.4 %collective-permute-done.1.after = bf16[4,128,256]{2,1,0:T(8,128)(2,1)S(1)} collective-permute-done((bf16[4,128,256]{2,1,0:T(8,128)(2,1)S(1)}, bf16[4,128,256]{2,1,0:T(8,128)(2,1)S(1)}, u32[]{:S(2)}, u32[]{:S(2)}) %collective-permute-start.1) | collective-permute-done | bytes 262176 | tf_op jit(solution)/shard_map/ppermute | solution.py:236
  15.9 0.0 copy-start
  15.9 0.0 copy-start.1
  15.9 1.4 %shard_map.66 = (f32[14,128,256]{2,1,0:T(8,128)S(1)}, f32[8,1,512]{2,1,0:T(1,128)S(1)}) custom-call(bf16[4,128,256]{2,1,0:T(8,128)(2,1)S(1)} %collective-permute-done.before, bf16[4,128,256]{2,1,0:T(8,128)(2,1)S(1)} %get-tuple-element.20.top, bf16[4,128,256]{2,1,0:T(8,128)(2,1)S(1)} %get-tuple-element.19.bot, ...), custom_call_target="tpu_custom_call", output_to_operand_aliasing={{0}: (6, {})} | custom-call | tf_op jit(solution)/shard_map/pallas_call | solution.py:258
  17.3 8.7 %all_to_all.40 = f32[8,1,512]{2,1,0:T(1,128)S(1)} all-to-all(f32[8,1,512]{2,1,0:T(1,128)S(1)} %get-tuple-element.25), channel_id=1, replica_groups=mesh['img'=32,'row'=8] {'row'}, dimensions={0} | all-to-all | bytes 32768 | tf_op jit(solution)/shard_map/all_to_all | solution.py:205
  26.2 19.6 %all_to_all.41.stats = f32[32,1,512]{2,1,0:T(1,128)S(1)} all-to-all(f32[32,1,512]{2,1,0:T(1,128)S(1)} %broadcast_in_dim.13), channel_id=1, replica_groups=mesh['img'=32,'row'=8] {'img'}, dimensions={0} | all-to-all | bytes 131072 | tf_op jit(solution)/shard_map/all_to_all | solution.py:205
  45.8 0.0 copy-done
  45.8 0.0 copy-done.1
  45.8 3.5 %shard_map.67 = (f32[14,128,256]{2,1,0:T(8,128)S(1)}, f32[8,1,512]{2,1,0:T(1,128)S(1)}) custom-call(f32[14,128,256]{2,1,0:T(8,128)S(1)} %get-tuple-element.24.c_in, f32[32,1,512]{2,1,0:T(1,128)S(1)} %all_to_all.41.stats, f32[4,256]{1,0:T(4,128)S(1)} %copy-done, f32[4,256]{1,0:T(4,128)S(1)} %copy-done.1, ...), custom_call_target="tpu_custom_call", output_to_operand_aliasing={{0}: (0, {})} | custom-call | tf_op jit(solution)/shard_map/pallas_call | solution.py:270
  49.3 9.1 %all_to_all.42 = f32[8,1,512]{2,1,0:T(1,128)S(1)} all-to-all(f32[8,1,512]{2,1,0:T(1,128)S(1)} %get-tuple-element.27), channel_id=1, replica_groups=mesh['img'=32,'row'=8] {'row'}, dimensions={0} | all-to-all | bytes 32768 | tf_op jit(solution)/shard_map/all_to_all | solution.py:205
  58.5 11.9 %all_to_all.43.stats = f32[32,1,512]{2,1,0:T(1,128)S(1)} all-to-all(f32[32,1,512]{2,1,0:T(1,128)S(1)} %broadcast_in_dim.14), channel_id=1, replica_groups=mesh['img'=32,'row'=8] {'img'}, dimensions={0} | all-to-all | bytes 131072 | tf_op jit(solution)/shard_map/all_to_all | solution.py:205
  70.5 3.0 %shard_map.68 = (f32[14,128,256]{2,1,0:T(8,128)S(1)}, f32[8,1,512]{2,1,0:T(1,128)S(1)}, bf16[8,128,256]{2,1,0:T(8,128)(2,1)S(1)}) custom-call(f32[14,128,256]{2,1,0:T(8,128)S(1)} %get-tuple-element.26.c_in, f32[32,1,512]{2,1,0:T(1,128)S(1)} %all_to_all.43.stats, f32[4,256]{1,0:T(4,128)S(1)} %copy-done, ...), custom_call_target="tpu_custom_call", output_to_operand_aliasing={{0}: (0, {})} | custom-call | tf_op jit(solution)/shard_map/pallas_call | solution.py:270
  73.5 8.9 %all_to_all.44 = f32[8,1,512]{2,1,0:T(1,128)S(1)} all-to-all(f32[8,1,512]{2,1,0:T(1,128)S(1)} %get-tuple-element.30), channel_id=1, replica_groups=mesh['img'=32,'row'=8] {'row'}, dimensions={0} | all-to-all | bytes 32768 | tf_op jit(solution)/shard_map/all_to_all | solution.py:205
  82.4 11.9 %all_to_all.45.stats = f32[32,1,512]{2,1,0:T(1,128)S(1)} all-to-all(f32[32,1,512]{2,1,0:T(1,128)S(1)} %broadcast_in_dim.15), channel_id=1, replica_groups=mesh['img'=32,'row'=8] {'img'}, dimensions={0} | all-to-all | bytes 131072 | tf_op jit(solution)/shard_map/all_to_all | solution.py:205
  94.3 2.7 %shard_map.69 = (f32[14,128,256]{2,1,0:T(8,128)S(1)}, f32[8,1,512]{2,1,0:T(1,128)S(1)}) custom-call(f32[14,128,256]{2,1,0:T(8,128)S(1)} %get-tuple-element.29.c_in, f32[32,1,512]{2,1,0:T(1,128)S(1)} %all_to_all.45.stats, f32[4,256]{1,0:T(4,128)S(1)} %copy-done, f32[4,256]{1,0:T(4,128)S(1)} %copy-done.1, ...), custom_call_target="tpu_custom_call", output_to_operand_aliasing={{0}: (0, {})} | custom-call | tf_op jit(solution)/shard_map/pallas_call | solution.py:270
  97.0 8.9 %all_to_all.46 = f32[8,1,512]{2,1,0:T(1,128)S(1)} all-to-all(f32[8,1,512]{2,1,0:T(1,128)S(1)} %get-tuple-element.32), channel_id=1, replica_groups=mesh['img'=32,'row'=8] {'row'}, dimensions={0} | all-to-all | bytes 32768 | tf_op jit(solution)/shard_map/all_to_all | solution.py:205
  106.0 11.9 %all_to_all.47.stats = f32[32,1,512]{2,1,0:T(1,128)S(1)} all-to-all(f32[32,1,512]{2,1,0:T(1,128)S(1)} %broadcast_in_dim.16), channel_id=1, replica_groups=mesh['img'=32,'row'=8] {'img'}, dimensions={0} | all-to-all | bytes 131072 | tf_op jit(solution)/shard_map/all_to_all | solution.py:205
  117.9 1.0 shard_map.70
  (8 shorter events, 0.3 us)
Async XLA Ops:
  0.0 0.7 copy-start.2
  3.6 8.9 %collective-permute-start = (bf16[4,128,256]{2,1,0:T(8,128)(2,1)S(1)}, bf16[4,128,256]{2,1,0:T(8,128)(2,1)S(1)}, u32[]{:S(2)}, u32[]{:S(2)}) collective-permute-start(bf16[4,128,256]{2,1,0:T(8,128)(2,1)S(1)} %get-tuple-element.19.bot), channel_id=1, source_target_pairs={{0,1},{1,2},{2,3},{3,4},{4,5},{5,6},{6,7},{8,9},{9,10},{10,11},{11... | collective-permute-start | bytes 786440 | tf_op jit(solution)/shard_map/ppermute | solution.py:235
  8.2 7.7 %collective-permute-start.1 = (bf16[4,128,256]{2,1,0:T(8,128)(2,1)S(1)}, bf16[4,128,256]{2,1,0:T(8,128)(2,1)S(1)}, u32[]{:S(2)}, u32[]{:S(2)}) collective-permute-start(bf16[4,128,256]{2,1,0:T(8,128)(2,1)S(1)} %get-tuple-element.20.top), channel_id=1, source_target_pairs={{1,0},{2,1},{3,2},{4,3},{5,4},{6,5},{7,6},{9,8},{10,9},{11,10},{12... | collective-permute-start | bytes 786440 | tf_op jit(solution)/shard_map/ppermute | solution.py:236
  15.9 29.9 %copy-start = (f32[4,256]{1,0:T(4,128)S(1)}, f32[4,256]{1,0:T(4,128)}, u32[]{:S(2)}) copy-start(f32[4,256]{1,0:T(4,128)} %gain.7) | copy-start | bytes 12292
  15.9 29.9 %copy-start.1 = (f32[4,256]{1,0:T(4,128)S(1)}, f32[4,256]{1,0:T(4,128)}, u32[]{:S(2)}) copy-start(f32[4,256]{1,0:T(4,128)} %shift.7) | copy-start | bytes 12292

commit v2 on v1

v2 whole, which is shorter than its diff:
```python
import functools

import jax
import jax.numpy as jnp
from jax import lax
from jax.experimental import pallas as pl
from jax.experimental.pallas import tpu as pltpu
from jax.sharding import PartitionSpec as P

EPS = 1e-05
HALO = 4
STEP = 2
PROWS = 8
TROWS = 1
DELAY = 0
LATE = 0
AHEAD = 0
VM = pl.BlockSpec(memory_space=pltpu.VMEM)
HBM = pl.BlockSpec(memory_space=pltpu.HBM)
BF = jnp.bfloat16
F32 = jnp.float32
PARAMS = pltpu.CompilerParams(vmem_limit_bytes=24 << 20)


def sds(shape, dtype):
    return jax.ShapeDtypeStruct(shape, dtype)


def in_hbm(x):
    return pltpu.with_memory_space_constraint(x, pltpu.HBM)


def in_vmem(x):
    return pltpu.with_memory_space_constraint(x, pltpu.VMEM)


def put_row(a3, row, x):
    cols, ch = x.shape
    col = lax.broadcasted_iota(jnp.int32, x.shape, 0)
    a3[row, :, ch : 2 * ch] = x.astype(BF)
    a3[row, :, 0:ch] = jnp.where(col == 0, 0.0, pltpu.roll(x, 1, 0)).astype(BF)
    a3[row, :, 2 * ch :] = jnp.where(col == cols - 1, 0.0, pltpu.roll(x, cols - 1, 0)).astype(BF)


def fold8(x):
    return x.reshape(-1, 8, x.shape[-1]).sum(axis=0)


def norm_terms(stats_ref, gain_ref, bias_ref, k, total):
    s = jnp.sum(stats_ref[...], axis=0)
    ch = s.shape[-1] // 2
    mean = s[:, :ch] / total
    spread = jnp.maximum(s[:, ch:] / total - mean * mean, 0.0)
    return mean, lax.rsqrt(spread + EPS) * gain_ref[k : k + 1, :], bias_ref[k : k + 1, :]


def write_stats(out_ref, sums, squares):
    both = jnp.concatenate(
        [jnp.sum(sums, axis=0, keepdims=True), jnp.sum(squares, axis=0, keepdims=True)], axis=1
    )
    out_ref[...] = jnp.broadcast_to(both[None], out_ref.shape)


def inside(local_row, strip, axis):
    if 0 <= local_row < strip:
        return None
    r = lax.axis_index(axis)
    edge = r > 0 if local_row < 0 else r < lax.axis_size(axis) - 1
    return edge.astype(F32)


def masked(x, m):
    return x if m is None else x * m


def run_conv(row_at, n_in, a3, w_parts, waits, c_ref, at, lo, strip, sums=None, squares=None, starts=((), ())):
    cols, ch = c_ref.shape[1:]
    n_out = n_in - 2
    filled = 0
    for dy in range(3):
        for copy in waits[dy]:
            copy.wait()
        for copy in starts[dy - 1] if dy else ():
            copy.start()
        w = w_parts[dy][...].reshape(3 * ch, ch)
        for done in range(0, n_out, STEP):
            rows = min(STEP, n_out - done)
            while filled < min(n_in, done + rows + dy + AHEAD):
                put_row(a3, filled, row_at(filled))
                filled += 1
            lhs = a3[done + dy : done + dy + rows].reshape(rows * cols, 3 * ch)
            acc = jnp.dot(lhs, w, preferred_element_type=F32)
            into = slice(at + done, at + done + rows)
            if dy:
                acc = acc + c_ref[into].reshape(rows * cols, ch)
            c_ref[into] = acc.reshape(rows, cols, ch)
            own_from = max(0, -(lo + done))
            own_to = min(rows, strip - (lo + done))
            if dy == 2 and own_to > own_from:
                own = acc[own_from * cols : own_to * cols]
                s, q = fold8(own), fold8(own * own)
                sums = s if sums is None else sums + s
                squares = q if squares is None else squares + q
    return sums, squares


def proj_kernel(tok, w, bias, top, bot, tbuf, wbuf, bbuf, sems):
    rows = tok.shape[0]
    first = [pltpu.make_async_copy(w, wbuf, sems.at[rows]), pltpu.make_async_copy(bias, bbuf, sems.at[rows + 1])]
    copies = [
        pltpu.make_async_copy(tok.at[i : i + TROWS], tbuf.at[i : i + TROWS], sems.at[i]) for i in range(0, rows, TROWS)
    ]
    for c in first:
        c.start()
    for i, c in enumerate(copies):
        if DELAY and i * TROWS == rows // 2:
            pl.delay(DELAY)
        c.start()
    for c in first:
        c.wait()
    half = rows // 2
    for i in range(0, rows, PROWS):
        for c in copies[i // TROWS : (i + PROWS + TROWS - 1) // TROWS]:
            c.wait()
        x = tbuf[i : i + PROWS].reshape(-1, tok.shape[2])
        y = jnp.dot(x, wbuf[...], preferred_element_type=F32) + bbuf[...]
        y = y.astype(BF).reshape(PROWS, tok.shape[1], -1)
        for j in range(PROWS):
            (top if i + j < half else bot)[(i + j) % half] = y[j]


def relu_row(x):
    return jnp.maximum(x.astype(F32), 0.0)


def conv0_inner_kernel(top, bot, cw, c_ref, part, w0, a3, sems, *, strip):
    waits = [[pltpu.make_async_copy(cw.at[0, dy], w0.at[dy], sems.at[dy])] for dy in range(3)]
    for (copy,) in waits:
        copy.start()

    def row_at(i):
        return relu_row(top[i] if i < HALO else bot[i - HALO])

    w_parts = [w0.at[dy] for dy in range(3)]
    part[0], part[1] = run_conv(row_at, strip, a3, w_parts, waits, c_ref, HALO, 1, strip)


def conv0_outer_kernel(before, top, bot, after, w0, part, c_in, cw, c_ref, st, feature, w_next, a3, sem, *, strip):
    late = pltpu.make_async_copy(cw.at[1, 0], w_next, sem)
    late.start()
    w_parts = [w0.at[dy] for dy in range(3)]

    def upper(i):
        return relu_row(before[i] if i < HALO else top[i - HALO])

    sums, squares = run_conv(
        upper, HALO + 2, a3.at[: HALO + 2], w_parts, [[]] * 3, c_ref, 0, 1 - HALO, strip, part[0], part[1]
    )

    def lower(i):
        return relu_row(bot[i + HALO - 2] if i < 2 else after[i - 2])

    sums, squares = run_conv(
        lower, HALO + 2, a3.at[HALO + 2 :], w_parts, [[]] * 3, c_ref, strip + HALO - 2, strip - 1, strip, sums, squares
    )
    write_stats(st, sums, squares)
    feature[0:2] = before[HALO - 2 :]
    feature[2 : HALO + 2] = top[...]
    feature[HALO + 2 : strip + 2] = bot[...]
    feature[strip + 2 :] = after[0:2]
    late.wait()


def weight_copies(cw, k, wbuf, w_next, sems):
    waits = [[]] + [[pltpu.make_async_copy(cw.at[k, dy], wbuf.at[dy - 1], sems.at[dy - 1])] for dy in (1, 2)]
    late = []
    if w_next is not None:
        late.append(pltpu.make_async_copy(cw.at[k + 1, 0], w_next, sems.at[2]))
    for c in waits[1]:
        c.start()
    after = [waits[2], [], []]
    after[LATE] = after[LATE] + late
    for c in after[0]:
        c.start()
    return waits, late, after[1:]


def hidden_conv_kernel(
    c_in, stats, gain, shift, w_first, cw, c_ref, st, *rest, k, lo, n_in, strip, total, axis
):
    *w_next, a3, wbuf, sems = rest
    waits, late, starts = weight_copies(cw, k + 1, wbuf, w_next[0] if w_next else None, sems)
    mean, scale, bias = norm_terms(stats, gain, shift, k, total)

    def row_at(i):
        x = jnp.maximum((c_in[i] - mean) * scale + bias, 0.0)
        return masked(x, inside(lo + i, strip, axis))

    w_parts = [w_first, wbuf.at[0], wbuf.at[1]]
    write_stats(st, *run_conv(row_at, n_in, a3, w_parts, waits, c_ref, 0, lo + 1, strip, starts=starts))
    for c in late:
        c.wait()


def joined_conv_kernel(
    c_in, stats, gain, shift, w_first, feature, cw, c_ref, st, w_next, joined, a3, wbuf, sems,
    *, k, lo, n_in, strip, total, axis
):
    waits, late, starts = weight_copies(cw, k + 1, wbuf, w_next, sems)
    mean, scale, bias = norm_terms(stats, gain, shift, k, total)

    def row_at(i):
        y = (feature[i].astype(F32) + ((c_in[i] - mean) * scale + bias)).astype(BF)
        joined[i] = y
        return masked(relu_row(y), inside(lo + i, strip, axis))

    w_parts = [w_first, wbuf.at[0], wbuf.at[1]]
    write_stats(st, *run_conv(row_at, n_in, a3, w_parts, waits, c_ref, 0, lo + 1, strip, starts=starts))
    for c in late:
        c.wait()


def final_kernel(joined, c_in, stats, gain, shift, out, *, k, total):
    mean, scale, bias = norm_terms(stats, gain, shift, k, total)
    for i in range(out.shape[0]):
        out[i] = (joined[i + 2].astype(F32) + ((c_in[i] - mean) * scale + bias)).astype(BF)


def sent_to_all(value, axis):
    return lax.all_to_all(value, axis, 0, 0, tiled=True)


def reduce_all(partial):
    near = sent_to_all(partial, "row").sum(axis=0)
    far = lax.axis_size("img")
    return sent_to_all(jnp.broadcast_to(near[None], (far, *near.shape)), "img")


def on_device(tokens, proj_weight, proj_bias, conv_weight, bn_gain, bn_bias):
    imgs, strip, cols, embed = tokens.shape
    ch = proj_weight.shape[1]
    nrow = lax.axis_size("row")
    total = float(lax.axis_size("img") * nrow * imgs * strip * cols)
    weights = in_hbm(conv_weight)
    norm_args = (bn_gain, bn_bias)

    half = sds((HALO, cols, ch), BF)
    w_third = sds((3, ch, ch), BF)
    top, bot = pl.pallas_call(
        proj_kernel,
        out_shape=(half, half),
        in_specs=[HBM] * 3,
        out_specs=(VM, VM),
        scratch_shapes=[
            pltpu.VMEM((strip, cols, embed), BF),
            pltpu.VMEM((embed, ch), BF),
            pltpu.VMEM((1, ch), F32),
            pltpu.SemaphoreType.DMA((strip + 2,)),
        ],
        compiler_params=PARAMS,
    )(in_hbm(tokens[0]), in_hbm(proj_weight), in_hbm(proj_bias[None]))
    before = lax.ppermute(bot, "row", [(i, i + 1) for i in range(nrow - 1)])
    after = lax.ppermute(top, "row", [(i + 1, i) for i in range(nrow - 1)])
    top, bot, before, after = map(in_vmem, (top, bot, before, after))

    field = sds((strip + 2 * HALO - 2, cols, ch), F32)
    stat = sds((nrow, 1, 2 * ch), F32)
    context = sds((strip + 4, cols, ch), BF)

    def rows_scratch(rows):
        return pltpu.VMEM((rows, cols, 3 * ch), BF)

    c0, part, w0 = pl.pallas_call(
        functools.partial(conv0_inner_kernel, strip=strip),
        out_shape=(field, sds((2, 8, ch), F32), sds((3, 3, ch, ch), BF)),
        in_specs=[VM, VM, HBM],
        out_specs=(VM,) * 3,
        scratch_shapes=[rows_scratch(strip), pltpu.SemaphoreType.DMA((3,))],
        compiler_params=PARAMS,
        cost_estimate=pl.CostEstimate(
            flops=2 * 9 * ch * ch * cols * (strip - 2), transcendentals=0, bytes_accessed=9 * ch * ch * 2
        ),
    )(top, bot, weights)
    c, st, feature, w_next = pl.pallas_call(
        functools.partial(conv0_outer_kernel, strip=strip),
        out_shape=(field, stat, context, w_third),
        in_specs=[VM] * 7 + [HBM],
        out_specs=(VM,) * 4,
        input_output_aliases={6: 0},
        scratch_shapes=[rows_scratch(2 * HALO + 4), pltpu.SemaphoreType.DMA(())],
        compiler_params=PARAMS,
    )(before, top, bot, after, in_vmem(w0), in_vmem(part), in_vmem(c0), weights)

    def call(kernel, extra_in, extra_out, n_in, aliases, **kw):
        args = (in_vmem(c), in_vmem(st), *norm_args, *map(in_vmem, extra_in))
        return pl.pallas_call(
            functools.partial(kernel, n_in=n_in, strip=strip, total=total, axis="row", **kw),
            out_shape=(field, stat, *extra_out),
            in_specs=[VM] * len(args) + [HBM],
            out_specs=(VM,) * (2 + len(extra_out)),
            input_output_aliases={0: 0, **aliases},
            scratch_shapes=[
                rows_scratch(n_in),
                pltpu.VMEM((2, 3, ch, ch), BF),
                pltpu.SemaphoreType.DMA((3,)),
            ],
            compiler_params=PARAMS,
        )(*args, weights)

    st = reduce_all(st)
    c, st, w_next = call(hidden_conv_kernel, (w_next,), (w_third,), strip + 6, {}, k=0, lo=-3)
    st = reduce_all(st)
    c, st, w_next, joined = call(
        joined_conv_kernel, (w_next, feature), (w_third, context), strip + 4, {5: 3}, k=1, lo=-2
    )
    st = reduce_all(st)
    c, st = call(hidden_conv_kernel, (w_next,), (), strip + 2, {}, k=2, lo=-1)
    st = reduce_all(st)
    out = pl.pallas_call(
        functools.partial(final_kernel, k=3, total=total),
        out_shape=sds((strip, cols, ch), BF),
        in_specs=[VM] * 5,
        out_specs=VM,
        compiler_params=PARAMS,
    )(in_vmem(joined), in_vmem(c), in_vmem(st), *norm_args)
    return out[None]


def solution(mesh):
    placed = (P("img", "row", None, None), P(), P(), P(), P(), P())
    return jax.shard_map(
        on_device, mesh=mesh, in_specs=placed, out_specs=P("img", "row", None, None), check_vma=False
    )
```

time: 119 us -> 117 us (0.983)
  Pallas kernels: 16.9 us -> 15.4 us
    pallas_call x3, Pallas kernels: 9.17 us -> 7.78 us  [call(): pl.pallas_call(functools.partial(kernel, n_in=n_in, strip=strip, total=to...]
where the time goes in v2:
time: 117 us; the launch traced here: 116 us
  blocking collectives  91 us (78%)
  Pallas kernels  15.4 us (13%)
  starting transfers between devices  6.5 us (6%)
  waiting for transfers between devices  3.03 us (3%)
    all_to_all x8, blocking collectives, sent_to_all(): return lax.all_to_all(value, axis, 0, 0, tiled=True)  91 us
    pallas_call x3, Pallas kernels, call(): pl.pallas_call(functools.partial(kernel, n_in=n_in, strip=strip, total=to...  7.78 us
    ppermute x1, starting transfers between devices, on_device(): before = lax.ppermute(bot, 'row', [(i, i + 1) for i in range(nrow - 1)])  4.58 us
    ppermute x1, waiting for transfers between devices, on_device(): after = lax.ppermute(top, 'row', [(i + 1, i) for i in range(nrow - 1)])  3.02 us
    pallas_call x1, Pallas kernels, on_device(): pl.pallas_call(functools.partial(conv0_inner_kernel, strip=strip), out_sh...  2.72 us
    pallas_call x1, Pallas kernels, on_device(): pl.pallas_call(proj_kernel, out_shape=(half, half), in_specs=[HBM] * 3, o...  2.47 us
  transfers between devices with their start and end apart: 2, of which 1 were waited for; matrix products, arithmetic and copies ran while one was open for 0% of the time, Pallas kernels for 2%

profile of v2, /device:TPU:1, one launch (start us, length us, event | category | flops | bytes accessed | tf_op | source)
XLA Modules:
  0.0 116.4 jit_solution(7247997476893558488)
XLA Ops:
  0.0 2.5 %shard_map.64 = (bf16[4,128,256]{2,1,0:T(8,128)(2,1)S(1)}, bf16[4,128,256]{2,1,0:T(8,128)(2,1)S(1)}) custom-call(bf16[8,128,1024]{2,1,0:T(8,128)(2,1)} %bitcast.3, bf16[1024,256]{1,0:T(8,128)(2,1)} %w.1, f32[1,256]{1,0:T(1,128)} %bitcast.4), custom_call_target="tpu_custom_call" | custom-call | tf_op jit(solution)/shard_map/pallas_call | solution.py:249
  2.5 4.6 %collective-permute-start = (bf16[4,128,256]{2,1,0:T(8,128)(2,1)S(1)}, bf16[4,128,256]{2,1,0:T(8,128)(2,1)S(1)}, u32[]{:S(2)}, u32[]{:S(2)}) collective-permute-start(bf16[4,128,256]{2,1,0:T(8,128)(2,1)S(1)} %get-tuple-element.23.bot), channel_id=1, source_target_pairs={{0,1},{1,2},{2,3},{3,4},{4,5},{5,6},{6,7},{8,9},{9,10},{10,11},{11... | collective-permute-start | bytes 786440 | tf_op jit(solution)/shard_map/ppermute | solution.py:262
  7.1 1.9 %collective-permute-start.1 = (bf16[4,128,256]{2,1,0:T(8,128)(2,1)S(1)}, bf16[4,128,256]{2,1,0:T(8,128)(2,1)S(1)}, u32[]{:S(2)}, u32[]{:S(2)}) collective-permute-start(bf16[4,128,256]{2,1,0:T(8,128)(2,1)S(1)} %get-tuple-element.24.top), channel_id=1, source_target_pairs={{1,0},{2,1},{3,2},{4,3},{5,4},{6,5},{7,6},{9,8},{10,9},{11,10},{12... | collective-permute-start | bytes 786440 | tf_op jit(solution)/shard_map/ppermute | solution.py:263
  9.0 2.7 %shard_map.65 = (f32[14,128,256]{2,1,0:T(8,128)S(1)}, f32[2,8,256]{2,1,0:T(8,128)S(1)}, bf16[3,3,256,256]{3,2,1,0:T(8,128)(2,1)S(1)}) custom-call(bf16[4,128,256]{2,1,0:T(8,128)(2,1)S(1)} %get-tuple-element.24.top, bf16[4,128,256]{2,1,0:T(8,128)(2,1)S(1)} %get-tuple-element.23.bot, bf16[4,3,3,256,256]{4,3,2,1,0:T(8,128)(2,1)} %cw.9), custom_call_target="tpu_custom_call" | custom-call | flops 905969664 | bytes 1179648 | tf_op jit(solution)/shard_map/pallas_call | solution.py:273
  11.7 0.0 collective-permute-done.before
  11.7 3.0 %collective-permute-done.1.after = bf16[4,128,256]{2,1,0:T(8,128)(2,1)S(1)} collective-permute-done((bf16[4,128,256]{2,1,0:T(8,128)(2,1)S(1)}, bf16[4,128,256]{2,1,0:T(8,128)(2,1)S(1)}, u32[]{:S(2)}, u32[]{:S(2)}) %collective-permute-start.1) | collective-permute-done | bytes 262176 | tf_op jit(solution)/shard_map/ppermute | solution.py:263
  14.8 0.0 copy-start
  14.8 0.0 copy-start.1
  14.8 1.4 %shard_map.66 = (f32[14,128,256]{2,1,0:T(8,128)S(1)}, f32[8,1,512]{2,1,0:T(1,128)S(1)}, bf16[12,128,256]{2,1,0:T(8,128)(2,1)S(1)}, bf16[3,256,256]{2,1,0:T(8,128)(2,1)S(1)}) custom-call(bf16[4,128,256]{2,1,0:T(8,128)(2,1)S(1)} %collective-permute-done.before, bf16[4,128,256]{2,1,0:T(8,128)(2,1)S(1)} %get-tuple-element.24.top, ...), custom_call_target="tpu_custom_call", output_to_operand_aliasing={{0}: (6, {})} | custom-call | tf_op jit(solution)/shard_map/pallas_call | solution.py:284
  16.2 8.7 %all_to_all.40 = f32[8,1,512]{2,1,0:T(1,128)S(1)} all-to-all(f32[8,1,512]{2,1,0:T(1,128)S(1)} %get-tuple-element.29), channel_id=1, replica_groups=mesh['img'=32,'row'=8] {'row'}, dimensions={0} | all-to-all | bytes 32768 | tf_op jit(solution)/shard_map/all_to_all | solution.py:230
  25.0 19.7 %all_to_all.41.stats = f32[32,1,512]{2,1,0:T(1,128)S(1)} all-to-all(f32[32,1,512]{2,1,0:T(1,128)S(1)} %broadcast_in_dim.13), channel_id=1, replica_groups=mesh['img'=32,'row'=8] {'img'}, dimensions={0} | all-to-all | bytes 131072 | tf_op jit(solution)/shard_map/all_to_all | solution.py:230
  44.6 0.0 copy-done
  44.6 0.0 copy-done.1
  44.6 2.5 %shard_map.67 = (f32[14,128,256]{2,1,0:T(8,128)S(1)}, f32[8,1,512]{2,1,0:T(1,128)S(1)}, bf16[3,256,256]{2,1,0:T(8,128)(2,1)S(1)}) custom-call(f32[14,128,256]{2,1,0:T(8,128)S(1)} %get-tuple-element.28.c_in, f32[32,1,512]{2,1,0:T(1,128)S(1)} %all_to_all.41.stats, f32[4,256]{1,0:T(4,128)S(1)} %copy-done, ...), custom_call_target="tpu_custom_call", output_to_operand_aliasing={{0}: (0, {})} | custom-call | tf_op jit(solution)/shard_map/pallas_call | solution.py:296
  47.1 9.1 %all_to_all.42 = f32[8,1,512]{2,1,0:T(1,128)S(1)} all-to-all(f32[8,1,512]{2,1,0:T(1,128)S(1)} %get-tuple-element.32), channel_id=1, replica_groups=mesh['img'=32,'row'=8] {'row'}, dimensions={0} | all-to-all | bytes 32768 | tf_op jit(solution)/shard_map/all_to_all | solution.py:230
  56.4 11.9 %all_to_all.43.stats = f32[32,1,512]{2,1,0:T(1,128)S(1)} all-to-all(f32[32,1,512]{2,1,0:T(1,128)S(1)} %broadcast_in_dim.14), channel_id=1, replica_groups=mesh['img'=32,'row'=8] {'img'}, dimensions={0} | all-to-all | bytes 131072 | tf_op jit(solution)/shard_map/all_to_all | solution.py:230
  68.3 3.2 %shard_map.68 = (f32[14,128,256]{2,1,0:T(8,128)S(1)}, f32[8,1,512]{2,1,0:T(1,128)S(1)}, bf16[3,256,256]{2,1,0:T(8,128)(2,1)S(1)}, bf16[12,128,256]{2,1,0:T(8,128)(2,1)S(1)}) custom-call(f32[14,128,256]{2,1,0:T(8,128)S(1)} %get-tuple-element.31.c_in, f32[32,1,512]{2,1,0:T(1,128)S(1)} %all_to_all.43.stats, ...), custom_call_target="tpu_custom_call", output_to_operand_aliasing={{0}: (0, {}), {3}: (5, {})} | custom-call | tf_op jit(solution)/shard_map/pallas_call | solution.py:296
  71.5 8.9 %all_to_all.44 = f32[8,1,512]{2,1,0:T(1,128)S(1)} all-to-all(f32[8,1,512]{2,1,0:T(1,128)S(1)} %get-tuple-element.37), channel_id=1, replica_groups=mesh['img'=32,'row'=8] {'row'}, dimensions={0} | all-to-all | bytes 32768 | tf_op jit(solution)/shard_map/all_to_all | solution.py:230
  80.4 11.9 %all_to_all.45.stats = f32[32,1,512]{2,1,0:T(1,128)S(1)} all-to-all(f32[32,1,512]{2,1,0:T(1,128)S(1)} %broadcast_in_dim.15), channel_id=1, replica_groups=mesh['img'=32,'row'=8] {'img'}, dimensions={0} | all-to-all | bytes 131072 | tf_op jit(solution)/shard_map/all_to_all | solution.py:230
  92.4 2.1 %shard_map.69 = (f32[14,128,256]{2,1,0:T(8,128)S(1)}, f32[8,1,512]{2,1,0:T(1,128)S(1)}) custom-call(f32[14,128,256]{2,1,0:T(8,128)S(1)} %get-tuple-element.36.c_in, f32[32,1,512]{2,1,0:T(1,128)S(1)} %all_to_all.45.stats, f32[4,256]{1,0:T(4,128)S(1)} %copy-done, f32[4,256]{1,0:T(4,128)S(1)} %copy-done.1, ...), custom_call_target="tpu_custom_call", output_to_operand_aliasing={{0}: (0, {})} | custom-call | tf_op jit(solution)/shard_map/pallas_call | solution.py:296
  94.5 8.9 %all_to_all.46 = f32[8,1,512]{2,1,0:T(1,128)S(1)} all-to-all(f32[8,1,512]{2,1,0:T(1,128)S(1)} %get-tuple-element.40), channel_id=1, replica_groups=mesh['img'=32,'row'=8] {'row'}, dimensions={0} | all-to-all | bytes 32768 | tf_op jit(solution)/shard_map/all_to_all | solution.py:230
  103.4 11.9 %all_to_all.47.stats = f32[32,1,512]{2,1,0:T(1,128)S(1)} all-to-all(f32[32,1,512]{2,1,0:T(1,128)S(1)} %broadcast_in_dim.16), channel_id=1, replica_groups=mesh['img'=32,'row'=8] {'img'}, dimensions={0} | all-to-all | bytes 131072 | tf_op jit(solution)/shard_map/all_to_all | solution.py:230
  115.3 1.0 shard_map.70
  (8 shorter events, 0.3 us)
Async XLA Ops:
  2.5 9.2 %collective-permute-start = (bf16[4,128,256]{2,1,0:T(8,128)(2,1)S(1)}, bf16[4,128,256]{2,1,0:T(8,128)(2,1)S(1)}, u32[]{:S(2)}, u32[]{:S(2)}) collective-permute-start(bf16[4,128,256]{2,1,0:T(8,128)(2,1)S(1)} %get-tuple-element.23.bot), channel_id=1, source_target_pairs={{0,1},{1,2},{2,3},{3,4},{4,5},{5,6},{6,7},{8,9},{9,10},{10,11},{11... | collective-permute-start | bytes 786440 | tf_op jit(solution)/shard_map/ppermute | solution.py:262
  7.1 7.7 %collective-permute-start.1 = (bf16[4,128,256]{2,1,0:T(8,128)(2,1)S(1)}, bf16[4,128,256]{2,1,0:T(8,128)(2,1)S(1)}, u32[]{:S(2)}, u32[]{:S(2)}) collective-permute-start(bf16[4,128,256]{2,1,0:T(8,128)(2,1)S(1)} %get-tuple-element.24.top), channel_id=1, source_target_pairs={{1,0},{2,1},{3,2},{4,3},{5,4},{6,5},{7,6},{9,8},{10,9},{11,10},{12... | collective-permute-start | bytes 786440 | tf_op jit(solution)/shard_map/ppermute | solution.py:263
  14.8 29.9 %copy-start = (f32[4,256]{1,0:T(4,128)S(1)}, f32[4,256]{1,0:T(4,128)}, u32[]{:S(2)}) copy-start(f32[4,256]{1,0:T(4,128)} %gain.7) | copy-start | bytes 12292
  14.8 29.9 %copy-start.1 = (f32[4,256]{1,0:T(4,128)S(1)}, f32[4,256]{1,0:T(4,128)}, u32[]{:S(2)}) copy-start(f32[4,256]{1,0:T(4,128)} %shift.7) | copy-start | bytes 12292

commit v3 on v2

--- a/solution.py
+++ b/solution.py
@@ -10,9 +10,6 @@
 EPS = 1e-05
 HALO = 4
 STEP = 2
-PROWS = 8
-TROWS = 1
-DELAY = 0
 LATE = 0
 AHEAD = 0
 VM = pl.BlockSpec(memory_space=pltpu.VMEM)
@@ -104,70 +101,84 @@
     return sums, squares
 
 
-def proj_kernel(tok, w, bias, top, bot, tbuf, wbuf, bbuf, sems):
+def near_is_top(axis):
+    return lax.axis_index(axis) % 2 == 1
+
+
+def proj_kernel(tok, w, bias, far, near, tbuf, wbuf, bbuf, sems, *, axis):
     rows = tok.shape[0]
-    first = [pltpu.make_async_copy(w, wbuf, sems.at[rows]), pltpu.make_async_copy(bias, bbuf, sems.at[rows + 1])]
+    near_at = jnp.where(near_is_top(axis), 0, HALO)
     copies = [
-        pltpu.make_async_copy(tok.at[i : i + TROWS], tbuf.at[i : i + TROWS], sems.at[i]) for i in range(0, rows, TROWS)
+        pltpu.make_async_copy(w, wbuf, sems.at[0]),
+        pltpu.make_async_copy(bias, bbuf, sems.at[1]),
+        pltpu.make_async_copy(tok.at[pl.ds(HALO - near_at, HALO)], tbuf.at[0:HALO], sems.at[2]),
+        pltpu.make_async_copy(tok.at[pl.ds(near_at, HALO)], tbuf.at[HALO:], sems.at[3]),
     ]
-    for c in first:
+    for c in copies:
         c.start()
-    for i, c in enumerate(copies):
-        if DELAY and i * TROWS == rows // 2:
-            pl.delay(DELAY)
-        c.start()
-    for c in first:
+    for c in copies:
         c.wait()
-    half = rows // 2
-    for i in range(0, rows, PROWS):
-        for c in copies[i // TROWS : (i + PROWS + TROWS - 1) // TROWS]:
-            c.wait()
-        x = tbuf[i : i + PROWS].reshape(-1, tok.shape[2])
-        y = jnp.dot(x, wbuf[...], preferred_element_type=F32) + bbuf[...]
-        y = y.astype(BF).reshape(PROWS, tok.shape[1], -1)
-        for j in range(PROWS):
-            (top if i + j < half else bot)[(i + j) % half] = y[j]
+    y = jnp.dot(tbuf[...].reshape(-1, tok.shape[2]), wbuf[...], preferred_element_type=F32) + bbuf[...]
+    y = y.astype(BF).reshape(rows, tok.shape[1], -1)
+    far[...] = y[:HALO]
+    near[...] = y[HALO:]
 
 
 def relu_row(x):
     return jnp.maximum(x.astype(F32), 0.0)
 
 
-def conv0_inner_kernel(top, bot, cw, c_ref, part, w0, a3, sems, *, strip):
+def pick(cond, a, b):
+    return jnp.where(cond, a.astype(F32), b.astype(F32))
+
+
+def conv0_inner_kernel(far, near, cw, c_ref, part, w0, a3, sems, *, strip, axis):
     waits = [[pltpu.make_async_copy(cw.at[0, dy], w0.at[dy], sems.at[dy])] for dy in range(3)]
     for (copy,) in waits:
         copy.start()
+    flip = near_is_top(axis)
 
     def row_at(i):
-        return relu_row(top[i] if i < HALO else bot[i - HALO])
+        j = i % HALO
+        return relu_row(pick(flip, near[j], far[j]) if i < HALO else pick(flip, far[j], near[j]))
 
     w_parts = [w0.at[dy] for dy in range(3)]
     part[0], part[1] = run_conv(row_at, strip, a3, w_parts, waits, c_ref, HALO, 1, strip)
 
 
-def conv0_outer_kernel(before, top, bot, after, w0, part, c_in, cw, c_ref, st, feature, w_next, a3, sem, *, strip):
+def conv0_outer_kernel(
+    got_far, far, near, got_near, w0, part, c_in, cw, c_ref, st, feature, w_next, a3, sem, *, strip, axis
+):
     late = pltpu.make_async_copy(cw.at[1, 0], w_next, sem)
     late.start()
     w_parts = [w0.at[dy] for dy in range(3)]
+    flip = near_is_top(axis)
+
+    def strip_row(i):
+        j = i % HALO
+        if i < 0:
+            return pick(flip, got_near[j], got_far[j])
+        if i < HALO:
+            return pick(flip, near[j], far[j])
+        if i < strip:
+            return pick(flip, far[j], near[j])
+        return pick(flip, got_far[j], got_near[j])
 
     def upper(i):
-        return relu_row(before[i] if i < HALO else top[i - HALO])
+        return relu_row(strip_row(i - HALO))
+
+    def lower(i):
+        return relu_row(strip_row(strip - 2 + i))
 
     sums, squares = run_conv(
         upper, HALO + 2, a3.at[: HALO + 2], w_parts, [[]] * 3, c_ref, 0, 1 - HALO, strip, part[0], part[1]
     )
-
-    def lower(i):
-        return relu_row(bot[i + HALO - 2] if i < 2 else after[i - 2])
-
     sums, squares = run_conv(
         lower, HALO + 2, a3.at[HALO + 2 :], w_parts, [[]] * 3, c_ref, strip + HALO - 2, strip - 1, strip, sums, squares
     )
     write_stats(st, sums, squares)
-    feature[0:2] = before[HALO - 2 :]
-    feature[2 : HALO + 2] = top[...]
-    feature[HALO + 2 : strip + 2] = bot[...]
-    feature[strip + 2 :] = after[0:2]
+    for i in range(feature.shape[0]):
+        feature[i] = strip_row(i - 2).astype(BF)
     late.wait()
 
 
@@ -236,6 +247,11 @@
     return sent_to_all(jnp.broadcast_to(near[None], (far, *near.shape)), "img")
 
 
+def swapped(value, firsts):
+    pairs = [(i, i + 1) for i in firsts]
+    return lax.ppermute(value, "row", pairs + [(j, i) for i, j in pairs])
+
+
 def on_device(tokens, proj_weight, proj_bias, conv_weight, bn_gain, bn_bias):
     imgs, strip, cols, embed = tokens.shape
     ch = proj_weight.shape[1]
@@ -246,8 +262,8 @@
 
     half = sds((HALO, cols, ch), BF)
     w_third = sds((3, ch, ch), BF)
-    top, bot = pl.pallas_call(
-        proj_kernel,
+    far, near = pl.pallas_call(
+        functools.partial(proj_kernel, axis="row"),
         out_shape=(half, half),
         in_specs=[HBM] * 3,
         out_specs=(VM, VM),
@@ -255,13 +271,13 @@
             pltpu.VMEM((strip, cols, embed), BF),
             pltpu.VMEM((embed, ch), BF),
             pltpu.VMEM((1, ch), F32),
-            pltpu.SemaphoreType.DMA((strip + 2,)),
+            pltpu.SemaphoreType.DMA((4,)),
         ],
         compiler_params=PARAMS,
     )(in_hbm(tokens[0]), in_hbm(proj_weight), in_hbm(proj_bias[None]))
-    before = lax.ppermute(bot, "row", [(i, i + 1) for i in range(nrow - 1)])
-    after = lax.ppermute(top, "row", [(i + 1, i) for i in range(nrow - 1)])
-    top, bot, before, after = map(in_vmem, (top, bot, before, after))
+    got_far = swapped(far, range(1, nrow - 1, 2))
+    got_near = swapped(near, range(0, nrow - 1, 2))
+    far, near, got_far, got_near = map(in_vmem, (far, near, got_far, got_near))
 
     field = sds((strip + 2 * HALO - 2, cols, ch), F32)
     stat = sds((nrow, 1, 2 * ch), F32)
@@ -271,7 +287,7 @@
         return pltpu.VMEM((rows, cols, 3 * ch), BF)
 
     c0, part, w0 = pl.pallas_call(
-        functools.partial(conv0_inner_kernel, strip=strip),
+        functools.partial(conv0_inner_kernel, strip=strip, axis="row"),
         out_shape=(field, sds((2, 8, ch), F32), sds((3, 3, ch, ch), BF)),
         in_specs=[VM, VM, HBM],
         out_specs=(VM,) * 3,
@@ -280,16 +296,16 @@
         cost_estimate=pl.CostEstimate(
             flops=2 * 9 * ch * ch * cols * (strip - 2), transcendentals=0, bytes_accessed=9 * ch * ch * 2
         ),
-    )(top, bot, weights)
+    )(far, near, weights)
     c, st, feature, w_next = pl.pallas_call(
-        functools.partial(conv0_outer_kernel, strip=strip),
+        functools.partial(conv0_outer_kernel, strip=strip, axis="row"),
         out_shape=(field, stat, context, w_third),
         in_specs=[VM] * 7 + [HBM],
         out_specs=(VM,) * 4,
         input_output_aliases={6: 0},
         scratch_shapes=[rows_scratch(2 * HALO + 4), pltpu.SemaphoreType.DMA(())],
         compiler_params=PARAMS,
-    )(before, top, bot, after, in_vmem(w0), in_vmem(part), in_vmem(c0), weights)
+    )(got_far, far, near, got_near, in_vmem(w0), in_vmem(part), in_vmem(c0), weights)
 
     def call(kernel, extra_in, extra_out, n_in, aliases, **kw):
         args = (in_vmem(c), in_vmem(st), *norm_args, *map(in_vmem, extra_in))

time: 117 us -> 114 us (0.974)
  starting transfers between devices: 6.5 us -> 4.68 us
  waiting for transfers between devices: 3.03 us -> 1.21 us
    ppermute x2, starting transfers between devices: 6.5 us -> 4.68 us  [swapped(): return lax.ppermute(value, 'row', pairs + [(j, i) for i, j in pairs])]
    ppermute x2, waiting for transfers between devices: 3.03 us -> 1.21 us  [swapped(): return lax.ppermute(value, 'row', pairs + [(j, i) for i, j in pairs])]
where the time goes in v3:
time: 114 us
  blocking collectives  91.8 us (81%)
  Pallas kernels  15.6 us (14%)
  starting transfers between devices  4.68 us (4%)
  waiting for transfers between devices  1.21 us (1%)
    all_to_all x8, blocking collectives, sent_to_all(): return lax.all_to_all(value, axis, 0, 0, tiled=True)  91.8 us
    pallas_call x3, Pallas kernels, call(): pl.pallas_call(functools.partial(kernel, n_in=n_in, strip=strip, total=to...  7.78 us
    ppermute x2, starting transfers between devices, swapped(): return lax.ppermute(value, 'row', pairs + [(j, i) for i, j in pairs])  4.68 us
    pallas_call x1, Pallas kernels, on_device(): pl.pallas_call(functools.partial(conv0_inner_kernel, strip=strip, axis='r...  2.72 us
    pallas_call x1, Pallas kernels, on_device(): pl.pallas_call(functools.partial(proj_kernel, axis='row'), out_shape=(hal...  2.46 us
  transfers between devices with their start and end apart: 2, of which 1 were waited for; matrix products, arithmetic and copies ran while one was open for 0% of the time, Pallas kernels for 2%

profile of v3, /device:TPU:1, one launch (start us, length us, event | category | flops | bytes accessed | tf_op | source)
XLA Modules:
  0.0 113.6 jit_solution(3456598455891702665)
XLA Ops:
  0.0 2.5 %shard_map.64 = (bf16[4,128,256]{2,1,0:T(8,128)(2,1)S(1)}, bf16[4,128,256]{2,1,0:T(8,128)(2,1)S(1)}) custom-call(bf16[8,128,1024]{2,1,0:T(8,128)(2,1)} %bitcast.3, bf16[1024,256]{1,0:T(8,128)(2,1)} %w.1, f32[1,256]{1,0:T(1,128)} %bitcast.4), custom_call_target="tpu_custom_call" | custom-call | tf_op jit(solution)/shard_map/pallas_call | solution.py:265
  2.5 4.6 %collective-permute-start = (bf16[4,128,256]{2,1,0:T(8,128)(2,1)S(1)}, bf16[4,128,256]{2,1,0:T(8,128)(2,1)S(1)}, u32[]{:S(2)}, u32[]{:S(2)}) collective-permute-start(bf16[4,128,256]{2,1,0:T(8,128)(2,1)S(1)} %get-tuple-element.23.far), channel_id=1, source_target_pairs={{1,2},{3,4},{5,6},{2,1},{4,3},{6,5},{9,10},{11,12},{13,14},{10,9},... | collective-permute-start | bytes 786440 | tf_op jit(solution)/shard_map/ppermute | solution.py:252
  7.1 0.1 collective-permute-start.1
  7.2 2.7 %shard_map.65 = (f32[14,128,256]{2,1,0:T(8,128)S(1)}, f32[2,8,256]{2,1,0:T(8,128)S(1)}, bf16[3,3,256,256]{3,2,1,0:T(8,128)(2,1)S(1)}) custom-call(bf16[4,128,256]{2,1,0:T(8,128)(2,1)S(1)} %get-tuple-element.23.far, bf16[4,128,256]{2,1,0:T(8,128)(2,1)S(1)} %get-tuple-element.24.near, bf16[4,3,3,256,256]{4,3,2,1,0:T(8,128)(2,1)} %cw.9), custom_call_target="tpu_custom_call" | custom-call | flops 905969664 | bytes 1179648 | tf_op jit(solution)/shard_map/pallas_call | solution.py:289
  9.9 1.2 %collective-permute-done.got_far = bf16[4,128,256]{2,1,0:T(8,128)(2,1)S(1)} collective-permute-done((bf16[4,128,256]{2,1,0:T(8,128)(2,1)S(1)}, bf16[4,128,256]{2,1,0:T(8,128)(2,1)S(1)}, u32[]{:S(2)}, u32[]{:S(2)}) %collective-permute-start) | collective-permute-done | bytes 262176 | tf_op jit(solution)/shard_map/ppermute | solution.py:252
  11.1 0.0 collective-permute-done.1.got_near
  11.1 0.0 copy-start
  11.1 0.0 copy-start.1
  11.1 1.6 %shard_map.66 = (f32[14,128,256]{2,1,0:T(8,128)S(1)}, f32[8,1,512]{2,1,0:T(1,128)S(1)}, bf16[12,128,256]{2,1,0:T(8,128)(2,1)S(1)}, bf16[3,256,256]{2,1,0:T(8,128)(2,1)S(1)}) custom-call(bf16[4,128,256]{2,1,0:T(8,128)(2,1)S(1)} %collective-permute-done.got_far, bf16[4,128,256]{2,1,0:T(8,128)(2,1)S(1)} %get-tuple-element.23.far, ...), custom_call_target="tpu_custom_call", output_to_operand_aliasing={{0}: (6, {})} | custom-call | tf_op jit(solution)/shard_map/pallas_call | solution.py:300
  12.7 9.5 %all_to_all.40 = f32[8,1,512]{2,1,0:T(1,128)S(1)} all-to-all(f32[8,1,512]{2,1,0:T(1,128)S(1)} %get-tuple-element.29), channel_id=1, replica_groups=mesh['img'=32,'row'=8] {'row'}, dimensions={0} | all-to-all | bytes 32768 | tf_op jit(solution)/shard_map/all_to_all | solution.py:241
  22.2 19.7 %all_to_all.41.stats = f32[32,1,512]{2,1,0:T(1,128)S(1)} all-to-all(f32[32,1,512]{2,1,0:T(1,128)S(1)} %broadcast_in_dim.13), channel_id=1, replica_groups=mesh['img'=32,'row'=8] {'img'}, dimensions={0} | all-to-all | bytes 131072 | tf_op jit(solution)/shard_map/all_to_all | solution.py:241
  41.9 0.0 copy-done
  41.9 0.0 copy-done.1
  41.9 2.5 %shard_map.67 = (f32[14,128,256]{2,1,0:T(8,128)S(1)}, f32[8,1,512]{2,1,0:T(1,128)S(1)}, bf16[3,256,256]{2,1,0:T(8,128)(2,1)S(1)}) custom-call(f32[14,128,256]{2,1,0:T(8,128)S(1)} %get-tuple-element.28.c_in, f32[32,1,512]{2,1,0:T(1,128)S(1)} %all_to_all.41.stats, f32[4,256]{1,0:T(4,128)S(1)} %copy-done, ...), custom_call_target="tpu_custom_call", output_to_operand_aliasing={{0}: (0, {})} | custom-call | tf_op jit(solution)/shard_map/pallas_call | solution.py:312
  44.4 9.1 %all_to_all.42 = f32[8,1,512]{2,1,0:T(1,128)S(1)} all-to-all(f32[8,1,512]{2,1,0:T(1,128)S(1)} %get-tuple-element.32), channel_id=1, replica_groups=mesh['img'=32,'row'=8] {'row'}, dimensions={0} | all-to-all | bytes 32768 | tf_op jit(solution)/shard_map/all_to_all | solution.py:241
  53.6 11.9 %all_to_all.43.stats = f32[32,1,512]{2,1,0:T(1,128)S(1)} all-to-all(f32[32,1,512]{2,1,0:T(1,128)S(1)} %broadcast_in_dim.14), channel_id=1, replica_groups=mesh['img'=32,'row'=8] {'img'}, dimensions={0} | all-to-all | bytes 131072 | tf_op jit(solution)/shard_map/all_to_all | solution.py:241
  65.5 3.2 %shard_map.68 = (f32[14,128,256]{2,1,0:T(8,128)S(1)}, f32[8,1,512]{2,1,0:T(1,128)S(1)}, bf16[3,256,256]{2,1,0:T(8,128)(2,1)S(1)}, bf16[12,128,256]{2,1,0:T(8,128)(2,1)S(1)}) custom-call(f32[14,128,256]{2,1,0:T(8,128)S(1)} %get-tuple-element.31.c_in, f32[32,1,512]{2,1,0:T(1,128)S(1)} %all_to_all.43.stats, ...), custom_call_target="tpu_custom_call", output_to_operand_aliasing={{0}: (0, {}), {3}: (5, {})} | custom-call | tf_op jit(solution)/shard_map/pallas_call | solution.py:312
  68.7 8.9 %all_to_all.44 = f32[8,1,512]{2,1,0:T(1,128)S(1)} all-to-all(f32[8,1,512]{2,1,0:T(1,128)S(1)} %get-tuple-element.37), channel_id=1, replica_groups=mesh['img'=32,'row'=8] {'row'}, dimensions={0} | all-to-all | bytes 32768 | tf_op jit(solution)/shard_map/all_to_all | solution.py:241
  77.7 11.9 %all_to_all.45.stats = f32[32,1,512]{2,1,0:T(1,128)S(1)} all-to-all(f32[32,1,512]{2,1,0:T(1,128)S(1)} %broadcast_in_dim.15), channel_id=1, replica_groups=mesh['img'=32,'row'=8] {'img'}, dimensions={0} | all-to-all | bytes 131072 | tf_op jit(solution)/shard_map/all_to_all | solution.py:241
  89.6 2.1 %shard_map.69 = (f32[14,128,256]{2,1,0:T(8,128)S(1)}, f32[8,1,512]{2,1,0:T(1,128)S(1)}) custom-call(f32[14,128,256]{2,1,0:T(8,128)S(1)} %get-tuple-element.36.c_in, f32[32,1,512]{2,1,0:T(1,128)S(1)} %all_to_all.45.stats, f32[4,256]{1,0:T(4,128)S(1)} %copy-done, f32[4,256]{1,0:T(4,128)S(1)} %copy-done.1, ...), custom_call_target="tpu_custom_call", output_to_operand_aliasing={{0}: (0, {})} | custom-call | tf_op jit(solution)/shard_map/pallas_call | solution.py:312
  91.7 8.9 %all_to_all.46 = f32[8,1,512]{2,1,0:T(1,128)S(1)} all-to-all(f32[8,1,512]{2,1,0:T(1,128)S(1)} %get-tuple-element.40), channel_id=1, replica_groups=mesh['img'=32,'row'=8] {'row'}, dimensions={0} | all-to-all | bytes 32768 | tf_op jit(solution)/shard_map/all_to_all | solution.py:241
  100.6 11.9 %all_to_all.47.stats = f32[32,1,512]{2,1,0:T(1,128)S(1)} all-to-all(f32[32,1,512]{2,1,0:T(1,128)S(1)} %broadcast_in_dim.16), channel_id=1, replica_groups=mesh['img'=32,'row'=8] {'img'}, dimensions={0} | all-to-all | bytes 131072 | tf_op jit(solution)/shard_map/all_to_all | solution.py:241
  112.6 1.0 shard_map.70
  (8 shorter events, 0.3 us)
Async XLA Ops:
  2.5 8.6 %collective-permute-start = (bf16[4,128,256]{2,1,0:T(8,128)(2,1)S(1)}, bf16[4,128,256]{2,1,0:T(8,128)(2,1)S(1)}, u32[]{:S(2)}, u32[]{:S(2)}) collective-permute-start(bf16[4,128,256]{2,1,0:T(8,128)(2,1)S(1)} %get-tuple-element.23.far), channel_id=1, source_target_pairs={{1,2},{3,4},{5,6},{2,1},{4,3},{6,5},{9,10},{11,12},{13,14},{10,9},... | collective-permute-start | bytes 786440 | tf_op jit(solution)/shard_map/ppermute | solution.py:252
  7.1 4.0 %collective-permute-start.1 = (bf16[4,128,256]{2,1,0:T(8,128)(2,1)S(1)}, bf16[4,128,256]{2,1,0:T(8,128)(2,1)S(1)}, u32[]{:S(2)}, u32[]{:S(2)}) collective-permute-start(bf16[4,128,256]{2,1,0:T(8,128)(2,1)S(1)} %get-tuple-element.24.near), channel_id=1, source_target_pairs={{0,1},{2,3},{4,5},{6,7},{1,0},{3,2},{5,4},{7,6},{8,9},{10,11},{12,... | collective-permute-start | bytes 786440 | tf_op jit(solution)/shard_map/ppermute | solution.py:252
  11.1 30.8 %copy-start = (f32[4,256]{1,0:T(4,128)S(1)}, f32[4,256]{1,0:T(4,128)}, u32[]{:S(2)}) copy-start(f32[4,256]{1,0:T(4,128)} %gain.7) | copy-start | bytes 12292
  11.1 30.8 %copy-start.1 = (f32[4,256]{1,0:T(4,128)S(1)}, f32[4,256]{1,0:T(4,128)}, u32[]{:S(2)}) copy-start(f32[4,256]{1,0:T(4,128)} %shift.7) | copy-start | bytes 12292

commit v4 on v3

--- a/solution.py
+++ b/solution.py
@@ -9,9 +9,7 @@
 
 EPS = 1e-05
 HALO = 4
-STEP = 2
-LATE = 0
-AHEAD = 0
+SHAPES = {'inner': (3, 0), 'outer': (2, 0), 0: (2, 0), 1: (5, 0), 2: (2, 0)}
 VM = pl.BlockSpec(memory_space=pltpu.VMEM)
 HBM = pl.BlockSpec(memory_space=pltpu.HBM)
 BF = jnp.bfloat16
@@ -70,19 +68,18 @@
     return x if m is None else x * m
 
 
-def run_conv(row_at, n_in, a3, w_parts, waits, c_ref, at, lo, strip, sums=None, squares=None, starts=((), ())):
+def run_conv(row_at, n_in, a3, w_parts, waits, c_ref, at, lo, strip, sums=None, squares=None, tile=(2, 0)):
     cols, ch = c_ref.shape[1:]
     n_out = n_in - 2
+    step, ahead = tile
     filled = 0
     for dy in range(3):
         for copy in waits[dy]:
             copy.wait()
-        for copy in starts[dy - 1] if dy else ():
-            copy.start()
         w = w_parts[dy][...].reshape(3 * ch, ch)
-        for done in range(0, n_out, STEP):
-            rows = min(STEP, n_out - done)
-            while filled < min(n_in, done + rows + dy + AHEAD):
+        for done in range(0, n_out, step):
+            rows = min(step, n_out - done)
+            while filled < min(n_in, done + rows + dy + ahead):
                 put_row(a3, filled, row_at(filled))
                 filled += 1
             lhs = a3[done + dy : done + dy + rows].reshape(rows * cols, 3 * ch)
@@ -143,7 +140,7 @@
         return relu_row(pick(flip, near[j], far[j]) if i < HALO else pick(flip, far[j], near[j]))
 
     w_parts = [w0.at[dy] for dy in range(3)]
-    part[0], part[1] = run_conv(row_at, strip, a3, w_parts, waits, c_ref, HALO, 1, strip)
+    part[0], part[1] = run_conv(row_at, strip, a3, w_parts, waits, c_ref, HALO, 1, strip, tile=SHAPES['inner'])
 
 
 def conv0_outer_kernel(
@@ -171,10 +168,12 @@
         return relu_row(strip_row(strip - 2 + i))
 
     sums, squares = run_conv(
-        upper, HALO + 2, a3.at[: HALO + 2], w_parts, [[]] * 3, c_ref, 0, 1 - HALO, strip, part[0], part[1]
+        upper, HALO + 2, a3.at[: HALO + 2], w_parts, [[]] * 3, c_ref, 0, 1 - HALO, strip, part[0], part[1],
+        tile=SHAPES['outer'],
     )
     sums, squares = run_conv(
-        lower, HALO + 2, a3.at[HALO + 2 :], w_parts, [[]] * 3, c_ref, strip + HALO - 2, strip - 1, strip, sums, squares
+        lower, HALO + 2, a3.at[HALO + 2 :], w_parts, [[]] * 3, c_ref, strip + HALO - 2, strip - 1, strip, sums, squares,
+        tile=SHAPES['outer'],
     )
     write_stats(st, sums, squares)
     for i in range(feature.shape[0]):
@@ -189,18 +188,16 @@
         late.append(pltpu.make_async_copy(cw.at[k + 1, 0], w_next, sems.at[2]))
     for c in waits[1]:
         c.start()
-    after = [waits[2], [], []]
-    after[LATE] = after[LATE] + late
-    for c in after[0]:
+    for c in waits[2] + late:
         c.start()
-    return waits, late, after[1:]
+    return waits, late
 
 
 def hidden_conv_kernel(
     c_in, stats, gain, shift, w_first, cw, c_ref, st, *rest, k, lo, n_in, strip, total, axis
 ):
     *w_next, a3, wbuf, sems = rest
-    waits, late, starts = weight_copies(cw, k + 1, wbuf, w_next[0] if w_next else None, sems)
+    waits, late = weight_copies(cw, k + 1, wbuf, w_next[0] if w_next else None, sems)
     mean, scale, bias = norm_terms(stats, gain, shift, k, total)
 
     def row_at(i):
@@ -208,7 +205,7 @@
         return masked(x, inside(lo + i, strip, axis))
 
     w_parts = [w_first, wbuf.at[0], wbuf.at[1]]
-    write_stats(st, *run_conv(row_at, n_in, a3, w_parts, waits, c_ref, 0, lo + 1, strip, starts=starts))
+    write_stats(st, *run_conv(row_at, n_in, a3, w_parts, waits, c_ref, 0, lo + 1, strip, tile=SHAPES[k]))
     for c in late:
         c.wait()
 
@@ -217,7 +214,7 @@
     c_in, stats, gain, shift, w_first, feature, cw, c_ref, st, w_next, joined, a3, wbuf, sems,
     *, k, lo, n_in, strip, total, axis
 ):
-    waits, late, starts = weight_copies(cw, k + 1, wbuf, w_next, sems)
+    waits, late = weight_copies(cw, k + 1, wbuf, w_next, sems)
     mean, scale, bias = norm_terms(stats, gain, shift, k, total)
 
     def row_at(i):
@@ -226,15 +223,21 @@
         return masked(relu_row(y), inside(lo + i, strip, axis))
 
     w_parts = [w_first, wbuf.at[0], wbuf.at[1]]
-    write_stats(st, *run_conv(row_at, n_in, a3, w_parts, waits, c_ref, 0, lo + 1, strip, starts=starts))
+    write_stats(st, *run_conv(row_at, n_in, a3, w_parts, waits, c_ref, 0, lo + 1, strip, tile=SHAPES[k]))
     for c in late:
         c.wait()
 
 
-def final_kernel(joined, c_in, stats, gain, shift, out, *, k, total):
+def final_kernel(joined, c_in, stats, gain, shift, out, rows, sems, *, k, total):
     mean, scale, bias = norm_terms(stats, gain, shift, k, total)
-    for i in range(out.shape[0]):
-        out[i] = (joined[i + 2].astype(F32) + ((c_in[i] - mean) * scale + bias)).astype(BF)
+    copies = []
+    for i in range(0, rows.shape[0], 2):
+        for j in (i, i + 1):
+            rows[j] = (joined[j + 2].astype(F32) + ((c_in[j] - mean) * scale + bias)).astype(BF)
+        copies.append(pltpu.make_async_copy(rows.at[i : i + 2], out.at[i : i + 2], sems.at[i // 2]))
+        copies[-1].start()
+    for c in copies:
+        c.wait()
 
 
 def sent_to_all(value, axis):
@@ -336,7 +339,8 @@
         functools.partial(final_kernel, k=3, total=total),
         out_shape=sds((strip, cols, ch), BF),
         in_specs=[VM] * 5,
-        out_specs=VM,
+        out_specs=HBM,
+        scratch_shapes=[pltpu.VMEM((strip, cols, ch), BF), pltpu.SemaphoreType.DMA((strip // 2,))],
         compiler_params=PARAMS,
     )(in_vmem(joined), in_vmem(c), in_vmem(st), *norm_args)
     return out[None]

time: 114 us -> 113 us (level)
  Pallas kernels: 15.6 us -> 14.1 us
where the time goes in v4:
time: 113 us
  blocking collectives  91.8 us (81%)
  Pallas kernels  14.1 us (12%)
  starting transfers between devices  4.68 us (4%)
  waiting for transfers between devices  1.64 us (1%)
    all_to_all x8, blocking collectives, sent_to_all(): return lax.all_to_all(value, axis, 0, 0, tiled=True)  91.8 us
    pallas_call x3, Pallas kernels, call(): pl.pallas_call(functools.partial(kernel, n_in=n_in, strip=strip, total=to...  6.88 us
    ppermute x2, starting transfers between devices, swapped(): return lax.ppermute(value, 'row', pairs + [(j, i) for i, j in pairs])  4.68 us
    pallas_call x1, Pallas kernels, on_device(): pl.pallas_call(functools.partial(proj_kernel, axis='row'), out_shape=(hal...  2.46 us
    pallas_call x1, Pallas kernels, on_device(): pl.pallas_call(functools.partial(conv0_inner_kernel, strip=strip, axis='r...  2.29 us
  transfers between devices with their start and end apart: 2, of which 1 were waited for; matrix products, arithmetic and copies ran while one was open for 0% of the time, Pallas kernels for 2%

profile of v4, /device:TPU:1, one launch (start us, length us, event | category | flops | bytes accessed | tf_op | source)
XLA Modules:
  0.0 112.6 jit_solution(611789728807083040)
XLA Ops:
  0.0 2.5 %shard_map.64 = (bf16[4,128,256]{2,1,0:T(8,128)(2,1)S(1)}, bf16[4,128,256]{2,1,0:T(8,128)(2,1)S(1)}) custom-call(bf16[8,128,1024]{2,1,0:T(8,128)(2,1)} %bitcast.3, bf16[1024,256]{1,0:T(8,128)(2,1)} %w.1, f32[1,256]{1,0:T(1,128)} %bitcast.4), custom_call_target="tpu_custom_call" | custom-call | tf_op jit(solution)/shard_map/pallas_call | solution.py:268
  2.5 4.6 %collective-permute-start = (bf16[4,128,256]{2,1,0:T(8,128)(2,1)S(1)}, bf16[4,128,256]{2,1,0:T(8,128)(2,1)S(1)}, u32[]{:S(2)}, u32[]{:S(2)}) collective-permute-start(bf16[4,128,256]{2,1,0:T(8,128)(2,1)S(1)} %get-tuple-element.23.far), channel_id=1, source_target_pairs={{1,2},{3,4},{5,6},{2,1},{4,3},{6,5},{9,10},{11,12},{13,14},{10,9},... | collective-permute-start | bytes 786440 | tf_op jit(solution)/shard_map/ppermute | solution.py:255
  7.1 0.1 collective-permute-start.1
  7.2 2.3 %shard_map.65 = (f32[14,128,256]{2,1,0:T(8,128)S(1)}, f32[2,8,256]{2,1,0:T(8,128)S(1)}, bf16[3,3,256,256]{3,2,1,0:T(8,128)(2,1)S(1)}) custom-call(bf16[4,128,256]{2,1,0:T(8,128)(2,1)S(1)} %get-tuple-element.23.far, bf16[4,128,256]{2,1,0:T(8,128)(2,1)S(1)} %get-tuple-element.24.near, bf16[4,3,3,256,256]{4,3,2,1,0:T(8,128)(2,1)} %cw.9), custom_call_target="tpu_custom_call" | custom-call | flops 905969664 | bytes 1179648 | tf_op jit(solution)/shard_map/pallas_call | solution.py:292
  9.5 1.6 %collective-permute-done.got_far = bf16[4,128,256]{2,1,0:T(8,128)(2,1)S(1)} collective-permute-done((bf16[4,128,256]{2,1,0:T(8,128)(2,1)S(1)}, bf16[4,128,256]{2,1,0:T(8,128)(2,1)S(1)}, u32[]{:S(2)}, u32[]{:S(2)}) %collective-permute-start) | collective-permute-done | bytes 262176 | tf_op jit(solution)/shard_map/ppermute | solution.py:255
  11.1 0.0 collective-permute-done.1.got_near
  11.1 0.0 copy-start
  11.1 0.0 copy-start.1
  11.1 1.6 %shard_map.66 = (f32[14,128,256]{2,1,0:T(8,128)S(1)}, f32[8,1,512]{2,1,0:T(1,128)S(1)}, bf16[12,128,256]{2,1,0:T(8,128)(2,1)S(1)}, bf16[3,256,256]{2,1,0:T(8,128)(2,1)S(1)}) custom-call(bf16[4,128,256]{2,1,0:T(8,128)(2,1)S(1)} %collective-permute-done.got_far, bf16[4,128,256]{2,1,0:T(8,128)(2,1)S(1)} %get-tuple-element.23.far, ...), custom_call_target="tpu_custom_call", output_to_operand_aliasing={{0}: (6, {})} | custom-call | tf_op jit(solution)/shard_map/pallas_call | solution.py:303
  12.7 9.5 %all_to_all.40 = f32[8,1,512]{2,1,0:T(1,128)S(1)} all-to-all(f32[8,1,512]{2,1,0:T(1,128)S(1)} %get-tuple-element.29), channel_id=1, replica_groups=mesh['img'=32,'row'=8] {'row'}, dimensions={0} | all-to-all | bytes 32768 | tf_op jit(solution)/shard_map/all_to_all | solution.py:244
  22.2 19.7 %all_to_all.41.stats = f32[32,1,512]{2,1,0:T(1,128)S(1)} all-to-all(f32[32,1,512]{2,1,0:T(1,128)S(1)} %broadcast_in_dim.13), channel_id=1, replica_groups=mesh['img'=32,'row'=8] {'img'}, dimensions={0} | all-to-all | bytes 131072 | tf_op jit(solution)/shard_map/all_to_all | solution.py:244
  41.9 0.0 copy-done
  41.9 0.0 copy-done.1
  41.9 2.5 %shard_map.67 = (f32[14,128,256]{2,1,0:T(8,128)S(1)}, f32[8,1,512]{2,1,0:T(1,128)S(1)}, bf16[3,256,256]{2,1,0:T(8,128)(2,1)S(1)}) custom-call(f32[14,128,256]{2,1,0:T(8,128)S(1)} %get-tuple-element.28.c_in, f32[32,1,512]{2,1,0:T(1,128)S(1)} %all_to_all.41.stats, f32[4,256]{1,0:T(4,128)S(1)} %copy-done, ...), custom_call_target="tpu_custom_call", output_to_operand_aliasing={{0}: (0, {})} | custom-call | tf_op jit(solution)/shard_map/pallas_call | solution.py:315
  44.4 9.1 %all_to_all.42 = f32[8,1,512]{2,1,0:T(1,128)S(1)} all-to-all(f32[8,1,512]{2,1,0:T(1,128)S(1)} %get-tuple-element.32), channel_id=1, replica_groups=mesh['img'=32,'row'=8] {'row'}, dimensions={0} | all-to-all | bytes 32768 | tf_op jit(solution)/shard_map/all_to_all | solution.py:244
  53.6 11.9 %all_to_all.43.stats = f32[32,1,512]{2,1,0:T(1,128)S(1)} all-to-all(f32[32,1,512]{2,1,0:T(1,128)S(1)} %broadcast_in_dim.14), channel_id=1, replica_groups=mesh['img'=32,'row'=8] {'img'}, dimensions={0} | all-to-all | bytes 131072 | tf_op jit(solution)/shard_map/all_to_all | solution.py:244
  65.5 2.3 %shard_map.68 = (f32[14,128,256]{2,1,0:T(8,128)S(1)}, f32[8,1,512]{2,1,0:T(1,128)S(1)}, bf16[3,256,256]{2,1,0:T(8,128)(2,1)S(1)}, bf16[12,128,256]{2,1,0:T(8,128)(2,1)S(1)}) custom-call(f32[14,128,256]{2,1,0:T(8,128)S(1)} %get-tuple-element.31.c_in, f32[32,1,512]{2,1,0:T(1,128)S(1)} %all_to_all.43.stats, ...), custom_call_target="tpu_custom_call", output_to_operand_aliasing={{0}: (0, {}), {3}: (5, {})} | custom-call | tf_op jit(solution)/shard_map/pallas_call | solution.py:315
  67.8 8.9 %all_to_all.44 = f32[8,1,512]{2,1,0:T(1,128)S(1)} all-to-all(f32[8,1,512]{2,1,0:T(1,128)S(1)} %get-tuple-element.37), channel_id=1, replica_groups=mesh['img'=32,'row'=8] {'row'}, dimensions={0} | all-to-all | bytes 32768 | tf_op jit(solution)/shard_map/all_to_all | solution.py:244
  76.8 11.9 %all_to_all.45.stats = f32[32,1,512]{2,1,0:T(1,128)S(1)} all-to-all(f32[32,1,512]{2,1,0:T(1,128)S(1)} %broadcast_in_dim.15), channel_id=1, replica_groups=mesh['img'=32,'row'=8] {'img'}, dimensions={0} | all-to-all | bytes 131072 | tf_op jit(solution)/shard_map/all_to_all | solution.py:244
  88.7 2.1 %shard_map.69 = (f32[14,128,256]{2,1,0:T(8,128)S(1)}, f32[8,1,512]{2,1,0:T(1,128)S(1)}) custom-call(f32[14,128,256]{2,1,0:T(8,128)S(1)} %get-tuple-element.36.c_in, f32[32,1,512]{2,1,0:T(1,128)S(1)} %all_to_all.45.stats, f32[4,256]{1,0:T(4,128)S(1)} %copy-done, f32[4,256]{1,0:T(4,128)S(1)} %copy-done.1, ...), custom_call_target="tpu_custom_call", output_to_operand_aliasing={{0}: (0, {})} | custom-call | tf_op jit(solution)/shard_map/pallas_call | solution.py:315
  90.8 8.9 %all_to_all.46 = f32[8,1,512]{2,1,0:T(1,128)S(1)} all-to-all(f32[8,1,512]{2,1,0:T(1,128)S(1)} %get-tuple-element.40), channel_id=1, replica_groups=mesh['img'=32,'row'=8] {'row'}, dimensions={0} | all-to-all | bytes 32768 | tf_op jit(solution)/shard_map/all_to_all | solution.py:244
  99.8 11.9 %all_to_all.47.stats = f32[32,1,512]{2,1,0:T(1,128)S(1)} all-to-all(f32[32,1,512]{2,1,0:T(1,128)S(1)} %broadcast_in_dim.16), channel_id=1, replica_groups=mesh['img'=32,'row'=8] {'img'}, dimensions={0} | all-to-all | bytes 131072 | tf_op jit(solution)/shard_map/all_to_all | solution.py:244
  111.7 0.9 shard_map.70
  (8 shorter events, 0.3 us)
Async XLA Ops:
  2.5 8.6 %collective-permute-start = (bf16[4,128,256]{2,1,0:T(8,128)(2,1)S(1)}, bf16[4,128,256]{2,1,0:T(8,128)(2,1)S(1)}, u32[]{:S(2)}, u32[]{:S(2)}) collective-permute-start(bf16[4,128,256]{2,1,0:T(8,128)(2,1)S(1)} %get-tuple-element.23.far), channel_id=1, source_target_pairs={{1,2},{3,4},{5,6},{2,1},{4,3},{6,5},{9,10},{11,12},{13,14},{10,9},... | collective-permute-start | bytes 786440 | tf_op jit(solution)/shard_map/ppermute | solution.py:255
  7.1 4.0 %collective-permute-start.1 = (bf16[4,128,256]{2,1,0:T(8,128)(2,1)S(1)}, bf16[4,128,256]{2,1,0:T(8,128)(2,1)S(1)}, u32[]{:S(2)}, u32[]{:S(2)}) collective-permute-start(bf16[4,128,256]{2,1,0:T(8,128)(2,1)S(1)} %get-tuple-element.24.near), channel_id=1, source_target_pairs={{0,1},{2,3},{4,5},{6,7},{1,0},{3,2},{5,4},{7,6},{8,9},{10,11},{12,... | collective-permute-start | bytes 786440 | tf_op jit(solution)/shard_map/ppermute | solution.py:255
  11.1 30.8 %copy-start = (f32[4,256]{1,0:T(4,128)S(1)}, f32[4,256]{1,0:T(4,128)}, u32[]{:S(2)}) copy-start(f32[4,256]{1,0:T(4,128)} %gain.7) | copy-start | bytes 12292
  11.1 30.8 %copy-start.1 = (f32[4,256]{1,0:T(4,128)S(1)}, f32[4,256]{1,0:T(4,128)}, u32[]{:S(2)}) copy-start(f32[4,256]{1,0:T(4,128)} %shift.7) | copy-start | bytes 12292

commit v5 on v4

--- a/solution.py
+++ b/solution.py
@@ -6,6 +6,7 @@
 from jax.experimental import pallas as pl
 from jax.experimental.pallas import tpu as pltpu
 from jax.sharding import PartitionSpec as P
+
 
 EPS = 1e-05
 HALO = 4
@@ -84,7 +85,7 @@
                 filled += 1
             lhs = a3[done + dy : done + dy + rows].reshape(rows * cols, 3 * ch)
             acc = jnp.dot(lhs, w, preferred_element_type=F32)
-            into = slice(at + done, at + done + rows)
+            into = pl.ds(at + done, rows)
             if dy:
                 acc = acc + c_ref[into].reshape(rows * cols, ch)
             c_ref[into] = acc.reshape(rows, cols, ch)
@@ -102,23 +103,30 @@
     return lax.axis_index(axis) % 2 == 1
 
 
-def proj_kernel(tok, w, bias, far, near, tbuf, wbuf, bbuf, sems, *, axis):
-    rows = tok.shape[0]
-    near_at = jnp.where(near_is_top(axis), 0, HALO)
+def project(tbuf, wbuf, bbuf, out):
+    y = jnp.dot(tbuf[...].reshape(-1, tbuf.shape[2]), wbuf[...], preferred_element_type=F32) + bbuf[...]
+    out[...] = y.astype(BF).reshape(out.shape)
+
+
+def far_proj_kernel(tok, w, bias, far, wbuf, bbuf, tbuf, sems, *, axis):
+    far_at = jnp.where(near_is_top(axis), HALO, 0)
     copies = [
         pltpu.make_async_copy(w, wbuf, sems.at[0]),
         pltpu.make_async_copy(bias, bbuf, sems.at[1]),
-        pltpu.make_async_copy(tok.at[pl.ds(HALO - near_at, HALO)], tbuf.at[0:HALO], sems.at[2]),
-        pltpu.make_async_copy(tok.at[pl.ds(near_at, HALO)], tbuf.at[HALO:], sems.at[3]),
+        pltpu.make_async_copy(tok.at[pl.ds(far_at, HALO)], tbuf, sems.at[2]),
     ]
     for c in copies:
         c.start()
     for c in copies:
         c.wait()
-    y = jnp.dot(tbuf[...].reshape(-1, tok.shape[2]), wbuf[...], preferred_element_type=F32) + bbuf[...]
-    y = y.astype(BF).reshape(rows, tok.shape[1], -1)
-    far[...] = y[:HALO]
-    near[...] = y[HALO:]
+    project(tbuf, wbuf, bbuf, far)
+
+
+def near_proj_kernel(wbuf, bbuf, tok, near, tbuf, sem, *, axis):
+    copy = pltpu.make_async_copy(tok.at[pl.ds(jnp.where(near_is_top(axis), 0, HALO), HALO)], tbuf, sem)
+    copy.start()
+    copy.wait()
+    project(tbuf, wbuf, bbuf, near)
 
 
 def relu_row(x):
@@ -129,9 +137,10 @@
     return jnp.where(cond, a.astype(F32), b.astype(F32))
 
 
-def conv0_inner_kernel(far, near, cw, c_ref, part, w0, a3, sems, *, strip, axis):
+def conv0_inner_kernel(far, near, cw, c_ref, part, w0, w_next, a3, sems, *, strip, axis):
     waits = [[pltpu.make_async_copy(cw.at[0, dy], w0.at[dy], sems.at[dy])] for dy in range(3)]
-    for (copy,) in waits:
+    late = pltpu.make_async_copy(cw.at[1, 0], w_next, sems.at[3])
+    for copy in (*waits[0], *waits[1], *waits[2], late):
         copy.start()
     flip = near_is_top(axis)
 
@@ -140,45 +149,38 @@
         return relu_row(pick(flip, near[j], far[j]) if i < HALO else pick(flip, far[j], near[j]))
 
     w_parts = [w0.at[dy] for dy in range(3)]
-    part[0], part[1] = run_conv(row_at, strip, a3, w_parts, waits, c_ref, HALO, 1, strip, tile=SHAPES['inner'])
-
-
-def conv0_outer_kernel(
-    got_far, far, near, got_near, w0, part, c_in, cw, c_ref, st, feature, w_next, a3, sem, *, strip, axis
-):
-    late = pltpu.make_async_copy(cw.at[1, 0], w_next, sem)
-    late.start()
+    part[0], part[1] = run_conv(row_at, strip, a3, w_parts, waits, c_ref, HALO, 1, strip, tile=SHAPES["inner"])
+    late.wait()
+
+
+def conv0_edge(got, own, w0, part, c_ref, a3, upper, strip):
+    def row_at(i):
+        above = got[i] if i < HALO else own[i - HALO]
+        below = own[i + HALO - 2] if i < 2 else got[i - 2]
+        return relu_row(pick(upper, above, below))
+
     w_parts = [w0.at[dy] for dy in range(3)]
+    at = jnp.where(upper, 0, strip + HALO - 2)
+    run_conv(row_at, HALO + 2, a3, w_parts, [[]] * 3, c_ref, at, strip, strip, tile=SHAPES["outer"])
+    row = c_ref[jnp.where(upper, HALO - 1, strip + HALO - 2)]
+    return part[0] + fold8(row), part[1] + fold8(row * row)
+
+
+def conv0_near_kernel(got, far, near, w0, part_in, c_in, c_ref, part, feature, a3, *, strip, axis):
     flip = near_is_top(axis)
-
-    def strip_row(i):
-        j = i % HALO
-        if i < 0:
-            return pick(flip, got_near[j], got_far[j])
-        if i < HALO:
-            return pick(flip, near[j], far[j])
-        if i < strip:
-            return pick(flip, far[j], near[j])
-        return pick(flip, got_far[j], got_near[j])
-
-    def upper(i):
-        return relu_row(strip_row(i - HALO))
-
-    def lower(i):
-        return relu_row(strip_row(strip - 2 + i))
-
-    sums, squares = run_conv(
-        upper, HALO + 2, a3.at[: HALO + 2], w_parts, [[]] * 3, c_ref, 0, 1 - HALO, strip, part[0], part[1],
-        tile=SHAPES['outer'],
-    )
-    sums, squares = run_conv(
-        lower, HALO + 2, a3.at[HALO + 2 :], w_parts, [[]] * 3, c_ref, strip + HALO - 2, strip - 1, strip, sums, squares,
-        tile=SHAPES['outer'],
-    )
+    part[0], part[1] = conv0_edge(got, near, w0, part_in, c_ref, a3, flip, strip)
+    near_at = jnp.where(flip, 0, HALO)
+    feature[pl.ds(2 + near_at, HALO)] = near[...]
+    feature[pl.ds(2 + HALO - near_at, HALO)] = far[...]
+    feature[pl.ds(jnp.where(flip, 0, strip + 2), 2)] = got[pl.ds(jnp.where(flip, HALO - 2, 0), 2)]
+
+
+def conv0_far_kernel(got, far, w0, part, c_in, feature_in, c_ref, st, feature, a3, *, strip, axis):
+    flip = near_is_top(axis)
+    upper = jnp.logical_not(flip)
+    sums, squares = conv0_edge(got, far, w0, part, c_ref, a3, upper, strip)
     write_stats(st, sums, squares)
-    for i in range(feature.shape[0]):
-        feature[i] = strip_row(i - 2).astype(BF)
-    late.wait()
+    feature[pl.ds(jnp.where(flip, strip + 2, 0), 2)] = got[pl.ds(jnp.where(flip, 0, HALO - 2), 2)]
 
 
 def weight_copies(cw, k, wbuf, w_next, sems):
@@ -265,20 +267,28 @@
 
     half = sds((HALO, cols, ch), BF)
     w_third = sds((3, ch, ch), BF)
-    far, near = pl.pallas_call(
-        functools.partial(proj_kernel, axis="row"),
-        out_shape=(half, half),
+    token_rows = in_hbm(tokens[0])
+    far, pw, pb = pl.pallas_call(
+        functools.partial(far_proj_kernel, axis="row"),
+        out_shape=(half, sds((embed, ch), BF), sds((1, ch), F32)),
         in_specs=[HBM] * 3,
-        out_specs=(VM, VM),
-        scratch_shapes=[
-            pltpu.VMEM((strip, cols, embed), BF),
-            pltpu.VMEM((embed, ch), BF),
-            pltpu.VMEM((1, ch), F32),
-            pltpu.SemaphoreType.DMA((4,)),
-        ],
-        compiler_params=PARAMS,
-    )(in_hbm(tokens[0]), in_hbm(proj_weight), in_hbm(proj_bias[None]))
+        out_specs=(VM,) * 3,
+        scratch_shapes=[pltpu.VMEM((HALO, cols, embed), BF), pltpu.SemaphoreType.DMA((3,))],
+        compiler_params=PARAMS,
+    )(token_rows, in_hbm(proj_weight), in_hbm(proj_bias[None]))
     got_far = swapped(far, range(1, nrow - 1, 2))
+    near_call = pl.pallas_call(
+        functools.partial(near_proj_kernel, axis="row"),
+        out_shape=half,
+        in_specs=[VM, VM, HBM],
+        out_specs=VM,
+        scratch_shapes=[pltpu.VMEM((HALO, cols, embed), BF), pltpu.SemaphoreType.DMA(())],
+        compiler_params=PARAMS,
+        cost_estimate=pl.CostEstimate(
+            flops=2 * embed * ch * cols * HALO, transcendentals=0, bytes_accessed=2 * HALO * cols * embed
+        ),
+    )
+    near = near_call(in_vmem(pw), in_vmem(pb), token_rows)
     got_near = swapped(near, range(0, nrow - 1, 2))
     far, near, got_far, got_near = map(in_vmem, (far, near, got_far, got_near))
 
@@ -289,26 +299,43 @@
     def rows_scratch(rows):
         return pltpu.VMEM((rows, cols, 3 * ch), BF)
 
-    c0, part, w0 = pl.pallas_call(
+    sums = sds((2, 8, ch), F32)
+
+    def conv_flops(rows):
+        return pl.CostEstimate(
+            flops=2 * 9 * ch * ch * cols * rows, transcendentals=0, bytes_accessed=9 * ch * ch * 2
+        )
+
+    c, part, w0, w_next = pl.pallas_call(
         functools.partial(conv0_inner_kernel, strip=strip, axis="row"),
-        out_shape=(field, sds((2, 8, ch), F32), sds((3, 3, ch, ch), BF)),
+        out_shape=(field, sums, sds((3, 3, ch, ch), BF), w_third),
         in_specs=[VM, VM, HBM],
+        out_specs=(VM,) * 4,
+        scratch_shapes=[rows_scratch(strip), pltpu.SemaphoreType.DMA((4,))],
+        compiler_params=PARAMS,
+        cost_estimate=conv_flops(strip - 2),
+    )(far, near, weights)
+    w0 = in_vmem(w0)
+    c, part, feature = pl.pallas_call(
+        functools.partial(conv0_near_kernel, strip=strip, axis="row"),
+        out_shape=(field, sums, context),
+        in_specs=[VM] * 6,
         out_specs=(VM,) * 3,
-        scratch_shapes=[rows_scratch(strip), pltpu.SemaphoreType.DMA((3,))],
-        compiler_params=PARAMS,
-        cost_estimate=pl.CostEstimate(
-            flops=2 * 9 * ch * ch * cols * (strip - 2), transcendentals=0, bytes_accessed=9 * ch * ch * 2
-        ),
-    )(far, near, weights)
-    c, st, feature, w_next = pl.pallas_call(
-        functools.partial(conv0_outer_kernel, strip=strip, axis="row"),
-        out_shape=(field, stat, context, w_third),
-        in_specs=[VM] * 7 + [HBM],
-        out_specs=(VM,) * 4,
-        input_output_aliases={6: 0},
-        scratch_shapes=[rows_scratch(2 * HALO + 4), pltpu.SemaphoreType.DMA(())],
-        compiler_params=PARAMS,
-    )(got_far, far, near, got_near, in_vmem(w0), in_vmem(part), in_vmem(c0), weights)
+        input_output_aliases={5: 0},
+        scratch_shapes=[rows_scratch(HALO + 2)],
+        compiler_params=PARAMS,
+        cost_estimate=conv_flops(HALO),
+    )(got_near, far, near, w0, in_vmem(part), in_vmem(c))
+    c, st, feature = pl.pallas_call(
+        functools.partial(conv0_far_kernel, strip=strip, axis="row"),
+        out_shape=(field, stat, context),
+        in_specs=[VM] * 6,
+        out_specs=(VM,) * 3,
+        input_output_aliases={4: 0, 5: 2},
+        scratch_shapes=[rows_scratch(HALO + 2)],
+        compiler_params=PARAMS,
+        cost_estimate=conv_flops(HALO),
+    )(got_far, far, w0, in_vmem(part), in_vmem(c), in_vmem(feature))
 
     def call(kernel, extra_in, extra_out, n_in, aliases, **kw):
         args = (in_vmem(c), in_vmem(st), *norm_args, *map(in_vmem, extra_in))

time: 113 us -> 114 us (level)
  blocking collectives: 91.8 us -> 89.6 us
  Pallas kernels: 14.1 us -> 15.4 us
    all_to_all x8, blocking collectives: 91.8 us -> 89.6 us  [sent_to_all(): return lax.all_to_all(value, axis, 0, 0, tiled=True)]
    pallas_call x2 -> x4, Pallas kernels: 4.03 us -> 5.24 us  [the longest x1 1.87 us: on_device(): pl.pallas_call(functools.partial(far_proj_kernel, axis='row'), out_shape=...]
  transfers between devices with their start and end apart: 2 -> 2, of which waited for: 1 -> 1; matrix products, arithmetic and copies ran while one was open for 0% -> 0% of each run, Pallas kernels for 2% -> 3%
where the time goes in v5:
time: 114 us; the launch traced here: 113 us
  blocking collectives  89.6 us (79%)
  Pallas kernels  15.4 us (14%)
  starting transfers between devices  5.2 us (5%)
  waiting for transfers between devices  2.6 us (2%)
    all_to_all x8, blocking collectives, sent_to_all(): return lax.all_to_all(value, axis, 0, 0, tiled=True)  89.6 us
    pallas_call x3, Pallas kernels, call(): pl.pallas_call(functools.partial(kernel, n_in=n_in, strip=strip, total=to...  6.89 us
    ppermute x2, starting transfers between devices, swapped(): return lax.ppermute(value, 'row', pairs + [(j, i) for i, j in pairs])  5.2 us
    ppermute x2, waiting for transfers between devices, swapped(): return lax.ppermute(value, 'row', pairs + [(j, i) for i, j in pairs])  2.6 us
    pallas_call x1, Pallas kernels, on_device(): pl.pallas_call(functools.partial(conv0_inner_kernel, strip=strip, axis='r...  2.3 us
  transfers between devices with their start and end apart: 2, of which 1 were waited for; matrix products, arithmetic and copies ran while one was open for 0% of the time, Pallas kernels for 3%

profile of v5, /device:TPU:1, one launch (start us, length us, event | category | flops | bytes accessed | tf_op | source)
XLA Modules:
  0.0 113.2 jit_solution(6622724089743520276)
XLA Ops:
  0.0 1.9 %shard_map.64 = (bf16[4,128,256]{2,1,0:T(8,128)(2,1)S(1)}, bf16[1024,256]{1,0:T(8,128)(2,1)S(1)}, f32[1,256]{1,0:T(1,128)S(1)}) custom-call(bf16[8,128,1024]{2,1,0:T(8,128)(2,1)} %bitcast.3, bf16[1024,256]{1,0:T(8,128)(2,1)} %w.1, f32[1,256]{1,0:T(1,128)} %bitcast.5), custom_call_target="tpu_custom_call" | custom-call | tf_op jit(solution)/shard_map/pallas_call | solution.py:271
  1.9 1.7 %shard_map.65.near = bf16[4,128,256]{2,1,0:T(8,128)(2,1)S(1)} custom-call(bf16[1024,256]{1,0:T(8,128)(2,1)S(1)} %get-tuple-element.28.wbuf, f32[1,256]{1,0:T(1,128)S(1)} %get-tuple-element.29.bbuf, bf16[8,128,1024]{2,1,0:T(8,128)(2,1)} %bitcast.4), custom_call_target="tpu_custom_call" | custom-call | flops 268435456 | bytes 1048576 | tf_op jit(solution)/shard_map/pallas_call | solution.py:291
  3.6 3.3 %collective-permute-start.1 = (bf16[4,128,256]{2,1,0:T(8,128)(2,1)S(1)}, bf16[4,128,256]{2,1,0:T(8,128)(2,1)S(1)}, u32[]{:S(2)}, u32[]{:S(2)}) collective-permute-start(bf16[4,128,256]{2,1,0:T(8,128)(2,1)S(1)} %shard_map.65.near), channel_id=1, source_target_pairs={{0,1},{2,3},{4,5},{6,7},{1,0},{3,2},{5,4},{7,6},{8,9},{10,11},{12,... | collective-permute-start | bytes 786440 | tf_op jit(solution)/shard_map/ppermute | solution.py:257
  6.9 1.9 %collective-permute-start = (bf16[4,128,256]{2,1,0:T(8,128)(2,1)S(1)}, bf16[4,128,256]{2,1,0:T(8,128)(2,1)S(1)}, u32[]{:S(2)}, u32[]{:S(2)}) collective-permute-start(bf16[4,128,256]{2,1,0:T(8,128)(2,1)S(1)} %get-tuple-element.27.far), channel_id=1, source_target_pairs={{1,2},{3,4},{5,6},{2,1},{4,3},{6,5},{9,10},{11,12},{13,14},{10,9},... | collective-permute-start | bytes 786440 | tf_op jit(solution)/shard_map/ppermute | solution.py:257
  8.8 2.3 %shard_map.66 = (f32[14,128,256]{2,1,0:T(8,128)S(1)}, f32[2,8,256]{2,1,0:T(8,128)S(1)}, bf16[3,3,256,256]{3,2,1,0:T(8,128)(2,1)S(1)}, bf16[3,256,256]{2,1,0:T(8,128)(2,1)S(1)}) custom-call(bf16[4,128,256]{2,1,0:T(8,128)(2,1)S(1)} %get-tuple-element.27.far, bf16[4,128,256]{2,1,0:T(8,128)(2,1)S(1)} %shard_map.65.near, bf16[4,3,3,256,256]{4,3,2,1,0:T(8,128)(2,1)} %cw.7), custom_call_target="tpu_custom_call" | custom-call | flops 905969664 | bytes 1179648 | tf_op jit(solution)/shard_map/pallas_call | solution.py:309
  11.1 0.0 collective-permute-done.1.got
  11.1 0.8 shard_map.67
  11.9 2.6 %collective-permute-done.got = bf16[4,128,256]{2,1,0:T(8,128)(2,1)S(1)} collective-permute-done((bf16[4,128,256]{2,1,0:T(8,128)(2,1)S(1)}, bf16[4,128,256]{2,1,0:T(8,128)(2,1)S(1)}, u32[]{:S(2)}, u32[]{:S(2)}) %collective-permute-start) | collective-permute-done | bytes 262176 | tf_op jit(solution)/shard_map/ppermute | solution.py:257
  14.5 0.0 copy-start
  14.5 0.0 copy-start.1
  14.5 0.8 shard_map.68
  15.4 7.3 %all_to_all.40 = f32[8,1,512]{2,1,0:T(1,128)S(1)} all-to-all(f32[8,1,512]{2,1,0:T(1,128)S(1)} %get-tuple-element.37), channel_id=1, replica_groups=mesh['img'=32,'row'=8] {'row'}, dimensions={0} | all-to-all | bytes 32768 | tf_op jit(solution)/shard_map/all_to_all | solution.py:246
  22.8 19.7 %all_to_all.41.stats = f32[32,1,512]{2,1,0:T(1,128)S(1)} all-to-all(f32[32,1,512]{2,1,0:T(1,128)S(1)} %broadcast_in_dim.13), channel_id=1, replica_groups=mesh['img'=32,'row'=8] {'img'}, dimensions={0} | all-to-all | bytes 131072 | tf_op jit(solution)/shard_map/all_to_all | solution.py:246
  42.4 0.0 copy-done
  42.4 0.0 copy-done.1
  42.4 2.5 %shard_map.69 = (f32[14,128,256]{2,1,0:T(8,128)S(1)}, f32[8,1,512]{2,1,0:T(1,128)S(1)}, bf16[3,256,256]{2,1,0:T(8,128)(2,1)S(1)}) custom-call(f32[14,128,256]{2,1,0:T(8,128)S(1)} %get-tuple-element.36.c_in, f32[32,1,512]{2,1,0:T(1,128)S(1)} %all_to_all.41.stats, f32[4,256]{1,0:T(4,128)S(1)} %copy-done, ...), custom_call_target="tpu_custom_call", output_to_operand_aliasing={{0}: (0, {})} | custom-call | tf_op jit(solution)/shard_map/pallas_call | solution.py:342
  45.0 9.1 %all_to_all.42 = f32[8,1,512]{2,1,0:T(1,128)S(1)} all-to-all(f32[8,1,512]{2,1,0:T(1,128)S(1)} %get-tuple-element.40), channel_id=1, replica_groups=mesh['img'=32,'row'=8] {'row'}, dimensions={0} | all-to-all | bytes 32768 | tf_op jit(solution)/shard_map/all_to_all | solution.py:246
  54.2 11.9 %all_to_all.43.stats = f32[32,1,512]{2,1,0:T(1,128)S(1)} all-to-all(f32[32,1,512]{2,1,0:T(1,128)S(1)} %broadcast_in_dim.14), channel_id=1, replica_groups=mesh['img'=32,'row'=8] {'img'}, dimensions={0} | all-to-all | bytes 131072 | tf_op jit(solution)/shard_map/all_to_all | solution.py:246
  66.1 2.3 %shard_map.70 = (f32[14,128,256]{2,1,0:T(8,128)S(1)}, f32[8,1,512]{2,1,0:T(1,128)S(1)}, bf16[3,256,256]{2,1,0:T(8,128)(2,1)S(1)}, bf16[12,128,256]{2,1,0:T(8,128)(2,1)S(1)}) custom-call(f32[14,128,256]{2,1,0:T(8,128)S(1)} %get-tuple-element.39.c_in, f32[32,1,512]{2,1,0:T(1,128)S(1)} %all_to_all.43.stats, ...), custom_call_target="tpu_custom_call", output_to_operand_aliasing={{0}: (0, {}), {3}: (5, {})} | custom-call | tf_op jit(solution)/shard_map/pallas_call | solution.py:342
  68.4 8.9 %all_to_all.44 = f32[8,1,512]{2,1,0:T(1,128)S(1)} all-to-all(f32[8,1,512]{2,1,0:T(1,128)S(1)} %get-tuple-element.45), channel_id=1, replica_groups=mesh['img'=32,'row'=8] {'row'}, dimensions={0} | all-to-all | bytes 32768 | tf_op jit(solution)/shard_map/all_to_all | solution.py:246
  77.3 11.9 %all_to_all.45.stats = f32[32,1,512]{2,1,0:T(1,128)S(1)} all-to-all(f32[32,1,512]{2,1,0:T(1,128)S(1)} %broadcast_in_dim.15), channel_id=1, replica_groups=mesh['img'=32,'row'=8] {'img'}, dimensions={0} | all-to-all | bytes 131072 | tf_op jit(solution)/shard_map/all_to_all | solution.py:246
  89.3 2.1 %shard_map.71 = (f32[14,128,256]{2,1,0:T(8,128)S(1)}, f32[8,1,512]{2,1,0:T(1,128)S(1)}) custom-call(f32[14,128,256]{2,1,0:T(8,128)S(1)} %get-tuple-element.44.c_in, f32[32,1,512]{2,1,0:T(1,128)S(1)} %all_to_all.45.stats, f32[4,256]{1,0:T(4,128)S(1)} %copy-done, f32[4,256]{1,0:T(4,128)S(1)} %copy-done.1, ...), custom_call_target="tpu_custom_call", output_to_operand_aliasing={{0}: (0, {})} | custom-call | tf_op jit(solution)/shard_map/pallas_call | solution.py:342
  91.4 8.9 %all_to_all.46 = f32[8,1,512]{2,1,0:T(1,128)S(1)} all-to-all(f32[8,1,512]{2,1,0:T(1,128)S(1)} %get-tuple-element.48), channel_id=1, replica_groups=mesh['img'=32,'row'=8] {'row'}, dimensions={0} | all-to-all | bytes 32768 | tf_op jit(solution)/shard_map/all_to_all | solution.py:246
  100.3 11.9 %all_to_all.47.stats = f32[32,1,512]{2,1,0:T(1,128)S(1)} all-to-all(f32[32,1,512]{2,1,0:T(1,128)S(1)} %broadcast_in_dim.16), channel_id=1, replica_groups=mesh['img'=32,'row'=8] {'img'}, dimensions={0} | all-to-all | bytes 131072 | tf_op jit(solution)/shard_map/all_to_all | solution.py:246
  112.2 0.9 shard_map.72
  (8 shorter events, 0.3 us)
Async XLA Ops:
  3.6 7.5 %collective-permute-start.1 = (bf16[4,128,256]{2,1,0:T(8,128)(2,1)S(1)}, bf16[4,128,256]{2,1,0:T(8,128)(2,1)S(1)}, u32[]{:S(2)}, u32[]{:S(2)}) collective-permute-start(bf16[4,128,256]{2,1,0:T(8,128)(2,1)S(1)} %shard_map.65.near), channel_id=1, source_target_pairs={{0,1},{2,3},{4,5},{6,7},{1,0},{3,2},{5,4},{7,6},{8,9},{10,11},{12,... | collective-permute-start | bytes 786440 | tf_op jit(solution)/shard_map/ppermute | solution.py:257
  6.9 7.7 %collective-permute-start = (bf16[4,128,256]{2,1,0:T(8,128)(2,1)S(1)}, bf16[4,128,256]{2,1,0:T(8,128)(2,1)S(1)}, u32[]{:S(2)}, u32[]{:S(2)}) collective-permute-start(bf16[4,128,256]{2,1,0:T(8,128)(2,1)S(1)} %get-tuple-element.27.far), channel_id=1, source_target_pairs={{1,2},{3,4},{5,6},{2,1},{4,3},{6,5},{9,10},{11,12},{13,14},{10,9},... | collective-permute-start | bytes 786440 | tf_op jit(solution)/shard_map/ppermute | solution.py:257
  14.5 27.9 %copy-start = (f32[4,256]{1,0:T(4,128)S(1)}, f32[4,256]{1,0:T(4,128)}, u32[]{:S(2)}) copy-start(f32[4,256]{1,0:T(4,128)} %gain.7) | copy-start | bytes 12292
  14.5 27.9 %copy-start.1 = (f32[4,256]{1,0:T(4,128)S(1)}, f32[4,256]{1,0:T(4,128)}, u32[]{:S(2)}) copy-start(f32[4,256]{1,0:T(4,128)} %shift.7) | copy-start | bytes 12292

commit v6 on v5

--- a/solution.py
+++ b/solution.py
@@ -153,10 +153,13 @@
     late.wait()
 
 
-def conv0_edge(got, own, w0, part, c_ref, a3, upper, strip):
+def conv0_edge(got, own, w0, part, c_ref, a3, upper, strip, exists=None):
+    def theirs(i):
+        return got[i] if exists is None else got[i].astype(F32) * exists
+
     def row_at(i):
-        above = got[i] if i < HALO else own[i - HALO]
-        below = own[i + HALO - 2] if i < 2 else got[i - 2]
+        above = theirs(i) if i < HALO else own[i - HALO]
+        below = own[i + HALO - 2] if i < 2 else theirs(i - 2)
         return relu_row(pick(upper, above, below))
 
     w_parts = [w0.at[dy] for dy in range(3)]
@@ -178,7 +181,9 @@
 def conv0_far_kernel(got, far, w0, part, c_in, feature_in, c_ref, st, feature, a3, *, strip, axis):
     flip = near_is_top(axis)
     upper = jnp.logical_not(flip)
-    sums, squares = conv0_edge(got, far, w0, part, c_ref, a3, upper, strip)
+    r = lax.axis_index(axis)
+    exists = jnp.logical_and(r > 0, r < lax.axis_size(axis) - 1).astype(F32)
+    sums, squares = conv0_edge(got, far, w0, part, c_ref, a3, upper, strip, exists)
     write_stats(st, sums, squares)
     feature[pl.ds(jnp.where(flip, strip + 2, 0), 2)] = got[pl.ds(jnp.where(flip, 0, HALO - 2), 2)]
 
@@ -253,7 +258,7 @@
 
 
 def swapped(value, firsts):
-    pairs = [(i, i + 1) for i in firsts]
+    pairs = [(i, (i + 1) % lax.axis_size("row")) for i in firsts]
     return lax.ppermute(value, "row", pairs + [(j, i) for i, j in pairs])
 
 
@@ -276,7 +281,7 @@
         scratch_shapes=[pltpu.VMEM((HALO, cols, embed), BF), pltpu.SemaphoreType.DMA((3,))],
         compiler_params=PARAMS,
     )(token_rows, in_hbm(proj_weight), in_hbm(proj_bias[None]))
-    got_far = swapped(far, range(1, nrow - 1, 2))
+    got_far = swapped(far, range(1, nrow, 2))
     near_call = pl.pallas_call(
         functools.partial(near_proj_kernel, axis="row"),
         out_shape=half,

time: 114 us -> 113 us (level)
  starting transfers between devices: 5.2 us -> 3.29 us
    ppermute x2, starting transfers between devices: 5.2 us -> 3.29 us  [swapped(): return lax.ppermute(value, 'row', pairs + [(j, i) for i, j in pairs])]
where the time goes in v6:
time: 113 us; the launch traced here: 112 us
  blocking collectives  90.4 us (80%)
  Pallas kernels  15.4 us (14%)
  starting transfers between devices  3.29 us (3%)
  waiting for transfers between devices  2.93 us (3%)
    all_to_all x8, blocking collectives, sent_to_all(): return lax.all_to_all(value, axis, 0, 0, tiled=True)  90.4 us
    pallas_call x3, Pallas kernels, call(): pl.pallas_call(functools.partial(kernel, n_in=n_in, strip=strip, total=to...  6.88 us
    ppermute x2, starting transfers between devices, swapped(): return lax.ppermute(value, 'row', pairs + [(j, i) for i, j in pairs])  3.29 us
    ppermute x2, waiting for transfers between devices, swapped(): return lax.ppermute(value, 'row', pairs + [(j, i) for i, j in pairs])  2.93 us
    pallas_call x1, Pallas kernels, on_device(): pl.pallas_call(functools.partial(conv0_inner_kernel, strip=strip, axis='r...  2.3 us
  transfers between devices with their start and end apart: 2, of which 1 were waited for; matrix products, arithmetic and copies ran while one was open for 0% of the time, Pallas kernels for 3%

profile of v6, /device:TPU:1, one launch (start us, length us, event | category | flops | bytes accessed | tf_op | source)
XLA Modules:
  0.0 112.4 jit_solution(17834617485352323007)
XLA Ops:
  0.0 1.9 %shard_map.64 = (bf16[4,128,256]{2,1,0:T(8,128)(2,1)S(1)}, bf16[1024,256]{1,0:T(8,128)(2,1)S(1)}, f32[1,256]{1,0:T(1,128)S(1)}) custom-call(bf16[8,128,1024]{2,1,0:T(8,128)(2,1)} %bitcast.3, bf16[1024,256]{1,0:T(8,128)(2,1)} %w.1, f32[1,256]{1,0:T(1,128)} %bitcast.5), custom_call_target="tpu_custom_call" | custom-call | tf_op jit(solution)/shard_map/pallas_call | solution.py:276
  1.9 1.7 %shard_map.65.near = bf16[4,128,256]{2,1,0:T(8,128)(2,1)S(1)} custom-call(bf16[1024,256]{1,0:T(8,128)(2,1)S(1)} %get-tuple-element.28.wbuf, f32[1,256]{1,0:T(1,128)S(1)} %get-tuple-element.29.bbuf, bf16[8,128,1024]{2,1,0:T(8,128)(2,1)} %bitcast.4), custom_call_target="tpu_custom_call" | custom-call | flops 268435456 | bytes 1048576 | tf_op jit(solution)/shard_map/pallas_call | solution.py:296
  3.6 3.3 %collective-permute-start.1 = (bf16[4,128,256]{2,1,0:T(8,128)(2,1)S(1)}, bf16[4,128,256]{2,1,0:T(8,128)(2,1)S(1)}, u32[]{:S(2)}, u32[]{:S(2)}) collective-permute-start(bf16[4,128,256]{2,1,0:T(8,128)(2,1)S(1)} %shard_map.65.near), channel_id=1, source_target_pairs={{0,1},{2,3},{4,5},{6,7},{1,0},{3,2},{5,4},{7,6},{8,9},{10,11},{12,... | collective-permute-start | bytes 786440 | tf_op jit(solution)/shard_map/ppermute | solution.py:262
  6.9 0.0 collective-permute-start
  6.9 2.3 %shard_map.66 = (f32[14,128,256]{2,1,0:T(8,128)S(1)}, f32[2,8,256]{2,1,0:T(8,128)S(1)}, bf16[3,3,256,256]{3,2,1,0:T(8,128)(2,1)S(1)}, bf16[3,256,256]{2,1,0:T(8,128)(2,1)S(1)}) custom-call(bf16[4,128,256]{2,1,0:T(8,128)(2,1)S(1)} %get-tuple-element.27.far, bf16[4,128,256]{2,1,0:T(8,128)(2,1)S(1)} %shard_map.65.near, bf16[4,3,3,256,256]{4,3,2,1,0:T(8,128)(2,1)} %cw.7), custom_call_target="tpu_custom_call" | custom-call | flops 905969664 | bytes 1179648 | tf_op jit(solution)/shard_map/pallas_call | solution.py:314
  9.2 0.0 collective-permute-done.1.got
  9.2 0.8 shard_map.67
  10.0 2.9 %collective-permute-done.got = bf16[4,128,256]{2,1,0:T(8,128)(2,1)S(1)} collective-permute-done((bf16[4,128,256]{2,1,0:T(8,128)(2,1)S(1)}, bf16[4,128,256]{2,1,0:T(8,128)(2,1)S(1)}, u32[]{:S(2)}, u32[]{:S(2)}) %collective-permute-start) | collective-permute-done | bytes 262176 | tf_op jit(solution)/shard_map/ppermute | solution.py:262
  12.9 0.0 copy-start
  13.0 0.0 copy-start.1
  13.0 0.9 shard_map.68
  13.8 8.1 %all_to_all.40 = f32[8,1,512]{2,1,0:T(1,128)S(1)} all-to-all(f32[8,1,512]{2,1,0:T(1,128)S(1)} %get-tuple-element.37), channel_id=1, replica_groups=mesh['img'=32,'row'=8] {'row'}, dimensions={0} | all-to-all | bytes 32768 | tf_op jit(solution)/shard_map/all_to_all | solution.py:251
  21.9 19.7 %all_to_all.41.stats = f32[32,1,512]{2,1,0:T(1,128)S(1)} all-to-all(f32[32,1,512]{2,1,0:T(1,128)S(1)} %broadcast_in_dim.13), channel_id=1, replica_groups=mesh['img'=32,'row'=8] {'img'}, dimensions={0} | all-to-all | bytes 131072 | tf_op jit(solution)/shard_map/all_to_all | solution.py:251
  41.6 0.0 copy-done
  41.6 0.0 copy-done.1
  41.6 2.5 %shard_map.69 = (f32[14,128,256]{2,1,0:T(8,128)S(1)}, f32[8,1,512]{2,1,0:T(1,128)S(1)}, bf16[3,256,256]{2,1,0:T(8,128)(2,1)S(1)}) custom-call(f32[14,128,256]{2,1,0:T(8,128)S(1)} %get-tuple-element.36.c_in, f32[32,1,512]{2,1,0:T(1,128)S(1)} %all_to_all.41.stats, f32[4,256]{1,0:T(4,128)S(1)} %copy-done, ...), custom_call_target="tpu_custom_call", output_to_operand_aliasing={{0}: (0, {})} | custom-call | tf_op jit(solution)/shard_map/pallas_call | solution.py:347
  44.1 9.1 %all_to_all.42 = f32[8,1,512]{2,1,0:T(1,128)S(1)} all-to-all(f32[8,1,512]{2,1,0:T(1,128)S(1)} %get-tuple-element.40), channel_id=1, replica_groups=mesh['img'=32,'row'=8] {'row'}, dimensions={0} | all-to-all | bytes 32768 | tf_op jit(solution)/shard_map/all_to_all | solution.py:251
  53.3 11.9 %all_to_all.43.stats = f32[32,1,512]{2,1,0:T(1,128)S(1)} all-to-all(f32[32,1,512]{2,1,0:T(1,128)S(1)} %broadcast_in_dim.14), channel_id=1, replica_groups=mesh['img'=32,'row'=8] {'img'}, dimensions={0} | all-to-all | bytes 131072 | tf_op jit(solution)/shard_map/all_to_all | solution.py:251
  65.2 2.3 %shard_map.70 = (f32[14,128,256]{2,1,0:T(8,128)S(1)}, f32[8,1,512]{2,1,0:T(1,128)S(1)}, bf16[3,256,256]{2,1,0:T(8,128)(2,1)S(1)}, bf16[12,128,256]{2,1,0:T(8,128)(2,1)S(1)}) custom-call(f32[14,128,256]{2,1,0:T(8,128)S(1)} %get-tuple-element.39.c_in, f32[32,1,512]{2,1,0:T(1,128)S(1)} %all_to_all.43.stats, ...), custom_call_target="tpu_custom_call", output_to_operand_aliasing={{0}: (0, {}), {3}: (5, {})} | custom-call | tf_op jit(solution)/shard_map/pallas_call | solution.py:347
  67.6 8.9 %all_to_all.44 = f32[8,1,512]{2,1,0:T(1,128)S(1)} all-to-all(f32[8,1,512]{2,1,0:T(1,128)S(1)} %get-tuple-element.45), channel_id=1, replica_groups=mesh['img'=32,'row'=8] {'row'}, dimensions={0} | all-to-all | bytes 32768 | tf_op jit(solution)/shard_map/all_to_all | solution.py:251
  76.5 11.9 %all_to_all.45.stats = f32[32,1,512]{2,1,0:T(1,128)S(1)} all-to-all(f32[32,1,512]{2,1,0:T(1,128)S(1)} %broadcast_in_dim.15), channel_id=1, replica_groups=mesh['img'=32,'row'=8] {'img'}, dimensions={0} | all-to-all | bytes 131072 | tf_op jit(solution)/shard_map/all_to_all | solution.py:251
  88.4 2.1 %shard_map.71 = (f32[14,128,256]{2,1,0:T(8,128)S(1)}, f32[8,1,512]{2,1,0:T(1,128)S(1)}) custom-call(f32[14,128,256]{2,1,0:T(8,128)S(1)} %get-tuple-element.44.c_in, f32[32,1,512]{2,1,0:T(1,128)S(1)} %all_to_all.45.stats, f32[4,256]{1,0:T(4,128)S(1)} %copy-done, f32[4,256]{1,0:T(4,128)S(1)} %copy-done.1, ...), custom_call_target="tpu_custom_call", output_to_operand_aliasing={{0}: (0, {})} | custom-call | tf_op jit(solution)/shard_map/pallas_call | solution.py:347
  90.5 8.9 %all_to_all.46 = f32[8,1,512]{2,1,0:T(1,128)S(1)} all-to-all(f32[8,1,512]{2,1,0:T(1,128)S(1)} %get-tuple-element.48), channel_id=1, replica_groups=mesh['img'=32,'row'=8] {'row'}, dimensions={0} | all-to-all | bytes 32768 | tf_op jit(solution)/shard_map/all_to_all | solution.py:251
  99.5 11.9 %all_to_all.47.stats = f32[32,1,512]{2,1,0:T(1,128)S(1)} all-to-all(f32[32,1,512]{2,1,0:T(1,128)S(1)} %broadcast_in_dim.16), channel_id=1, replica_groups=mesh['img'=32,'row'=8] {'img'}, dimensions={0} | all-to-all | bytes 131072 | tf_op jit(solution)/shard_map/all_to_all | solution.py:251
  111.4 0.9 shard_map.72
  (8 shorter events, 0.3 us)
Async XLA Ops:
  3.6 5.6 %collective-permute-start.1 = (bf16[4,128,256]{2,1,0:T(8,128)(2,1)S(1)}, bf16[4,128,256]{2,1,0:T(8,128)(2,1)S(1)}, u32[]{:S(2)}, u32[]{:S(2)}) collective-permute-start(bf16[4,128,256]{2,1,0:T(8,128)(2,1)S(1)} %shard_map.65.near), channel_id=1, source_target_pairs={{0,1},{2,3},{4,5},{6,7},{1,0},{3,2},{5,4},{7,6},{8,9},{10,11},{12,... | collective-permute-start | bytes 786440 | tf_op jit(solution)/shard_map/ppermute | solution.py:262
  6.9 6.1 %collective-permute-start = (bf16[4,128,256]{2,1,0:T(8,128)(2,1)S(1)}, bf16[4,128,256]{2,1,0:T(8,128)(2,1)S(1)}, u32[]{:S(2)}, u32[]{:S(2)}) collective-permute-start(bf16[4,128,256]{2,1,0:T(8,128)(2,1)S(1)} %get-tuple-element.27.far), channel_id=1, source_target_pairs={{1,2},{3,4},{5,6},{7,0},{2,1},{4,3},{6,5},{0,7},{9,10},{11,12},{13... | collective-permute-start | bytes 786440 | tf_op jit(solution)/shard_map/ppermute | solution.py:262
  12.9 28.7 %copy-start = (f32[4,256]{1,0:T(4,128)S(1)}, f32[4,256]{1,0:T(4,128)}, u32[]{:S(2)}) copy-start(f32[4,256]{1,0:T(4,128)} %gain.7) | copy-start | bytes 12292
  13.0 28.7 %copy-start.1 = (f32[4,256]{1,0:T(4,128)S(1)}, f32[4,256]{1,0:T(4,128)}, u32[]{:S(2)}) copy-start(f32[4,256]{1,0:T(4,128)} %shift.7) | copy-start | bytes 12292

commit v7 on v6

--- a/solution.py
+++ b/solution.py
@@ -9,7 +9,7 @@
 
 
 EPS = 1e-05
-HALO = 4
+HALO = 2
 SHAPES = {'inner': (3, 0), 'outer': (2, 0), 0: (2, 0), 1: (5, 0), 2: (2, 0)}
 VM = pl.BlockSpec(memory_space=pltpu.VMEM)
 HBM = pl.BlockSpec(memory_space=pltpu.HBM)
@@ -109,7 +109,7 @@
 
 
 def far_proj_kernel(tok, w, bias, far, wbuf, bbuf, tbuf, sems, *, axis):
-    far_at = jnp.where(near_is_top(axis), HALO, 0)
+    far_at = jnp.where(near_is_top(axis), tok.shape[0] - HALO, 0)
     copies = [
         pltpu.make_async_copy(w, wbuf, sems.at[0]),
         pltpu.make_async_copy(bias, bbuf, sems.at[1]),
@@ -122,11 +122,16 @@
     project(tbuf, wbuf, bbuf, far)
 
 
-def near_proj_kernel(wbuf, bbuf, tok, near, tbuf, sem, *, axis):
-    copy = pltpu.make_async_copy(tok.at[pl.ds(jnp.where(near_is_top(axis), 0, HALO), HALO)], tbuf, sem)
+def near_proj_kernel(wbuf, bbuf, far, tok, feature, near, tbuf, rest, sem, *, axis):
+    flip = near_is_top(axis)
+    count = rest.shape[0]
+    copy = pltpu.make_async_copy(tok.at[pl.ds(jnp.where(flip, 0, HALO), count)], tbuf, sem)
     copy.start()
     copy.wait()
-    project(tbuf, wbuf, bbuf, near)
+    project(tbuf, wbuf, bbuf, rest)
+    feature[pl.ds(jnp.where(flip, HALO, 2 * HALO), count)] = rest[...]
+    feature[pl.ds(jnp.where(flip, HALO + count, HALO), HALO)] = far[...]
+    near[...] = rest[pl.ds(jnp.where(flip, 0, count - HALO), HALO)]
 
 
 def relu_row(x):
@@ -137,55 +142,43 @@
     return jnp.where(cond, a.astype(F32), b.astype(F32))
 
 
-def conv0_inner_kernel(far, near, cw, c_ref, part, w0, w_next, a3, sems, *, strip, axis):
+def conv0_inner_kernel(feature, cw, c_ref, part, w0, w_next, a3, sems, *, strip):
     waits = [[pltpu.make_async_copy(cw.at[0, dy], w0.at[dy], sems.at[dy])] for dy in range(3)]
     late = pltpu.make_async_copy(cw.at[1, 0], w_next, sems.at[3])
     for copy in (*waits[0], *waits[1], *waits[2], late):
         copy.start()
-    flip = near_is_top(axis)
 
     def row_at(i):
-        j = i % HALO
-        return relu_row(pick(flip, near[j], far[j]) if i < HALO else pick(flip, far[j], near[j]))
+        return relu_row(feature[HALO + i])
 
     w_parts = [w0.at[dy] for dy in range(3)]
-    part[0], part[1] = run_conv(row_at, strip, a3, w_parts, waits, c_ref, HALO, 1, strip, tile=SHAPES["inner"])
+    part[0], part[1] = run_conv(row_at, strip, a3, w_parts, waits, c_ref, 4, 1, strip, tile=SHAPES["inner"])
     late.wait()
 
 
-def conv0_edge(got, own, w0, part, c_ref, a3, upper, strip, exists=None):
-    def theirs(i):
-        return got[i] if exists is None else got[i].astype(F32) * exists
+def conv0_edge(got, feature, w0, part, c_ref, a3, upper, strip):
+    feature[pl.ds(jnp.where(upper, 0, strip + HALO), HALO)] = got
+    base = jnp.where(upper, 0, strip)
 
     def row_at(i):
-        above = theirs(i) if i < HALO else own[i - HALO]
-        below = own[i + HALO - 2] if i < 2 else theirs(i - 2)
-        return relu_row(pick(upper, above, below))
+        return relu_row(feature[base + i])
 
     w_parts = [w0.at[dy] for dy in range(3)]
-    at = jnp.where(upper, 0, strip + HALO - 2)
-    run_conv(row_at, HALO + 2, a3, w_parts, [[]] * 3, c_ref, at, strip, strip, tile=SHAPES["outer"])
-    row = c_ref[jnp.where(upper, HALO - 1, strip + HALO - 2)]
+    run_conv(row_at, HALO + 2, a3, w_parts, [[]] * 3, c_ref, base + 2, strip, strip, tile=SHAPES["outer"])
+    row = c_ref[jnp.where(upper, 3, strip + 2)]
     return part[0] + fold8(row), part[1] + fold8(row * row)
 
 
-def conv0_near_kernel(got, far, near, w0, part_in, c_in, c_ref, part, feature, a3, *, strip, axis):
-    flip = near_is_top(axis)
-    part[0], part[1] = conv0_edge(got, near, w0, part_in, c_ref, a3, flip, strip)
-    near_at = jnp.where(flip, 0, HALO)
-    feature[pl.ds(2 + near_at, HALO)] = near[...]
-    feature[pl.ds(2 + HALO - near_at, HALO)] = far[...]
-    feature[pl.ds(jnp.where(flip, 0, strip + 2), 2)] = got[pl.ds(jnp.where(flip, HALO - 2, 0), 2)]
-
-
-def conv0_far_kernel(got, far, w0, part, c_in, feature_in, c_ref, st, feature, a3, *, strip, axis):
-    flip = near_is_top(axis)
-    upper = jnp.logical_not(flip)
+def conv0_near_kernel(got, w0, part_in, c_in, feature_in, c_ref, part, feature, a3, *, strip, axis):
+    part[0], part[1] = conv0_edge(got[...], feature, w0, part_in, c_ref, a3, near_is_top(axis), strip)
+
+
+def conv0_far_kernel(got, w0, part, c_in, feature_in, c_ref, st, feature, a3, *, strip, axis):
     r = lax.axis_index(axis)
     exists = jnp.logical_and(r > 0, r < lax.axis_size(axis) - 1).astype(F32)
-    sums, squares = conv0_edge(got, far, w0, part, c_ref, a3, upper, strip, exists)
-    write_stats(st, sums, squares)
-    feature[pl.ds(jnp.where(flip, strip + 2, 0), 2)] = got[pl.ds(jnp.where(flip, 0, HALO - 2), 2)]
+    rows = (got[...].astype(F32) * exists).astype(BF)
+    upper = jnp.logical_not(near_is_top(axis))
+    write_stats(st, *conv0_edge(rows, feature, w0, part, c_ref, a3, upper, strip))
 
 
 def weight_copies(cw, k, wbuf, w_next, sems):
@@ -201,36 +194,49 @@
 
 
 def hidden_conv_kernel(
-    c_in, stats, gain, shift, w_first, cw, c_ref, st, *rest, k, lo, n_in, strip, total, axis
+    c_in, stats, gain, shift, w_first, cw, c_ref, st, *rest, k, lo, n_in, at, strip, total, axis
 ):
-    *w_next, a3, wbuf, sems = rest
-    waits, late = weight_copies(cw, k + 1, wbuf, w_next[0] if w_next else None, sems)
+    *more, a3, wbuf, sems = rest
+    waits, late = weight_copies(cw, k + 1, wbuf, more[0] if more else None, sems)
     mean, scale, bias = norm_terms(stats, gain, shift, k, total)
 
     def row_at(i):
-        x = jnp.maximum((c_in[i] - mean) * scale + bias, 0.0)
+        x = jnp.maximum((c_in[at + i] - mean) * scale + bias, 0.0)
         return masked(x, inside(lo + i, strip, axis))
 
     w_parts = [w_first, wbuf.at[0], wbuf.at[1]]
-    write_stats(st, *run_conv(row_at, n_in, a3, w_parts, waits, c_ref, 0, lo + 1, strip, tile=SHAPES[k]))
+    write_stats(st, *run_conv(row_at, n_in, a3, w_parts, waits, c_ref, at, lo + 1, strip, tile=SHAPES[k]))
+    if more:
+        flip = near_is_top(axis)
+        far, near = more[1:]
+        far[...] = c_ref[pl.ds(jnp.where(flip, at + strip - HALO, at), HALO)].astype(BF)
+        near[...] = c_ref[pl.ds(jnp.where(flip, at, at + strip - HALO), HALO)].astype(BF)
     for c in late:
         c.wait()
 
 
 def joined_conv_kernel(
-    c_in, stats, gain, shift, w_first, feature, cw, c_ref, st, w_next, joined, a3, wbuf, sems,
-    *, k, lo, n_in, strip, total, axis
+    c_in, stats, gain, shift, w_first, feature, got_far, got_near, cw, c_ref, st, w_next, joined, a3, wbuf, sems,
+    *, k, lo, n_in, at, strip, total, axis
 ):
     waits, late = weight_copies(cw, k + 1, wbuf, w_next, sems)
     mean, scale, bias = norm_terms(stats, gain, shift, k, total)
+    flip = near_is_top(axis)
+
+    def conv_row(i):
+        if i < HALO:
+            return pick(flip, got_near[i], got_far[i])
+        if i < HALO + strip:
+            return c_in[i]
+        return pick(flip, got_far[i - HALO - strip], got_near[i - HALO - strip])
 
     def row_at(i):
-        y = (feature[i].astype(F32) + ((c_in[i] - mean) * scale + bias)).astype(BF)
+        y = (feature[i].astype(F32) + ((conv_row(i) - mean) * scale + bias)).astype(BF)
         joined[i] = y
         return masked(relu_row(y), inside(lo + i, strip, axis))
 
     w_parts = [w_first, wbuf.at[0], wbuf.at[1]]
-    write_stats(st, *run_conv(row_at, n_in, a3, w_parts, waits, c_ref, 0, lo + 1, strip, tile=SHAPES[k]))
+    write_stats(st, *run_conv(row_at, n_in, a3, w_parts, waits, c_ref, at, lo + 1, strip, tile=SHAPES[k]))
     for c in late:
         c.wait()
 
@@ -281,25 +287,29 @@
         scratch_shapes=[pltpu.VMEM((HALO, cols, embed), BF), pltpu.SemaphoreType.DMA((3,))],
         compiler_params=PARAMS,
     )(token_rows, in_hbm(proj_weight), in_hbm(proj_bias[None]))
-    got_far = swapped(far, range(1, nrow, 2))
+    far_pairs, near_pairs = range(1, nrow, 2), range(0, nrow - 1, 2)
+    context = sds((strip + 2 * HALO, cols, ch), BF)
+    got_far = swapped(far, far_pairs)
     near_call = pl.pallas_call(
         functools.partial(near_proj_kernel, axis="row"),
-        out_shape=half,
-        in_specs=[VM, VM, HBM],
-        out_specs=VM,
-        scratch_shapes=[pltpu.VMEM((HALO, cols, embed), BF), pltpu.SemaphoreType.DMA(())],
+        out_shape=(context, half),
+        in_specs=[VM, VM, VM, HBM],
+        out_specs=(VM, VM),
+        scratch_shapes=[
+            pltpu.VMEM((strip - HALO, cols, embed), BF),
+            pltpu.VMEM((strip - HALO, cols, ch), BF),
+            pltpu.SemaphoreType.DMA(()),
+        ],
         compiler_params=PARAMS,
         cost_estimate=pl.CostEstimate(
-            flops=2 * embed * ch * cols * HALO, transcendentals=0, bytes_accessed=2 * HALO * cols * embed
+            flops=2 * embed * ch * cols * (strip - HALO), transcendentals=0, bytes_accessed=2 * strip * cols * embed
         ),
     )
-    near = near_call(in_vmem(pw), in_vmem(pb), token_rows)
-    got_near = swapped(near, range(0, nrow - 1, 2))
-    far, near, got_far, got_near = map(in_vmem, (far, near, got_far, got_near))
-
-    field = sds((strip + 2 * HALO - 2, cols, ch), F32)
+    feature, near = near_call(in_vmem(pw), in_vmem(pb), in_vmem(far), token_rows)
+    got_near = swapped(near, near_pairs)
+
+    field = sds((strip + 4, cols, ch), F32)
     stat = sds((nrow, 1, 2 * ch), F32)
-    context = sds((strip + 4, cols, ch), BF)
 
     def rows_scratch(rows):
         return pltpu.VMEM((rows, cols, 3 * ch), BF)
@@ -312,35 +322,29 @@
         )
 
     c, part, w0, w_next = pl.pallas_call(
-        functools.partial(conv0_inner_kernel, strip=strip, axis="row"),
+        functools.partial(conv0_inner_kernel, strip=strip),
         out_shape=(field, sums, sds((3, 3, ch, ch), BF), w_third),
-        in_specs=[VM, VM, HBM],
+        in_specs=[VM, HBM],
         out_specs=(VM,) * 4,
         scratch_shapes=[rows_scratch(strip), pltpu.SemaphoreType.DMA((4,))],
         compiler_params=PARAMS,
         cost_estimate=conv_flops(strip - 2),
-    )(far, near, weights)
-    w0 = in_vmem(w0)
-    c, part, feature = pl.pallas_call(
-        functools.partial(conv0_near_kernel, strip=strip, axis="row"),
-        out_shape=(field, sums, context),
-        in_specs=[VM] * 6,
-        out_specs=(VM,) * 3,
-        input_output_aliases={5: 0},
-        scratch_shapes=[rows_scratch(HALO + 2)],
-        compiler_params=PARAMS,
-        cost_estimate=conv_flops(HALO),
-    )(got_near, far, near, w0, in_vmem(part), in_vmem(c))
-    c, st, feature = pl.pallas_call(
-        functools.partial(conv0_far_kernel, strip=strip, axis="row"),
-        out_shape=(field, stat, context),
-        in_specs=[VM] * 6,
-        out_specs=(VM,) * 3,
-        input_output_aliases={4: 0, 5: 2},
-        scratch_shapes=[rows_scratch(HALO + 2)],
-        compiler_params=PARAMS,
-        cost_estimate=conv_flops(HALO),
-    )(got_far, far, w0, in_vmem(part), in_vmem(c), in_vmem(feature))
+    )(in_vmem(feature), weights)
+
+    def edge(kernel, got, part, c, feature, out):
+        return pl.pallas_call(
+            functools.partial(kernel, strip=strip, axis="row"),
+            out_shape=(field, out, context),
+            in_specs=[VM] * 5,
+            out_specs=(VM,) * 3,
+            input_output_aliases={3: 0, 4: 2},
+            scratch_shapes=[rows_scratch(HALO + 2)],
+            compiler_params=PARAMS,
+            cost_estimate=conv_flops(HALO),
+        )(*map(in_vmem, (got, w0, part, c, feature)))
+
+    c, part, feature = edge(conv0_near_kernel, got_near, part, c, feature, sums)
+    c, st, feature = edge(conv0_far_kernel, got_far, part, c, feature, stat)
 
     def call(kernel, extra_in, extra_out, n_in, aliases, **kw):
         args = (in_vmem(c), in_vmem(st), *norm_args, *map(in_vmem, extra_in))
@@ -358,14 +362,20 @@
             compiler_params=PARAMS,
         )(*args, weights)
 
+    edge_rows = pltpu.VMEM((HALO, cols, ch), BF)
     st = reduce_all(st)
-    c, st, w_next = call(hidden_conv_kernel, (w_next,), (w_third,), strip + 6, {}, k=0, lo=-3)
+    c, st, w_next, far, near = call(
+        hidden_conv_kernel, (w_next,), (w_third, edge_rows, edge_rows), strip + 2, {}, k=0, lo=-1, at=2
+    )
+    got_far = swapped(far, far_pairs)
+    got_near = swapped(near, near_pairs)
     st = reduce_all(st)
     c, st, w_next, joined = call(
-        joined_conv_kernel, (w_next, feature), (w_third, context), strip + 4, {5: 3}, k=1, lo=-2
+        joined_conv_kernel, (w_next, feature, got_far, got_near), (w_third, context), strip + 4, {5: 3},
+        k=1, lo=-2, at=0,
     )
     st = reduce_all(st)
-    c, st = call(hidden_conv_kernel, (w_next,), (), strip + 2, {}, k=2, lo=-1)
+    c, st = call(hidden_conv_kernel, (w_next,), (), strip + 2, {}, k=2, lo=-1, at=0)
     st = reduce_all(st)
     out = pl.pallas_call(
         functools.partial(final_kernel, k=3, total=total),

time: 113 us -> 114 us (level)
  blocking collectives: 90.4 us -> 69.2 us
  starting transfers between devices: 3.29 us -> 15.5 us
  waiting for transfers between devices: 2.93 us -> 12.4 us
  local copies, waits for them, and re-layouts: 0.16 us -> 1.42 us
    all_to_all x8 -> x6, blocking collectives: 90.4 us -> 69.2 us  [sent_to_all(): return lax.all_to_all(value, axis, 0, 0, tiled=True)]
    all_to_all x0 -> x2, waiting for transfers between devices: none -> 10.5 us  [sent_to_all(): return lax.all_to_all(value, axis, 0, 0, tiled=True)]
    all_to_all x0 -> x2, starting transfers between devices: none -> 9.19 us  [sent_to_all(): return lax.all_to_all(value, axis, 0, 0, tiled=True)]
    ppermute x2 -> x4, starting transfers between devices: 3.29 us -> 6.3 us  [swapped(): return lax.ppermute(value, 'row', pairs + [(j, i) for i, j in pairs])]
    ppermute x2 -> x4, waiting for transfers between devices: 2.93 us -> 1.89 us  [swapped(): return lax.ppermute(value, 'row', pairs + [(j, i) for i, j in pairs])]
  transfers between devices with their start and end apart: 2 -> 6, of which waited for: 1 -> 3; matrix products, arithmetic and copies ran while one was open for 0% -> 1% of each run, Pallas kernels for 3% -> 2%
where the time goes in v7:
time: 114 us
  blocking collectives  69.2 us (61%)
  starting transfers between devices  15.5 us (14%)
  Pallas kernels  15.2 us (13%)
  waiting for transfers between devices  12.4 us (11%)
  local copies, waits for them, and re-layouts  1.42 us (1%)
    all_to_all x6, blocking collectives, sent_to_all(): return lax.all_to_all(value, axis, 0, 0, tiled=True)  69.2 us
    all_to_all x2, waiting for transfers between devices, sent_to_all(): return lax.all_to_all(value, axis, 0, 0, tiled=True)  10.5 us
    all_to_all x2, starting transfers between devices, sent_to_all(): return lax.all_to_all(value, axis, 0, 0, tiled=True)  9.19 us
    pallas_call x3, Pallas kernels, call(): pl.pallas_call(functools.partial(kernel, n_in=n_in, strip=strip, total=to...  7.29 us
    ppermute x4, starting transfers between devices, swapped(): return lax.ppermute(value, 'row', pairs + [(j, i) for i, j in pairs])  6.3 us
  transfers between devices with their start and end apart: 6, of which 3 were waited for; matrix products, arithmetic and copies ran while one was open for 1% of the time, Pallas kernels for 2%

profile of v7, /device:TPU:1, one launch (start us, length us, event | category | flops | bytes accessed | tf_op | source)
XLA Modules:
  0.0 113.9 jit_solution(2067913063690069933)
XLA Ops:
  0.0 1.5 %shard_map.64 = (bf16[2,128,256]{2,1,0:T(8,128)(2,1)S(1)}, bf16[1024,256]{1,0:T(8,128)(2,1)S(1)}, f32[1,256]{1,0:T(1,128)S(1)}) custom-call(bf16[8,128,1024]{2,1,0:T(8,128)(2,1)} %bitcast.3, bf16[1024,256]{1,0:T(8,128)(2,1)} %w.1, f32[1,256]{1,0:T(1,128)} %bitcast.5), custom_call_target="tpu_custom_call" | custom-call | tf_op jit(solution)/shard_map/pallas_call | solution.py:282
  1.6 2.0 %shard_map.65 = (bf16[12,128,256]{2,1,0:T(8,128)(2,1)S(1)}, bf16[2,128,256]{2,1,0:T(8,128)(2,1)S(1)}) custom-call(bf16[1024,256]{1,0:T(8,128)(2,1)S(1)} %get-tuple-element.32.wbuf, f32[1,256]{1,0:T(1,128)S(1)} %get-tuple-element.33.bbuf, bf16[2,128,256]{2,1,0:T(8,128)(2,1)S(1)} %get-tuple-element.31.far, bf16[8,128,1024]{2,1,0:T(8,128)(2,1)} %bitcast.4), custom_call_target="tpu_custom_call" | custom-call | flops 402653184 | bytes 2097152 | tf_op jit(solution)/shard_map/pallas_call | solution.py:308
  3.6 3.3 %collective-permute-start.1 = (bf16[2,128,256]{2,1,0:T(8,128)(2,1)S(1)}, bf16[2,128,256]{2,1,0:T(8,128)(2,1)S(1)}, u32[]{:S(2)}, u32[]{:S(2)}) collective-permute-start(bf16[2,128,256]{2,1,0:T(8,128)(2,1)S(1)} %get-tuple-element.36), channel_id=1, source_target_pairs={{0,1},{2,3},{4,5},{6,7},{1,0},{3,2},{5,4},{7,6},{8,9},{10,11},{12,... | collective-permute-start | bytes 393224 | tf_op jit(solution)/shard_map/ppermute | solution.py:268
  6.9 0.0 collective-permute-start
  6.9 2.2 %shard_map.66 = (f32[12,128,256]{2,1,0:T(8,128)S(1)}, f32[2,8,256]{2,1,0:T(8,128)S(1)}, bf16[3,3,256,256]{3,2,1,0:T(8,128)(2,1)S(1)}, bf16[3,256,256]{2,1,0:T(8,128)(2,1)S(1)}) custom-call(bf16[12,128,256]{2,1,0:T(8,128)(2,1)S(1)} %get-tuple-element.34.feature.feature_in, bf16[4,3,3,256,256]{4,3,2,1,0:T(8,128)(2,1)} %cw.7), custom_call_target="tpu_custom_call" | custom-call | flops 905969664 | bytes 1179648 | tf_op jit(solution)/shard_map/pallas_call | solution.py:324
  9.1 0.0 collective-permute-done.1.got
  9.2 0.5 shard_map.67
  9.7 1.9 %collective-permute-done.got = bf16[2,128,256]{2,1,0:T(8,128)(2,1)S(1)} collective-permute-done((bf16[2,128,256]{2,1,0:T(8,128)(2,1)S(1)}, bf16[2,128,256]{2,1,0:T(8,128)(2,1)S(1)}, u32[]{:S(2)}, u32[]{:S(2)}) %collective-permute-start) | collective-permute-done | bytes 131104 | tf_op jit(solution)/shard_map/ppermute | solution.py:268
  11.6 0.6 shard_map.68
  12.1 8.1 %all_to_all.40 = f32[8,1,512]{2,1,0:T(1,128)S(1)} all-to-all(f32[8,1,512]{2,1,0:T(1,128)S(1)} %get-tuple-element.43), channel_id=1, replica_groups=mesh['img'=32,'row'=8] {'row'}, dimensions={0} | all-to-all | bytes 32768 | tf_op jit(solution)/shard_map/all_to_all | solution.py:257
  20.3 19.7 %all_to_all.41.stats = f32[32,1,512]{2,1,0:T(1,128)S(1)} all-to-all(f32[32,1,512]{2,1,0:T(1,128)S(1)} %broadcast_in_dim.13), channel_id=1, replica_groups=mesh['img'=32,'row'=8] {'img'}, dimensions={0} | all-to-all | bytes 131072 | tf_op jit(solution)/shard_map/all_to_all | solution.py:257
  39.9 0.0 copy-done
  39.9 0.0 copy-done.1
  39.9 2.9 %shard_map.69 = (f32[12,128,256]{2,1,0:T(8,128)S(1)}, f32[8,1,512]{2,1,0:T(1,128)}, bf16[3,256,256]{2,1,0:T(8,128)(2,1)S(1)}, bf16[2,128,256]{2,1,0:T(8,128)(2,1)}, bf16[2,128,256]{2,1,0:T(8,128)(2,1)S(1)}) custom-call(f32[12,128,256]{2,1,0:T(8,128)S(1)} %get-tuple-element.42.c_in, ...), custom_call_target="tpu_custom_call", output_to_operand_aliasing={{0}: (0, {})} | custom-call | tf_op jit(solution)/shard_map/pallas_call | solution.py:351
  42.8 0.0 copy-start.2
  42.9 0.6 copy-done.2
  43.5 5.4 %all-to-all-start.2 = ((f32[8,1,512]{2,1,0:T(1,128)}), f32[8,1,512]{2,1,0:T(1,128)S(1)}, u32[]{:S(2)}, u32[]{:S(2)}) async-start(f32[8,1,512]{2,1,0:T(1,128)} %get-tuple-element.46), calls=%async_computation.2 | async-start | bytes 32768 | tf_op jit(solution)/shard_map/all_to_all | solution.py:257
  48.9 1.6 %collective-permute-start.2 = (bf16[2,128,256]{2,1,0:T(8,128)(2,1)}, bf16[2,128,256]{2,1,0:T(8,128)(2,1)S(1)}, u32[]{:S(2)}, u32[]{:S(2)}) collective-permute-start(bf16[2,128,256]{2,1,0:T(8,128)(2,1)} %get-tuple-element.49), channel_id=1, source_target_pairs={{1,2},{3,4},{5,6},{7,0},{2,1},{4,3},{6,5},{0,7},{9,10},{11,12},{13... | collective-permute-start | bytes 393224 | tf_op jit(solution)/shard_map/ppermute | solution.py:268
  50.5 1.4 %collective-permute-start.3 = (bf16[2,128,256]{2,1,0:T(8,128)(2,1)}, bf16[2,128,256]{2,1,0:T(8,128)(2,1)S(1)}, u32[]{:S(2)}, u32[]{:S(2)}) collective-permute-start(bf16[2,128,256]{2,1,0:T(8,128)(2,1)} %copy-done.2), channel_id=1, source_target_pairs={{0,1},{2,3},{4,5},{6,7},{1,0},{3,2},{5,4},{7,6},{8,9},{10,11},{12,... | collective-permute-start | bytes 393224 | tf_op jit(solution)/shard_map/ppermute | solution.py:268
  51.9 1.7 %all-to-all-done.2 = f32[8,1,512]{2,1,0:T(1,128)S(1)} async-done(((f32[8,1,512]{2,1,0:T(1,128)}), f32[8,1,512]{2,1,0:T(1,128)S(1)}, u32[]{:S(2)}, u32[]{:S(2)}) %all-to-all-start.2) | async-done | bytes 16416 | tf_op jit(solution)/shard_map/all_to_all | solution.py:257
  53.6 0.7 broadcast_in_dim.14
  54.2 3.8 %all-to-all-start.3 = ((f32[32,1,512]{2,1,0:T(1,128)}), f32[32,1,512]{2,1,0:T(1,128)S(1)}, u32[]{:S(2)}, u32[]{:S(2)}) async-start(f32[32,1,512]{2,1,0:T(1,128)} %broadcast_in_dim.14), calls=%async_computation.3 | async-start | bytes 131072 | tf_op jit(solution)/shard_map/all_to_all | solution.py:257
  58.1 0.0 collective-permute-done.2.got_far
  58.1 0.0 collective-permute-done.3.got_near
  58.1 8.9 %all-to-all-done.3.stats = f32[32,1,512]{2,1,0:T(1,128)S(1)} async-done(((f32[32,1,512]{2,1,0:T(1,128)}), f32[32,1,512]{2,1,0:T(1,128)S(1)}, u32[]{:S(2)}, u32[]{:S(2)}) %all-to-all-start.3) | async-done | bytes 65568 | tf_op jit(solution)/shard_map/all_to_all | solution.py:257
  67.0 2.3 %shard_map.70 = (f32[12,128,256]{2,1,0:T(8,128)S(1)}, f32[8,1,512]{2,1,0:T(1,128)S(1)}, bf16[3,256,256]{2,1,0:T(8,128)(2,1)S(1)}, bf16[12,128,256]{2,1,0:T(8,128)(2,1)S(1)}) custom-call(f32[12,128,256]{2,1,0:T(8,128)S(1)} %get-tuple-element.45.c_in, f32[32,1,512]{2,1,0:T(1,128)S(1)} %all-to-all-done.3.stats, ...), custom_call_target="tpu_custom_call", output_to_operand_aliasing={{0}: (0, {}), {3}: (5, {})} | custom-call | tf_op jit(solution)/shard_map/pallas_call | solution.py:351
  69.3 8.8 %all_to_all.42 = f32[8,1,512]{2,1,0:T(1,128)S(1)} all-to-all(f32[8,1,512]{2,1,0:T(1,128)S(1)} %get-tuple-element.53), channel_id=1, replica_groups=mesh['img'=32,'row'=8] {'row'}, dimensions={0} | all-to-all | bytes 32768 | tf_op jit(solution)/shard_map/all_to_all | solution.py:257
  78.2 11.8 %all_to_all.43.stats = f32[32,1,512]{2,1,0:T(1,128)S(1)} all-to-all(f32[32,1,512]{2,1,0:T(1,128)S(1)} %broadcast_in_dim.15), channel_id=1, replica_groups=mesh['img'=32,'row'=8] {'img'}, dimensions={0} | all-to-all | bytes 131072 | tf_op jit(solution)/shard_map/all_to_all | solution.py:257
  90.0 2.1 %shard_map.71 = (f32[12,128,256]{2,1,0:T(8,128)S(1)}, f32[8,1,512]{2,1,0:T(1,128)S(1)}) custom-call(f32[12,128,256]{2,1,0:T(8,128)S(1)} %get-tuple-element.52.c_in, f32[32,1,512]{2,1,0:T(1,128)S(1)} %all_to_all.43.stats, f32[4,256]{1,0:T(4,128)S(1)} %copy-done, f32[4,256]{1,0:T(4,128)S(1)} %copy-done.1, ...), custom_call_target="tpu_custom_call", output_to_operand_aliasing={{0}: (0, {})} | custom-call | tf_op jit(solution)/shard_map/pallas_call | solution.py:351
  92.1 8.9 %all_to_all.44 = f32[8,1,512]{2,1,0:T(1,128)S(1)} all-to-all(f32[8,1,512]{2,1,0:T(1,128)S(1)} %get-tuple-element.56), channel_id=1, replica_groups=mesh['img'=32,'row'=8] {'row'}, dimensions={0} | all-to-all | bytes 32768 | tf_op jit(solution)/shard_map/all_to_all | solution.py:257
  101.1 11.9 %all_to_all.45.stats = f32[32,1,512]{2,1,0:T(1,128)S(1)} all-to-all(f32[32,1,512]{2,1,0:T(1,128)S(1)} %broadcast_in_dim.16), channel_id=1, replica_groups=mesh['img'=32,'row'=8] {'img'}, dimensions={0} | all-to-all | bytes 131072 | tf_op jit(solution)/shard_map/all_to_all | solution.py:257
  113.0 0.9 shard_map.72
  (9 shorter events, 0.2 us)
Async XLA Ops:
  3.6 5.5 %collective-permute-start.1 = (bf16[2,128,256]{2,1,0:T(8,128)(2,1)S(1)}, bf16[2,128,256]{2,1,0:T(8,128)(2,1)S(1)}, u32[]{:S(2)}, u32[]{:S(2)}) collective-permute-start(bf16[2,128,256]{2,1,0:T(8,128)(2,1)S(1)} %get-tuple-element.36), channel_id=1, source_target_pairs={{0,1},{2,3},{4,5},{6,7},{1,0},{3,2},{5,4},{7,6},{8,9},{10,11},{12,... | collective-permute-start | bytes 393224 | tf_op jit(solution)/shard_map/ppermute | solution.py:268
  6.9 4.7 %collective-permute-start = (bf16[2,128,256]{2,1,0:T(8,128)(2,1)S(1)}, bf16[2,128,256]{2,1,0:T(8,128)(2,1)S(1)}, u32[]{:S(2)}, u32[]{:S(2)}) collective-permute-start(bf16[2,128,256]{2,1,0:T(8,128)(2,1)S(1)} %get-tuple-element.31.far), channel_id=1, source_target_pairs={{1,2},{3,4},{5,6},{7,0},{2,1},{4,3},{6,5},{0,7},{9,10},{11,12},{13... | collective-permute-start | bytes 393224 | tf_op jit(solution)/shard_map/ppermute | solution.py:268
  11.6 28.3 %copy-start = (f32[4,256]{1,0:T(4,128)S(1)}, f32[4,256]{1,0:T(4,128)}, u32[]{:S(2)}) copy-start(f32[4,256]{1,0:T(4,128)} %gain.7) | copy-start | bytes 12292
  11.6 28.3 %copy-start.1 = (f32[4,256]{1,0:T(4,128)S(1)}, f32[4,256]{1,0:T(4,128)}, u32[]{:S(2)}) copy-start(f32[4,256]{1,0:T(4,128)} %shift.7) | copy-start | bytes 12292
  42.8 0.7 copy-start.2
  43.5 10.0 %all-to-all-start.2 = ((f32[8,1,512]{2,1,0:T(1,128)}), f32[8,1,512]{2,1,0:T(1,128)S(1)}, u32[]{:S(2)}, u32[]{:S(2)}) async-start(f32[8,1,512]{2,1,0:T(1,128)} %get-tuple-element.46), calls=%async_computation.2 | async-start | bytes 32768 | tf_op jit(solution)/shard_map/all_to_all | solution.py:257
  48.9 9.2 %collective-permute-start.2 = (bf16[2,128,256]{2,1,0:T(8,128)(2,1)}, bf16[2,128,256]{2,1,0:T(8,128)(2,1)S(1)}, u32[]{:S(2)}, u32[]{:S(2)}) collective-permute-start(bf16[2,128,256]{2,1,0:T(8,128)(2,1)} %get-tuple-element.49), channel_id=1, source_target_pairs={{1,2},{3,4},{5,6},{7,0},{2,1},{4,3},{6,5},{0,7},{9,10},{11,12},{13... | collective-permute-start | bytes 393224 | tf_op jit(solution)/shard_map/ppermute | solution.py:268
  50.5 7.6 %collective-permute-start.3 = (bf16[2,128,256]{2,1,0:T(8,128)(2,1)}, bf16[2,128,256]{2,1,0:T(8,128)(2,1)S(1)}, u32[]{:S(2)}, u32[]{:S(2)}) collective-permute-start(bf16[2,128,256]{2,1,0:T(8,128)(2,1)} %copy-done.2), channel_id=1, source_target_pairs={{0,1},{2,3},{4,5},{6,7},{1,0},{3,2},{5,4},{7,6},{8,9},{10,11},{12,... | collective-permute-start | bytes 393224 | tf_op jit(solution)/shard_map/ppermute | solution.py:268
  54.2 12.7 %all-to-all-start.3 = ((f32[32,1,512]{2,1,0:T(1,128)}), f32[32,1,512]{2,1,0:T(1,128)S(1)}, u32[]{:S(2)}, u32[]{:S(2)}) async-start(f32[32,1,512]{2,1,0:T(1,128)} %broadcast_in_dim.14), calls=%async_computation.3 | async-start | bytes 131072 | tf_op jit(solution)/shard_map/all_to_all | solution.py:257
